TPU v7x, 32 devices: a whole 2x2x4 slice. The times are simulated.
32 devices in a mesh: wide: 16 (over z, y, x), narrow: 2 (over core).
Axes of the slice: x: 2, y: 2, z: 4, core: 2. Of those that a mesh axis runs over, the one named last changes fastest.
Arguments:
- tokens: bfloat16 [32768, 768], P(('wide', 'narrow')), may hold values from -6 to 6
- segment: int32 [32, 1024], P(('wide', 'narrow')), may hold values from 0 to 3, as said below
- keep: int32 [32, 1024], P(('wide', 'narrow')), may hold values 0 or 1
- cotangent: bfloat16 [32768, 768], P(('wide', 'narrow')), may hold values from -6 to 6
- gain_one: bfloat16 [768], P('wide'), may hold values from 0.5 to 1.5
- bias_one: bfloat16 [768], P('wide'), may hold values from -3 to 3
- w_query: bfloat16 [768, 768], P(None, 'wide'), may hold values from -0.3125 to 0.3125
- b_query: bfloat16 [768], P('wide'), may hold values from -3 to 3
- w_key: bfloat16 [768, 768], P(None, 'wide'), may hold values from -0.21875 to 0.21875
- w_value: bfloat16 [768, 768], P(None, 'wide'), may hold values from -0.21875 to 0.21875
- b_value: bfloat16 [768], P('wide'), may hold values from -3 to 3
- w_out: bfloat16 [768, 768], P(None, 'wide'), may hold values from -1.75 to 1.75
- b_out: bfloat16 [768], P('wide'), may hold values from -3 to 3
- gain_two: bfloat16 [768], P('wide'), may hold values from 0.5 to 1.5
- bias_two: bfloat16 [768], P('wide'), may hold values from -3 to 3
- w_hidden: bfloat16 [768, 3072], P(None, 'wide'), may hold values from -0.21875 to 0.21875
- b_hidden: bfloat16 [3072], P('wide'), may hold values from -3 to 3
- w_proj: bfloat16 [3072, 768], P(None, 'wide'), may hold values from -0.109375 to 0.109375
- b_proj: bfloat16 [768], P('wide'), may hold values from -3 to 3
Outputs:
- mixed: bfloat16 [32768, 768], P(('wide', 'narrow'))
- grad_tokens: float32 [32768, 768], P(('wide', 'narrow'))
- grad_gain_one: float32 [768], P('wide')
- grad_bias_one: float32 [768], P('wide')
- grad_w_query: float32 [768, 768], P(None, 'wide')
- grad_b_query: float32 [768], P('wide')
- grad_w_key: float32 [768, 768], P(None, 'wide')
- grad_w_value: float32 [768, 768], P(None, 'wide')
- grad_b_value: float32 [768], P('wide')
- grad_w_out: float32 [768, 768], P(None, 'wide')
- grad_b_out: float32 [768], P('wide')
- grad_gain_two: float32 [768], P('wide')
- grad_bias_two: float32 [768], P('wide')
- grad_w_hidden: float32 [768, 3072], P(None, 'wide')
- grad_b_hidden: float32 [3072], P('wide')
- grad_w_proj: float32 [3072, 768], P(None, 'wide')
- grad_b_proj: float32 [768], P('wide')
Inputs may be any that keep to these rules, and one draw needn't show every extreme that they name: `segment`: each device's row holds either 4 images of 1024 // 4 slots each, numbered 0 to 3 in order, or one image of all 1024 slots, numbered 0; both kinds occur in every draw.
All inputs are finite; a program needn't handle non-finite values. No bound on the sum of `keep` on one device may be relied on, other than what follows from the above.
Results may differ from a plain program's by a relative error of at most 0.014.
Values may be sent and summed in bfloat16 or wider, within the bound.
A program may use at most 384 MiB of HBM per device.

v0:
```python
import math

import jax
import jax.numpy as jnp
from jax import lax
from jax.sharding import PartitionSpec as P

HEADS = 16


def matmul(left, right):
    return jnp.dot(left, right, preferred_element_type=jnp.float32)


def left_product(left, right):
    return lax.dot_general(
        left, right, (((0,), (0,)), ((), ())), preferred_element_type=jnp.float32
    )


def right_product(left, right):
    return lax.dot_general(
        left, right, (((1,), (1,)), ((), ())), preferred_element_type=jnp.float32
    )


def layer_norm_rows(values, gain, bias):
    centred = values - jnp.mean(values, -1, keepdims=True)
    var = jnp.mean(centred * centred, -1, keepdims=True)
    factor = lax.rsqrt(var + 1e-05)
    normed = centred * factor
    return (normed * gain + bias, normed, factor)


def norm_back(grad, normed, factor, gain):
    scaled = grad * gain
    inner = (
        scaled
        - jnp.mean(scaled, -1, keepdims=True)
        - normed * jnp.mean(scaled * normed, -1, keepdims=True)
    )
    return (factor * inner, jnp.sum(grad * normed, 0), jnp.sum(grad, 0))


def gelu_slope(values):
    cdf = 0.5 * (1.0 + lax.erf(values * (1.0 / math.sqrt(2.0))))
    pdf = jnp.exp(-0.5 * values * values) * (1.0 / math.sqrt(2.0 * math.pi))
    return cdf + values * pdf


def head_scores(query, keys, allowed, scale):
    raw = jnp.einsum("qhd,khd->hqk", query, keys, preferred_element_type=jnp.float32) * scale
    return jnp.where(allowed[None], raw, jnp.float32(-1e30))


def row_sums(values):
    return jnp.sum(values.astype(jnp.float32), 0)


def shards(
    tokens,
    segment,
    keep,
    cotangent,
    gain_one,
    bias_one,
    w_query,
    b_query,
    w_key,
    w_value,
    b_value,
    w_out,
    b_out,
    gain_two,
    bias_two,
    w_hidden,
    b_hidden,
    w_proj,
    b_proj,
):
    single_float = jnp.float32
    bf16 = jnp.bfloat16
    forward_rule = (
        lax.all_gather(gain_one, "wide", axis=0, tiled=True),
        lax.all_gather(bias_one, "wide", axis=0, tiled=True),
        lax.all_gather(w_query, "wide", axis=1, tiled=True),
        lax.all_gather(b_query, "wide", axis=0, tiled=True),
        lax.all_gather(w_key, "wide", axis=1, tiled=True),
        lax.all_gather(w_value, "wide", axis=1, tiled=True),
        lax.all_gather(b_value, "wide", axis=0, tiled=True),
        lax.all_gather(w_out, "wide", axis=1, tiled=True),
        lax.all_gather(b_out, "wide", axis=0, tiled=True),
        lax.all_gather(gain_two, "wide", axis=0, tiled=True),
        lax.all_gather(bias_two, "wide", axis=0, tiled=True),
        lax.all_gather(w_hidden, "wide", axis=1, tiled=True),
        lax.all_gather(b_hidden, "wide", axis=0, tiled=True),
        lax.all_gather(w_proj, "wide", axis=1, tiled=True),
        lax.all_gather(b_proj, "wide", axis=0, tiled=True),
    )
    count = tokens.shape[0]
    width = tokens.shape[1]
    head_dim = width // HEADS
    scale = float(head_dim) ** (-0.5)
    seg = segment[0]
    live = keep[0]
    index = jnp.arange(count)
    allowed = (seg[:, None] == seg[None, :]) & (
        (live[None, :] > 0) | (index[:, None] == index[None, :])
    )
    input_float = tokens.astype(single_float)
    normalized_first, centred_scaled_first, inverse_deviation_first = layer_norm_rows(
        input_float, forward_rule[0].astype(single_float), forward_rule[1].astype(single_float)
    )
    h_one = normalized_first.astype(bf16)
    query = (
        (matmul(h_one, forward_rule[2]) + forward_rule[3].astype(single_float))
        .astype(bf16)
        .reshape(count, HEADS, head_dim)
    )
    keys = matmul(h_one, forward_rule[4]).astype(bf16).reshape(count, HEADS, head_dim)
    value = (
        (matmul(h_one, forward_rule[5]) + forward_rule[6].astype(single_float))
        .astype(bf16)
        .reshape(count, HEADS, head_dim)
    )
    scores = head_scores(query, keys, allowed, scale)
    top = jnp.max(scores, -1, keepdims=True)
    expo = jnp.exp(scores - top)
    total = jnp.sum(expo, -1, keepdims=True)
    lse = top + jnp.log(total)
    probs_low = (expo / total).astype(bf16)
    joined = (
        jnp.einsum("hqk,khd->qhd", probs_low, value, preferred_element_type=single_float)
        .reshape(count, width)
        .astype(bf16)
    )
    input_first = (
        input_float + matmul(joined, forward_rule[7]) + forward_rule[8].astype(single_float)
    )
    normalized_second, centred_scaled_second, inverse_deviation_second = layer_norm_rows(
        input_first, forward_rule[9].astype(single_float), forward_rule[10].astype(single_float)
    )
    h_two = normalized_second.astype(bf16)
    upper = matmul(h_two, forward_rule[11]) + forward_rule[12].astype(single_float)
    act = jax.nn.gelu(upper, approximate=False).astype(bf16)
    mixed = (
        input_first + matmul(act, forward_rule[13]) + forward_rule[14].astype(single_float)
    ).astype(bf16)
    backward_rule = (
        lax.all_gather(gain_one, "wide", axis=0, tiled=True),
        lax.all_gather(bias_one, "wide", axis=0, tiled=True),
        lax.all_gather(w_query, "wide", axis=1, tiled=True),
        lax.all_gather(b_query, "wide", axis=0, tiled=True),
        lax.all_gather(w_key, "wide", axis=1, tiled=True),
        lax.all_gather(w_value, "wide", axis=1, tiled=True),
        lax.all_gather(b_value, "wide", axis=0, tiled=True),
        lax.all_gather(w_out, "wide", axis=1, tiled=True),
        lax.all_gather(b_out, "wide", axis=0, tiled=True),
        lax.all_gather(gain_two, "wide", axis=0, tiled=True),
        lax.all_gather(bias_two, "wide", axis=0, tiled=True),
        lax.all_gather(w_hidden, "wide", axis=1, tiled=True),
        lax.all_gather(b_hidden, "wide", axis=0, tiled=True),
        lax.all_gather(w_proj, "wide", axis=1, tiled=True),
        lax.all_gather(b_proj, "wide", axis=0, tiled=True),
    )
    d_out = cotangent.astype(single_float) * live.astype(single_float)[:, None]
    d_branch = d_out.astype(bf16)
    grad_b_proj = row_sums(d_branch)
    grad_w_proj = left_product(act, d_branch)
    d_act = right_product(d_branch, backward_rule[13])
    d_upper = (d_act * gelu_slope(upper)).astype(bf16)
    grad_b_hidden = row_sums(d_upper)
    grad_w_hidden = left_product(h_two, d_upper)
    grad_hidden_second = right_product(d_upper, backward_rule[11])
    d_norm_two, grad_gain_two, grad_bias_two = norm_back(
        grad_hidden_second,
        centred_scaled_second,
        inverse_deviation_second,
        backward_rule[9].astype(single_float),
    )
    d_x_one = d_out + d_norm_two
    d_attn = d_x_one.astype(bf16)
    grad_b_out = row_sums(d_attn)
    grad_w_out = left_product(joined, d_attn)
    d_joined = right_product(d_attn, backward_rule[7]).astype(bf16).reshape(count, HEADS, head_dim)
    probs = jnp.exp(head_scores(query, keys, allowed, scale) - lse)
    d_value = (
        jnp.einsum(
            "hqk,qhd->khd", probs.astype(bf16), d_joined, preferred_element_type=single_float
        )
        .astype(bf16)
        .reshape(count, width)
    )
    d_probs = jnp.einsum("qhd,khd->hqk", d_joined, value, preferred_element_type=single_float)
    d_scores = (probs * (d_probs - jnp.sum(d_probs * probs, -1, keepdims=True))).astype(bf16)
    d_query = (
        (jnp.einsum("hqk,khd->qhd", d_scores, keys, preferred_element_type=single_float) * scale)
        .astype(bf16)
        .reshape(count, width)
    )
    d_keys = (
        (jnp.einsum("hqk,qhd->khd", d_scores, query, preferred_element_type=single_float) * scale)
        .astype(bf16)
        .reshape(count, width)
    )
    grad_b_query = row_sums(d_query)
    grad_b_value = row_sums(d_value)
    grad_w_query = left_product(h_one, d_query)
    grad_w_key = left_product(h_one, d_keys)
    grad_w_value = left_product(h_one, d_value)
    grad_hidden_first = (
        right_product(d_query, backward_rule[2])
        + right_product(d_keys, backward_rule[4])
        + right_product(d_value, backward_rule[5])
    )
    d_norm_one, grad_gain_one, grad_bias_one = norm_back(
        grad_hidden_first,
        centred_scaled_first,
        inverse_deviation_first,
        backward_rule[0].astype(single_float),
    )
    grad_tokens = d_x_one + d_norm_one
    shares = (
        lax.psum_scatter(grad_gain_one, "wide", scatter_dimension=0, tiled=True),
        lax.psum_scatter(grad_bias_one, "wide", scatter_dimension=0, tiled=True),
        lax.psum_scatter(grad_w_query, "wide", scatter_dimension=1, tiled=True),
        lax.psum_scatter(grad_b_query, "wide", scatter_dimension=0, tiled=True),
        lax.psum_scatter(grad_w_key, "wide", scatter_dimension=1, tiled=True),
        lax.psum_scatter(grad_w_value, "wide", scatter_dimension=1, tiled=True),
        lax.psum_scatter(grad_b_value, "wide", scatter_dimension=0, tiled=True),
        lax.psum_scatter(grad_w_out, "wide", scatter_dimension=1, tiled=True),
        lax.psum_scatter(grad_b_out, "wide", scatter_dimension=0, tiled=True),
        lax.psum_scatter(grad_gain_two, "wide", scatter_dimension=0, tiled=True),
        lax.psum_scatter(grad_bias_two, "wide", scatter_dimension=0, tiled=True),
        lax.psum_scatter(grad_w_hidden, "wide", scatter_dimension=1, tiled=True),
        lax.psum_scatter(grad_b_hidden, "wide", scatter_dimension=0, tiled=True),
        lax.psum_scatter(grad_w_proj, "wide", scatter_dimension=1, tiled=True),
        lax.psum_scatter(grad_b_proj, "wide", scatter_dimension=0, tiled=True),
    )
    summed = (
        lax.psum(shares[0].astype(jnp.bfloat16), "narrow").astype(jnp.float32),
        lax.psum(shares[1].astype(jnp.bfloat16), "narrow").astype(jnp.float32),
        lax.psum(shares[2].astype(jnp.bfloat16), "narrow").astype(jnp.float32),
        lax.psum(shares[3].astype(jnp.bfloat16), "narrow").astype(jnp.float32),
        lax.psum(shares[4].astype(jnp.bfloat16), "narrow").astype(jnp.float32),
        lax.psum(shares[5].astype(jnp.bfloat16), "narrow").astype(jnp.float32),
        lax.psum(shares[6].astype(jnp.bfloat16), "narrow").astype(jnp.float32),
        lax.psum(shares[7].astype(jnp.bfloat16), "narrow").astype(jnp.float32),
        lax.psum(shares[8].astype(jnp.bfloat16), "narrow").astype(jnp.float32),
        lax.psum(shares[9].astype(jnp.bfloat16), "narrow").astype(jnp.float32),
        lax.psum(shares[10].astype(jnp.bfloat16), "narrow").astype(jnp.float32),
        lax.psum(shares[11].astype(jnp.bfloat16), "narrow").astype(jnp.float32),
        lax.psum(shares[12].astype(jnp.bfloat16), "narrow").astype(jnp.float32),
        lax.psum(shares[13].astype(jnp.bfloat16), "narrow").astype(jnp.float32),
        lax.psum(shares[14].astype(jnp.bfloat16), "narrow").astype(jnp.float32),
    )
    return (
        mixed,
        grad_tokens,
        summed[0],
        summed[1],
        summed[2],
        summed[3],
        summed[4],
        summed[5],
        summed[6],
        summed[7],
        summed[8],
        summed[9],
        summed[10],
        summed[11],
        summed[12],
        summed[13],
        summed[14],
    )


def solution(mesh):
    placed = (
        P(("wide", "narrow"), None),
        P(("wide", "narrow"), None),
        P(("wide", "narrow"), None),
        P(("wide", "narrow"), None),
        P("wide"),
        P("wide"),
        P(None, "wide"),
        P("wide"),
        P(None, "wide"),
        P(None, "wide"),
        P("wide"),
        P(None, "wide"),
        P("wide"),
        P("wide"),
        P("wide"),
        P(None, "wide"),
        P("wide"),
        P(None, "wide"),
        P("wide"),
    )
    return jax.shard_map(
        shards,
        mesh=mesh,
        in_specs=placed,
        out_specs=(
            P(("wide", "narrow"), None),
            P(("wide", "narrow"), None),
            P("wide"),
            P("wide"),
            P(None, "wide"),
            P("wide"),
            P(None, "wide"),
            P(None, "wide"),
            P("wide"),
            P(None, "wide"),
            P("wide"),
            P("wide"),
            P("wide"),
            P(None, "wide"),
            P("wide"),
            P(None, "wide"),
            P("wide"),
        ),
        check_vma=False,
    )
```

profile of v0, /device:TPU:9, one launch (start us, length us, event | category | flops | bytes accessed | tf_op | source)
XLA Modules:
  0.0 1359.5 jit_solution(17243252473467389047)
XLA Ops:
  23.4 57.1 %all-reduce.19 = (bf16[768]{0:T(1024)(128)(2,1)S(1)}, bf16[768]{0:T(1024)(128)(2,1)S(1)}, bf16[768]{0:T(1024)(128)(2,1)S(1)}, bf16[768]{0:T(1024)(128)(2,1)S(1)}...) all-reduce(bf16[768]{0:T(1024)(128)(2,1)S(1)} %dynamic-update-slice, ...), channel_id=1, replica_groups=mesh['wide'=16,'narrow'=2] {'wide'}, use_global_device_ids=true, to_apply=%add.2 | all-reduce | flops 9216 | bytes 36864
  85.4 2.6 copy.53
  89.5 3.9 convolution_convert_fusion
  93.4 29.8 %all-gather.9.cloned.1.call-done = bf16[768,768]{0,1:T(8,128)(2,1)} async-done(((bf16[768,48]{0,1:T(8,128)(2,1)}), bf16[768,768]{0,1:T(8,128)(2,1)}) %all-gather.9.cloned.1.call-update) | async-done | bytes 1179664 | tf_op jit(solution)/shard_map/all_gather | solution.py:86
  123.3 2.9 add_convert_fusion.2
  126.2 23.7 %fusion.6 = (f32[16,1024]{1,0:T(8,128)S(1)}, f32[16,1024,1024]{1,2,0:T(8,128)}) fusion(pred[1024,1024]{0,1:T(8,128)(4,1)S(1)} %fusion.24, bf16[1024,16,48]{0,2,1:T(8,128)(2,1)S(1)} %bitcast.57, bf16[1024,16,48]{0,2,1:T(8,128)(2,1)S(1)} %bitcast.60), kind=kOutput, calls=%fused_computation.11 | convolution fusion | flops 1660928000 | bytes 71368704 | tf_op jit(solution)/shard_map/qhd,khd->hqk/dot_general | solution.py:52
  149.9 21.8 %fusion = f32[16,1024]{1,0:T(8,128)S(1)} fusion(f32[16,1024]{1,0:T(8,128)S(1)} %get-tuple-element.96, f32[16,1024,1024]{1,2,0:T(8,128)} %get-tuple-element.97, pred[1024,1024]{0,1:T(8,128)(4,1)S(1)} %fusion.24), kind=kLoop, calls=%fused_computation.6 | loop fusion | flops 67092480 | bytes 68288512 | tf_op jit(solution)/shard_map/reduce_sum | solution.py:129
  172.4 8.4 all-gather.7.cloned.1.call-done
  180.7 2.8 add_convert_fusion.3
  184.7 27.5 %fusion.44 = bf16[16,48,1024]{2,1,0:T(8,128)(2,1)} fusion(bf16[1024,16,48]{0,2,1:T(8,128)(2,1)S(1)} %bitcast.61, f32[16,1024]{1,0:T(8,128)S(1)} %fusion, f32[16,1024]{1,0:T(8,128)S(1)} %get-tuple-element.96, f32[16,1024,1024]{1,2,0:T(8,128)} %get-tuple-element.97, pred[1024,1024]{0,1:T(8,128)(4,1)S(1)} %fusion.24), kind=kOutput, calls=%fused_computation.83 | convolution fusion | flops 1695285248 | bytes 71434240 | tf_op jit(solution)/shard_map/hqk,khd->qhd/dot_general | solution.py:133
  212.2 25.8 %all-gather.13.cloned.1.call-done = bf16[768,768]{0,1:T(8,128)(2,1)} async-done(((bf16[768,48]{0,1:T(8,128)(2,1)}), bf16[768,768]{0,1:T(8,128)(2,1)}) %all-gather.13.cloned.1.call-update) | async-done | bytes 1179664 | tf_op jit(solution)/shard_map/all_gather | solution.py:91
  238.1 3.2 fusion.67
  243.4 77.0 %all-gather.15.cloned.1.call-done = bf16[768,3072]{0,1:T(8,128)(2,1)} async-done(((bf16[768,192]{0,1:T(8,128)(2,1)}), bf16[768,3072]{0,1:T(8,128)(2,1)}) %all-gather.15.cloned.1.call-update) | async-done | bytes 4718608 | tf_op jit(solution)/shard_map/all_gather | solution.py:95
  320.3 38.0 %fusion.9 = (bf16[1024,3072]{1,0:T(8,128)(2,1)}, f32[1024,3072]{1,0:T(8,128)}) fusion(f32[3072]{0:T(1024)S(1)} %copy-done.35, bf16[768,3072]{0,1:T(8,128)(2,1)} %all-gather.15.cloned.1.call-done, f32[1024,768]{0,1:T(8,128)} %copy-done, f32[768]{0:T(1024)S(1)} %copy-done.38, f32[768]{0:T(1024)S(1)} %copy-done.21, f32[1024]{0:T(1024)S(1)} %add_rsqrt_fusion, ...), kind=kOutput, calls=%fused_computation.16 | convolution fusion | flops 5043388416 | bytes 26765312 | tf_op jit(solution)/shard_map/dot_general | solution.py:12
  358.4 43.0 %all-gather.17.cloned.1.call-done = bf16[3072,768]{0,1:T(8,128)(2,1)} async-done(((bf16[3072,48]{0,1:T(8,128)(2,1)}), bf16[3072,768]{0,1:T(8,128)(2,1)}) %all-gather.17.cloned.1.call-update) | async-done | bytes 4718608 | tf_op jit(solution)/shard_map/all_gather | solution.py:97
  401.4 13.7 %convert_reduce_fusion = (f32[3072]{0:T(1024)}, bf16[1024,3072]{1,0:T(8,128)(2,1)S(1)}) fusion(f32[1024,3072]{1,0:T(8,128)} %get-tuple-element.101, f32[3072]{0:T(1024)S(1)} %copy-done.35, bf16[3072,768]{0,1:T(8,128)(2,1)} %all-gather.17.cloned.1.call-done, bf16[1024,768]{0,1:T(8,128)(2,1)S(1)} %copy-done.11, f32[1024]{0:T(1024)S(1)} %bitcast.70), kind=kOutput, calls=%fused_computation.23 | convolution fusion | flops 4875088896 | bytes 25194496 | tf_op jit(solution)/shard_map/dot_general | solution.py:22
  415.1 7.4 fusion.68
  422.4 3.6 copy.54
  426.0 4.6 multiply_reduce_fusion.1
  430.7 2.3 convert_reduce_fusion.3
  434.7 2.9 fusion.48
  437.9 4.5 convolution_convert_fusion.1
  442.4 27.2 %convert_reduce_fusion.4 = (f32[16,48]{1,0:T(8,128)}, bf16[16,48,1024]{2,1,0:T(8,128)(2,1)}) fusion(bf16[1024,16,48]{0,2,1:T(8,128)(2,1)} %bitcast.63, f32[16,1024]{1,0:T(8,128)S(1)} %copy-done.13, f32[16,1024,1024]{1,2,0:T(8,128)} %get-tuple-element.97, pred[1024,1024]{0,1:T(8,128)(4,1)S(1)} %fusion.24), kind=kOutput, calls=%fused_computation.63 | convolution fusion | flops 1680080128 | bytes 71371776 | tf_op jit(solution)/shard_map/hqk,qhd->khd/dot_general | solution.py:188
  469.6 4.3 fusion.57
  474.0 50.7 %multiply_reduce_fusion = (f32[16,1024]{1,0:T(8,128)S(1)}, f32[16,1024,1024]{1,2,0:T(8,128)}) fusion(f32[16,1024]{1,0:T(8,128)S(1)} %copy-done.13, f32[16,1024,1024]{1,2,0:T(8,128)} %get-tuple-element.97, pred[1024,1024]{0,1:T(8,128)(4,1)S(1)} %fusion.24, bf16[1024,16,48]{0,2,1:T(8,128)(2,1)} %bitcast.64, bf16[1024,16,48]{0,2,1:T(8,128)(2,1)} %bitcast.62), kind=kOutput, calls=%fused_computation.1 | convolution fusion | flops 1694482432 | bytes 138543104 | tf_op jit(solution)/shard_map/qhd,khd->hqk/dot_general | solution.py:194
  525.1 54.6 %multiply_convert_fusion = bf16[16,1024,1024]{1,2,0:T(8,128)(2,1)} fusion(f32[16,1024,1024]{1,2,0:T(8,128)} %get-tuple-element.103, f32[16,1024]{1,0:T(8,128)S(1)} %get-tuple-element.102, f32[16,1024]{1,0:T(8,128)S(1)} %copy-done.13, f32[16,1024,1024]{1,2,0:T(8,128)} %get-tuple-element.97, pred[1024,1024]{0,1:T(8,128)(4,1)S(1)} %fusion.24), kind=kLoop, calls=%fused_computation | loop fusion | flops 100663296 | bytes 168951808 | tf_op jit(solution)/shard_map/convert_element_type | solution.py:195
  579.8 17.3 %convert_reduce_fusion.5 = (f32[16,48]{1,0:T(8,128)S(1)}, bf16[16,48,1024]{2,1,0:T(8,128)(2,1)S(1)}) fusion(bf16[1024,16,48]{0,2,1:T(8,128)(2,1)} %bitcast.59, bf16[16,1024,1024]{1,2,0:T(8,128)(2,1)} %multiply_convert_fusion), kind=kOutput, calls=%fused_computation.64 | convolution fusion | flops 1613757696 | bytes 36703232 | tf_op jit(solution)/shard_map/hqk,khd->qhd/dot_general | solution.py:197
  598.2 3.0 fusion.61
  602.6 16.2 %multiply_convert_fusion.1 = bf16[16,48,1024]{2,1,0:T(8,128)(2,1)} fusion(bf16[1024,16,48]{0,2,1:T(8,128)(2,1)S(1)} %bitcast.58, bf16[16,1024,1024]{1,2,0:T(8,128)(2,1)} %multiply_convert_fusion), kind=kOutput, calls=%fused_computation.66 | convolution fusion | flops 1612185600 | bytes 36700160 | tf_op jit(solution)/shard_map/hqk,qhd->khd/dot_general | solution.py:202
  618.8 5.0 fusion.59
  624.2 12.8 fusion.55
  637.6 9.8 fusion.45
  648.8 9.5 add_convert_fusion
  658.3 2.7 copy.62
  661.2 2.9 fusion.69
  666.3 3.8 fusion.37
  670.2 56.7 %all-reduce.18 = (bf16[768]{0:T(1024)(128)(2,1)S(1)}, bf16[768]{0:T(1024)(128)(2,1)S(1)}, bf16[768]{0:T(1024)(128)(2,1)S(1)}, bf16[768]{0:T(1024)(128)(2,1)S(1)}...) all-reduce(f32[768]{0:T(1024)S(1)} %get-tuple-element.53, ...), channel_id=2, replica_groups=mesh['wide'=16,'narrow'=2] {'wide'}, use_global_device_ids=true, to_apply=%region_12.13.clone | all-reduce | flops 9216 | bytes 55296
  727.6 16.6 %all-reduce.20 = (bf16[48]{0:T(256)(128)(2,1)S(1)}, bf16[48]{0:T(256)(128)(2,1)S(1)}, bf16[48]{0:T(256)(128)(2,1)S(1)}, bf16[48]{0:T(256)(128)(2,1)S(1)}, bf16[4...) all-reduce(bf16[48]{0:T(256)(128)(2,1)S(1)} %dynamic-slice.44, ...), channel_id=1, replica_groups=mesh['wide'=16,'narrow'=2] {'narrow'}, use_global_device_ids=true, to_apply=%region_13.14 | all-reduce | flops 576 | bytes 2304 | tf_op jit(solution)/shard_map/psum | solution.py:241
  751.9 80.1 %reduce-scatter.7.cloned.1.call-done = f32[768,48]{0,1:T(8,128)} async-done(((f32[768,768]{0,1:T(8,128)}), f32[768,48]{0,1:T(8,128)}) %reduce-scatter.7.cloned.1.call-update) | async-done | bytes 147472 | tf_op jit(solution)/shard_map/reduce_scatter | solution.py:226
  833.6 131.6 %reduce-scatter.9.cloned.1.call-done = f32[768,48]{0,1:T(8,128)} async-done(((f32[768,768]{0,1:T(8,128)}), f32[768,48]{0,1:T(8,128)}) %reduce-scatter.9.cloned.1.call-update) | async-done | bytes 147472 | tf_op jit(solution)/shard_map/reduce_scatter | solution.py:228
  966.7 175.2 %reduce-scatter.15.cloned.1.call-done = f32[768,192]{0,1:T(8,128)} async-done(((f32[768,3072]{0,1:T(8,128)}), f32[768,192]{0,1:T(8,128)}) %reduce-scatter.15.cloned.1.call-update) | async-done | bytes 589840 | tf_op jit(solution)/shard_map/reduce_scatter | solution.py:235
  1142.0 1.8 convert_element_type.282
  1143.8 174.3 %reduce-scatter.17.cloned.1.call-done = f32[3072,48]{0,1:T(8,128)} async-done(((f32[3072,768]{0,1:T(8,128)}), f32[3072,48]{0,1:T(8,128)}) %reduce-scatter.17.cloned.1.call-update) | async-done | bytes 589840 | tf_op jit(solution)/shard_map/reduce_scatter | solution.py:237
  1319.9 5.5 fusion.36
  1325.4 3.5 copy.63
  1328.9 14.0 %all-reduce.24.cloned.1.call-done = (bf16[768,48]{0,1:T(8,128)(2,1)}, bf16[768,48]{0,1:T(8,128)(2,1)}, bf16[768,48]{0,1:T(8,128)(2,1)}, bf16[768,48]{0,1:T(8,128...) async-done(((bf16[768,48]{0,1:T(8,128)(2,1)}, bf16[768,48]{0,1:T(8,128)(2,1)}, bf16[768,48]{0,1:T(8,128)(2,1)}, bf16[768,48]{0,1:T(8,128)(2,1)}, ...) | async-done | bytes 884752 | tf_op jit(solution)/shard_map/psum | solution.py:243
  1349.1 1.8 convert_element_type.283
  1351.0 1.8 convert_element_type.288
  (206 shorter events, 53.1 us)
Async XLA Ops:
  7.2 82.3 %all-gather.11.cloned.1.call-start = ((), (), s32[]{:S(2)}) async-start(), calls=%async_computation.8 | async-start | bytes 1253376 | tf_op jit(solution)/shard_map/all_gather | solution.py:88
  7.9 115.3 %all-gather.9.cloned.1.call-start = ((), (), s32[]{:S(2)}) async-start(), calls=%async_computation.7 | async-start | bytes 1253376 | tf_op jit(solution)/shard_map/all_gather | solution.py:86
  8.7 172.1 %all-gather.7.cloned.1.call-start = ((), (), s32[]{:S(2)}) async-start(), calls=%async_computation.6 | async-start | bytes 1253376 | tf_op jit(solution)/shard_map/all_gather | solution.py:89
  9.4 228.6 %all-gather.13.cloned.1.call-start = ((), (), s32[]{:S(2)}) async-start(), calls=%async_computation.9 | async-start | bytes 1253376 | tf_op jit(solution)/shard_map/all_gather | solution.py:91
  10.0 310.3 %all-gather.15.cloned.1.call-start = ((), (), s32[]{:S(2)}) async-start(), calls=%async_computation.10 | async-start | bytes 5013504 | tf_op jit(solution)/shard_map/all_gather | solution.py:95
  10.6 390.8 %all-gather.17.cloned.1.call-start = ((), (), s32[]{:S(2)}) async-start(), calls=%async_computation.11 | async-start | bytes 5013504 | tf_op jit(solution)/shard_map/all_gather | solution.py:97
  11.1 737.7 %reduce-scatter.13.cloned.1.call-start = ((), (), s32[]{:S(2)}) async-start(), calls=%async_computation.15 | async-start | bytes 2506752 | tf_op jit(solution)/shard_map/reduce_scatter | solution.py:231
  80.5 100.2 %copy-start.25 = (f32[768]{0:T(1024)}, f32[768]{0:T(1024)S(1)}, u32[]{:S(2)}) copy-start(f32[768]{0:T(1024)S(1)} %convert_element_type.222) | copy-start | bytes 9220
  80.5 100.2 %copy-start.40 = (f32[768]{0:T(1024)}, f32[768]{0:T(1024)S(1)}, u32[]{:S(2)}) copy-start(f32[768]{0:T(1024)S(1)} %convert_element_type.223) | copy-start | bytes 9220
  84.6 153.4 %copy-start.4 = (bf16[1024,768]{0,1:T(8,128)(2,1)}, bf16[1024,768]{0,1:T(8,128)(2,1)S(1)}, u32[]{:S(2)}) copy-start(bf16[1024,768]{0,1:T(8,128)(2,1)S(1)} %copy.50) | copy-start | bytes 4718596
  84.9 95.8 %copy-start.19 = (f32[1024]{0:T(1024)}, f32[1024]{0:T(1024)S(1)}, u32[]{:S(2)}) copy-start(f32[1024]{0:T(1024)S(1)} %broadcast_multiply_fusion.5) | copy-start | bytes 12292
  85.4 95.4 %copy-start.27 = (f32[1024]{0:T(1024)}, f32[1024]{0:T(1024)S(1)}, u32[]{:S(2)}) copy-start(f32[1024]{0:T(1024)S(1)} %add_rsqrt_fusion.1) | copy-start | bytes 12292
  126.2 23.7 %copy-start.8 = (bf16[1024,768]{0,1:T(8,128)(2,1)}, bf16[1024,768]{0,1:T(8,128)(2,1)S(1)}, u32[]{:S(2)}) copy-start(bf16[1024,768]{0,1:T(8,128)(2,1)S(1)} %add_convert_fusion.2) | copy-start | bytes 4718596
  184.7 53.3 %copy-start.42 = (f32[768]{0:T(1024)S(1)}, f32[768]{0:T(1024)}, u32[]{:S(2)}) copy-start(f32[768]{0:T(1024)} %convert_element_type.234) | copy-start | bytes 9220
  241.3 79.1 %copy-start.21 = (f32[768]{0:T(1024)S(1)}, f32[768]{0:T(1024)}, u32[]{:S(2)}) copy-start(f32[768]{0:T(1024)} %convert_element_type.235) | copy-start | bytes 9220
  241.3 79.1 %copy-start.35 = (f32[3072]{0:T(1024)S(1)}, f32[3072]{0:T(1024)}, u32[]{:S(2)}) copy-start(f32[3072]{0:T(1024)} %convert_element_type.238) | copy-start | bytes 36868
  241.3 79.0 %copy-start.38 = (f32[768]{0:T(1024)S(1)}, f32[768]{0:T(1024)}, u32[]{:S(2)}) copy-start(f32[768]{0:T(1024)} %convert_element_type.236) | copy-start | bytes 9220
  241.3 189.3 %copy-start.17 = (f32[1024]{0:T(1024)}, f32[1024]{0:T(1024)S(1)}, u32[]{:S(2)}) copy-start(f32[1024]{0:T(1024)S(1)} %broadcast_multiply_fusion.4) | copy-start | bytes 12292
  243.3 187.2 %copy-start.23 = (f32[1024]{0:T(1024)}, f32[1024]{0:T(1024)S(1)}, u32[]{:S(2)}) copy-start(f32[1024]{0:T(1024)S(1)} %add_rsqrt_fusion) | copy-start | bytes 12292
  243.3 158.0 %copy-start.11 = (bf16[1024,768]{0,1:T(8,128)(2,1)S(1)}, bf16[1024,768]{0,1:T(8,128)(2,1)}, u32[]{:S(2)}) copy-start(bf16[1024,768]{0,1:T(8,128)(2,1)} %copy.53) | copy-start | bytes 4718596
  243.3 158.0 %copy-start.30 = (f32[1,1024]{1,0:T(1,128)S(1)}, f32[1,1024]{1,0:T(1,128)}, u32[]{:S(2)}) copy-start(f32[1,1024]{1,0:T(1,128)} %convert_element_type.243) | copy-start | bytes 12292
  401.4 13.7 %copy-start.45 = (bf16[768,3072]{0,1:T(8,128)(2,1)S(1)}, bf16[768,3072]{0,1:T(8,128)(2,1)}, u32[]{:S(2)}) copy-start(bf16[768,3072]{0,1:T(8,128)(2,1)} %all-gather.15.cloned.1.call-done) | copy-start | bytes 14155780
  415.1 7.4 copy-start.51
  426.0 4.6 copy-start.1
  426.0 4.7 copy-start.3
  430.7 4.0 copy-start.50
  437.6 4.7 copy-start.13
  437.6 312.8 %reduce-scatter.11.cloned.1.call-start = ((), (), s32[]{:S(2)}) async-start(), calls=%async_computation.14 | async-start | bytes 2506752 | tf_op jit(solution)/shard_map/reduce_scatter | solution.py:229
  442.3 27.3 %copy-start.5 = (bf16[1024,768]{0,1:T(8,128)(2,1)S(1)}, bf16[1024,768]{0,1:T(8,128)(2,1)}, u32[]{:S(2)}) copy-start(bf16[1024,768]{0,1:T(8,128)(2,1)} %copy-done.4) | copy-start | bytes 4718596
  442.3 27.3 %copy-start.20 = (f32[1024]{0:T(1024)S(1)}, f32[1024]{0:T(1024)}, u32[]{:S(2)}) copy-start(f32[1024]{0:T(1024)} %copy-done.19) | copy-start | bytes 12292
  442.3 27.3 %copy-start.26 = (f32[768]{0:T(1024)S(1)}, f32[768]{0:T(1024)}, u32[]{:S(2)}) copy-start(f32[768]{0:T(1024)} %copy-done.25) | copy-start | bytes 9220
  442.3 27.3 %copy-start.28 = (f32[1024]{0:T(1024)S(1)}, f32[1024]{0:T(1024)}, u32[]{:S(2)}) copy-start(f32[1024]{0:T(1024)} %copy-done.27) | copy-start | bytes 12292
  442.4 27.3 %copy-start.41 = (f32[768]{0:T(1024)S(1)}, f32[768]{0:T(1024)}, u32[]{:S(2)}) copy-start(f32[768]{0:T(1024)} %copy-done.40) | copy-start | bytes 9220
  524.7 307.4 %reduce-scatter.7.cloned.1.call-start = ((), (), s32[]{:S(2)}) async-start(), calls=%async_computation.12 | async-start | bytes 2506752 | tf_op jit(solution)/shard_map/reduce_scatter | solution.py:226
  601.2 363.9 %reduce-scatter.9.cloned.1.call-start = ((), (), s32[]{:S(2)}) async-start(), calls=%async_computation.13 | async-start | bytes 2506752 | tf_op jit(solution)/shard_map/reduce_scatter | solution.py:228
  618.8 5.3 copy-start.2
  618.8 5.3 copy-start.18
  618.8 5.3 copy-start.22
  618.8 5.3 copy-start.24
  618.8 5.3 copy-start.39
  623.9 518.1 %reduce-scatter.15.cloned.1.call-start = ((), (), s32[]{:S(2)}) async-start(), calls=%async_computation.16 | async-start | bytes 10027008 | tf_op jit(solution)/shard_map/reduce_scatter | solution.py:235
  637.0 681.1 %reduce-scatter.17.cloned.1.call-start = ((), (), s32[]{:S(2)}) async-start(), calls=%async_computation.17 | async-start | bytes 10027008 | tf_op jit(solution)/shard_map/reduce_scatter | solution.py:237
  647.5 695.5 %all-reduce.24.cloned.1.call-start = ((), (), s32[]{:S(2)}) async-start(), calls=%async_computation.18 | async-start | bytes 1769472 | tf_op jit(solution)/shard_map/psum | solution.py:243
  666.3 3.8 copy-start.32
  666.3 3.8 copy-start.33
  666.3 3.8 copy-start.34
  666.3 3.8 copy-start.36
  666.3 3.8 copy-start.43
  (17 other events, 35.4 us)
Sparse Core Ops, SparseCore 0:
  10.8 55.0 all-gather.10
  68.7 54.5 all-gather.8
  126.1 54.6 all-gather.6
  183.4 54.6 all-gather.12
  240.7 79.5 all-gather.14
  323.0 78.3 all-gather.16
  437.7 127.5 reduce-scatter.12
  570.3 128.3 reduce-scatter.10
  703.6 128.4 reduce-scatter.6
  836.8 128.2 reduce-scatter.8
  970.9 171.0 reduce-scatter.14
  1147.5 170.5 reduce-scatter.16
  1322.0 20.8 all-reduce.23
where the time goes:
time: 1370 us; the launch traced here: 1360 us
  waiting for transfers between devices  763 us (56%)
  matrix products  294 us (21%)
  blocking collectives  130 us (9%)
  other arithmetic  121 us (9%)
  local copies, waits for them, and re-layouts  32.4 us (2%)
  between operations  17.3 us (1%)
    reduce_scatter x1, waiting for transfers between devices, shards(): lax.psum_scatter(grad_w_hidden, 'wide', scatter_dimension=1, tiled=True)  175 us
    reduce_scatter x1, waiting for transfers between devices, shards(): lax.psum_scatter(grad_w_proj, 'wide', scatter_dimension=1, tiled=True)  174 us
    reduce_scatter x1, waiting for transfers between devices, shards(): lax.psum_scatter(grad_w_key, 'wide', scatter_dimension=1, tiled=True)  132 us
    unnamed x2, blocking collectives  114 us
    reduce_scatter x1, waiting for transfers between devices, shards(): lax.psum_scatter(grad_w_query, 'wide', scatter_dimension=1, tiled=True)  80.1 us
    all_gather x1, waiting for transfers between devices, shards(): lax.all_gather(w_hidden, 'wide', axis=1, tiled=True)  77 us
    dot_general x6, matrix products, matmul(): return jnp.dot(left, right, preferred_element_type=jnp.float32)  60.4 us
    convert_element_type x1, other arithmetic, shards(): (probs * (d_probs - jnp.sum(d_probs * probs, -1, keepdims=True))).astype(...  54.6 us
  transfers between devices with their start and end apart: 13, of which 10 were waited for; matrix products, arithmetic and copies ran while one was open for 29% of the time, Pallas kernels for 0%

commit v1 on v0

v1 whole, which is shorter than its diff:
```python
import functools
import math

import jax
import jax.numpy as jnp
from jax import lax
from jax.experimental import pallas as pl
from jax.experimental.pallas import tpu as pltpu
from jax.sharding import PartitionSpec as P

HEADS = 16
F32 = jnp.float32
BF16 = jnp.bfloat16
MESH = pl.DeviceIdType.MESH
LOG2E = math.log2(math.e)
MASKED = -1e30
SPARE = 16
CHUNK = 256


def dims(left, right, a, b):
    return lax.dot_general(left, right, (((a,), (b,)), ((), ())), preferred_element_type=F32)


def chip_axes(chips):
    if chips == 16:
        return ((4, 4), (2, 2), (1, 2))
    return ((1, chips),)


def axis_orders(axes):
    if len(axes) == 3:
        return ((0, 1, 2), (2, 0, 1))
    return (tuple(range(len(axes))),) * 2


def place(me, axis):
    stride, size = axis
    return lax.rem(lax.div(me, stride), size)


def peer(me, axis, step):
    stride, size = axis
    mine = place(me, axis)
    other = lax.rem(mine + step, size)
    return me + (other - mine) * stride


def greet(me, core, axes):
    barrier = pltpu.get_barrier_semaphore()
    count = 1
    pl.semaphore_signal(barrier, 1, device_id=(me, 1 - core), device_id_type=MESH)
    for axis in axes:
        for step in range(1, axis[1]):
            pl.semaphore_signal(
                barrier, 1, device_id=(peer(me, axis, step), core), device_id_type=MESH
            )
            count += 1
    pl.semaphore_wait(barrier, count)


def held_blocks(me, axes, done):
    ids = [me]
    for a in done:
        stride, size = axes[a]
        ids = [i + (v - place(me, axes[a])) * stride for i in ids for v in range(size)]
    return ids


def half(ref, block, c):
    width = ref.shape[-1] // 2
    return ref.at[block, :, pl.ds(c * width, width)]


def flat_half(ref, c):
    width = ref.shape[-1] // 2
    return ref.at[:, pl.ds(c * width, width)]


def gather_plan(ins, outs, sems, me, c, axes):
    order = axis_orders(axes)[c]
    send, recv, pass_send, pass_recv, own = sems
    chips = outs[0].shape[0]
    stages = []
    count = [0]
    passed = [0]
    pending = []

    def hand_over(ids, first=False):
        for n, block in enumerate(ids):
            for k, (src, dst) in enumerate(zip(ins, outs)):
                slot = passed[0] + n * len(outs) + k
                source = flat_half(src, c) if first else half(dst, block, c)
                pltpu.make_async_remote_copy(
                    source, half(dst, block, c), pass_send.at[slot], pass_recv.at[slot],
                    device_id=(me, 1 - c), device_id_type=MESH,
                ).start()
        passed[0] += len(ids) * len(outs)

    def copies(number):
        axis = axes[order[number]]
        ids = held_blocks(me, axes, order[:number])
        base = sum(
            (axes[order[m]][1] - 1) * math.prod(axes[a][1] for a in order[:m]) * len(outs)
            for m in range(number)
        )
        out = []
        slot = base
        for step in range(1, axis[1]):
            target = peer(me, axis, step)
            source = peer(me, axis, axis[1] - step)
            for block in ids:
                for k, (src, dst) in enumerate(zip(ins, outs)):
                    first = number == 0
                    out.append((
                        pltpu.make_async_remote_copy(
                            flat_half(src, c) if first else half(dst, block, c),
                            half(dst, block, c), send.at[slot], recv.at[slot],
                            device_id=(target, c), device_id_type=MESH,
                        ),
                        block + (source - me),
                    ))
                    slot += 1
        return out

    def begin(number):
        for copy, _ in copies(number):
            copy.start()

    def land(number):
        got = copies(number)
        for copy, _ in got:
            copy.wait_recv()
        return [block for _, block in got[:: len(outs)]]

    def first():
        for k, (src, dst) in enumerate(zip(ins, outs)):
            pltpu.make_async_copy(src, dst.at[me], own.at[k]).start()
        begin(0)

    def middle(number):
        def run():
            blocks = land(number)
            if number == 0:
                for k, (src, dst) in enumerate(zip(ins, outs)):
                    pltpu.make_async_copy(src, dst.at[me], own.at[k]).wait()
            if number + 1 < len(order):
                begin(number + 1)
            hand_over(blocks)
        return run

    def last():
        total = (chips - 1) * len(outs)
        for number in range(len(order)):
            for copy, _ in copies(number):
                copy.wait_send()
        for k in range(total):
            dst = outs[k % len(outs)]
            pltpu.make_async_remote_copy(
                half(dst, me, c), half(dst, me, 1 - c), pass_send.at[k], pass_recv.at[k],
                device_id=(me, 1 - c), device_id_type=MESH,
            ).wait()

    stages.append(first)
    for number in range(len(order)):
        stages.append(middle(number))
    stages.append(last)
    return stages


def gather_sems(chips, arrays):
    total = (chips - 1) * arrays
    return [pltpu.SemaphoreType.DMA((total,)) for _ in range(4)] + [
        pltpu.SemaphoreType.DMA((arrays,))
    ]


def gather_kernel(chips, arrays, *refs):
    ins, outs, sems = refs[:arrays], refs[arrays : 2 * arrays], refs[2 * arrays :]
    me, core = lax.axis_index("wide"), lax.axis_index("narrow")
    axes = chip_axes(chips)
    greet(me, core, axes)
    for c in range(2):
        @pl.when(core == c)
        def _():
            for stage in gather_plan(ins, outs, sems, me, c, axes):
                stage()


def gather(arrays, chips, ident):
    vm = pl.BlockSpec(memory_space=pltpu.VMEM)
    return pl.pallas_call(
        functools.partial(gather_kernel, chips, len(arrays)),
        out_shape=[jax.ShapeDtypeStruct((chips,) + a.shape, a.dtype) for a in arrays],
        in_specs=[vm] * len(arrays),
        out_specs=[pl.BlockSpec(memory_space=pl.ANY)] * len(arrays),
        scratch_shapes=gather_sems(chips, len(arrays)),
        compiler_params=pltpu.CompilerParams(collective_id=ident, has_side_effects=True),
    )(*arrays)


def phase_base(axes, order, number, arrays):
    return sum(
        (axes[order[m]][1] - 1) * math.prod(axes[a][1] for a in order[:m]) * arrays
        for m in range(number)
    )


def scatter_plan(ins, outs, accs, halves, landed, results, sems, me, c, axes):
    order = axis_orders(axes)[c]
    send, recv, swap_send, swap_recv, own, out_sem = sems
    arrays = len(ins)

    def swap():
        copies = []
        for k in range(arrays):
            width = ins[k].shape[-1] // 2
            copies.append((
                pltpu.make_async_remote_copy(
                    ins[k].at[:, :, pl.ds((1 - c) * width, width)], halves[k],
                    swap_send.at[k], swap_recv.at[k],
                    device_id=(me, 1 - c), device_id_type=MESH,
                ),
                pltpu.make_async_copy(
                    ins[k].at[:, :, pl.ds(c * width, width)], accs[k], own.at[k]
                ),
            ))
        return copies

    def copies(number):
        axis = axes[order[number]]
        ids = held_blocks(me, axes, order[:number])
        slot = phase_base(axes, order, number, 1)
        out = []
        for step in range(1, axis[1]):
            target = peer(me, axis, step)
            for block in ids:
                for k in range(arrays):
                    n = slot * arrays + k
                    out.append((
                        pltpu.make_async_remote_copy(
                            accs[k].at[block + (target - me)], landed[k].at[slot],
                            send.at[n], recv.at[n],
                            device_id=(target, c), device_id_type=MESH,
                        ),
                        block, k, slot,
                    ))
                slot += 1
        return out

    def begin(number):
        for copy, *_ in copies(number):
            copy.start()

    def first():
        for remote, local in swap():
            remote.start()
            local.start()

    def add_pair():
        for remote, local in swap():
            local.wait()
            remote.wait()
        for k in range(arrays):
            @pl.loop(0, accs[k].shape[0])
            def _(block):
                accs[k][block] = (
                    accs[k][block].astype(F32) + halves[k][block].astype(F32)
                ).astype(BF16)
        begin(len(order) - 1)

    def add(number):
        def run():
            got = copies(number)
            for copy, *_ in got:
                copy.wait()
            groups = {}
            for position, (_, block, k, slot) in enumerate(got):
                ids = math.prod(axes[a][1] for a in order[:number])
                groups.setdefault((position // arrays % ids, k), (block, []))[1].append(slot)
            for (_, k), (block, slots) in groups.items():
                total = accs[k][block].astype(F32)
                for slot in slots:
                    total = total + landed[k][slot].astype(F32)
                if number:
                    accs[k][block] = total.astype(BF16)
                else:
                    width = total.shape[-1]
                    results[k][:, pl.ds(c * width, width)] = total
            if number:
                begin(number - 1)
            else:
                for copy in finals():
                    copy.start()
        return run

    def finals():
        return [
            pltpu.make_async_remote_copy(
                flat_half(results[k], c), flat_half(results[k], c),
                swap_send.at[arrays + k], swap_recv.at[arrays + k],
                device_id=(me, 1 - c), device_id_type=MESH,
            )
            for k in range(arrays)
        ]

    def last():
        outgoing = [pltpu.make_async_copy(results[k], outs[k], out_sem.at[k]) for k in range(arrays)]
        for copy, out in zip(finals(), outgoing):
            copy.wait()
            out.start()
        for out in outgoing:
            out.wait()

    return [first, add_pair] + [add(n) for n in reversed(range(len(order)))] + [last]


def scatter_scratch(arrays):
    chips = arrays[0].shape[0]
    number = len(arrays)
    scratch = []
    for rows in (chips, chips, chips - 1):
        scratch += [pltpu.VMEM((rows, a.shape[1], a.shape[2] // 2), BF16) for a in arrays]
    scratch += [pltpu.VMEM(a.shape[1:], F32) for a in arrays]
    dma = pltpu.SemaphoreType.DMA
    return scratch + [dma(((chips - 1) * number,)) for _ in range(2)] + [
        dma((n,)) for n in (2 * number, 2 * number, number, number)
    ]


def scatter_parts(arrays, refs):
    parts = [refs[n * arrays : (n + 1) * arrays] for n in range(4)]
    return parts, refs[4 * arrays :]


def scatter_kernel(chips, arrays, *refs):
    ins, outs = refs[:arrays], refs[arrays : 2 * arrays]
    parts, sems = scatter_parts(arrays, refs[2 * arrays :])
    me, core = lax.axis_index("wide"), lax.axis_index("narrow")
    axes = chip_axes(chips)
    greet(me, core, axes)
    for c in range(2):
        @pl.when(core == c)
        def _():
            for stage in scatter_plan(ins, outs, *parts, sems, me, c, axes):
                stage()


def scatter(arrays, ident):
    any_space = pl.BlockSpec(memory_space=pl.ANY)
    return pl.pallas_call(
        functools.partial(scatter_kernel, arrays[0].shape[0], len(arrays)),
        out_shape=[jax.ShapeDtypeStruct(a.shape[1:], F32) for a in arrays],
        in_specs=[any_space] * len(arrays),
        out_specs=[any_space] * len(arrays),
        scratch_shapes=scatter_scratch(arrays),
        compiler_params=pltpu.CompilerParams(
            collective_id=ident, has_side_effects=True, vmem_limit_bytes=60 * 2**20
        ),
    )(*arrays)


def forward_head(qkv, mask, out, lse, head_dim):
    count = qkv.shape[-1]
    factor = head_dim**-0.5 * LOG2E
    keys = qkv[0, head_dim : 2 * head_dim, :]
    value = qkv[0, 2 * head_dim : 3 * head_dim + SPARE, :]

    for start in range(0, count, CHUNK):
        part = pl.ds(start, CHUNK)
        raw = dims(keys, qkv[0, :head_dim, part], 0, 0) * factor + mask[:, part].astype(F32)
        top = jnp.max(raw, 0, keepdims=True)
        probs = jnp.exp2(raw - top).astype(BF16)
        both = dims(value, probs, 1, 0)
        total = both[head_dim : head_dim + 1]
        out[0, :, part] = (both[:head_dim] / total).astype(BF16)
        lse[0, :, part] = top + jnp.log2(total)


def backward_head(qkv, mask, out, d_out, lse, grad, d_key, d_value, head_dim):
    count = qkv.shape[-1]
    scale = head_dim**-0.5
    factor = scale * LOG2E
    keys = qkv[0, head_dim : 2 * head_dim, :]
    value = qkv[0, 2 * head_dim : 3 * head_dim, :]

    for start in range(0, count, CHUNK):
        part = pl.ds(start, CHUNK)
        query = qkv[0, :head_dim, part]
        d_part = d_out[0, :, part]
        probs = jnp.exp2(
            dims(keys, query, 0, 0) * factor + (mask[:, part].astype(F32) - lse[0, :, part])
        )
        share = jnp.sum(d_part.astype(F32) * out[0, :, part].astype(F32), 0, keepdims=True)
        d_probs = dims(value, d_part, 0, 0)
        d_scores = (probs * (d_probs - share)).astype(BF16)
        probs_low = probs.astype(BF16)
        grad[0, :head_dim, part] = (dims(keys, d_scores, 1, 0) * scale).astype(BF16)
        more_value = dims(d_part, probs_low, 1, 1)
        more_key = dims(query, d_scores, 1, 1)
        if start == 0:
            d_value[...] = more_value
            d_key[...] = more_key
        else:
            d_value[...] += more_value
            d_key[...] += more_key
    grad[0, head_dim : 2 * head_dim, :] = (d_key[...] * scale).astype(BF16)
    grad[0, 2 * head_dim : 3 * head_dim, :] = d_value[...].astype(BF16)
    grad[0, 3 * head_dim :, :] = jnp.zeros((SPARE, count), BF16)


def head_spec(rows, count):
    return pl.BlockSpec((1, rows, count), lambda h: (h, 0, 0))


def attention(qkv, mask):
    rows, count = qkv.shape[1:]
    head_dim = (rows - SPARE) // 3

    def body(qkv_ref, mask_ref, out, lse):
        forward_head(qkv_ref, mask_ref, out, lse, head_dim)

    return pl.pallas_call(
        body,
        grid=(HEADS,),
        out_shape=[
            jax.ShapeDtypeStruct((HEADS, head_dim, count), BF16),
            jax.ShapeDtypeStruct((HEADS, 1, count), F32),
        ],
        in_specs=[head_spec(rows, count), pl.BlockSpec((count, count), lambda h: (0, 0))],
        out_specs=[head_spec(head_dim, count), head_spec(1, count)],
        compiler_params=pltpu.CompilerParams(vmem_limit_bytes=60 * 2**20),
    )(qkv, mask)


def attention_back(qkv, mask, out, d_out, lse):
    rows, count = qkv.shape[1:]
    head_dim = (rows - SPARE) // 3

    def body(qkv_ref, mask_ref, out_ref, d_out_ref, lse_ref, grad, d_key, d_value):
        backward_head(
            qkv_ref, mask_ref, out_ref, d_out_ref, lse_ref, grad, d_key, d_value, head_dim
        )

    return pl.pallas_call(
        body,
        grid=(HEADS,),
        out_shape=jax.ShapeDtypeStruct((HEADS, rows, count), BF16),
        in_specs=[
            head_spec(rows, count),
            pl.BlockSpec((count, count), lambda h: (0, 0)),
            head_spec(head_dim, count),
            head_spec(head_dim, count),
            head_spec(1, count),
        ],
        out_specs=head_spec(rows, count),
        scratch_shapes=[pltpu.VMEM((head_dim, count), F32)] * 2,
        compiler_params=pltpu.CompilerParams(vmem_limit_bytes=60 * 2**20),
    )(qkv, mask, out, d_out, lse)


def norm(values):
    centred = values - jnp.mean(values, -1, keepdims=True)
    factor = lax.rsqrt(jnp.mean(centred * centred, -1, keepdims=True) + 1e-05)
    return centred * factor, factor


def norm_back(grad, normed, factor, gain):
    scaled = grad * gain
    inner = (
        scaled
        - jnp.mean(scaled, -1, keepdims=True)
        - normed * jnp.mean(scaled * normed, -1, keepdims=True)
    )
    return factor * inner, jnp.sum(grad * normed, 0), jnp.sum(grad, 0)


def gelu_slope(values):
    cdf = 0.5 * (1.0 + lax.erf(values * (1.0 / math.sqrt(2.0))))
    pdf = jnp.exp(-0.5 * values * values) * (1.0 / math.sqrt(2.0 * math.pi))
    return cdf + values * pdf


def row_sums(values):
    return jnp.sum(values.astype(F32), 0)


def widen(vector, width):
    return jnp.pad(vector, (0, width - vector.shape[0]))


def shards(
    chips,
    replicas,
    tokens,
    segment,
    keep,
    cotangent,
    gain_one,
    bias_one,
    w_query,
    b_query,
    w_key,
    w_value,
    b_value,
    w_out,
    b_out,
    gain_two,
    bias_two,
    w_hidden,
    b_hidden,
    w_proj,
    b_proj,
):
    own_copies = chips == HEADS and replicas == 2
    count, width = tokens.shape
    head_dim = width // HEADS
    hidden = w_hidden.shape[1] * chips
    vectors = (gain_one, bias_one, b_query, b_value, b_out, gain_two, bias_two, b_hidden, b_proj)
    packed = jnp.stack([widen(v, width) for v in vectors])
    packed = jnp.pad(packed, ((0, SPARE - len(vectors)), (0, 0)))

    if own_copies:
        first = jnp.concatenate([w_query.T, w_key.T, w_value.T, packed], 0)
        (first,) = gather([first], chips, 0)
        out_t, hidden_t, proj_t = gather([w_out.T, w_hidden.T, w_proj.T], chips, 1)
        joined_t = first
        vector_rows = first[:, 3 * head_dim :, :]
    else:
        whole = [
            lax.all_gather(w.T, "wide", axis=0, tiled=True) for w in (w_query, w_key, w_value)
        ]
        whole = [w.reshape(HEADS, head_dim, width) for w in whole]
        whole.append(jnp.zeros((HEADS, SPARE, width), BF16))
        joined_t = jnp.concatenate(whole, 1)
        vector_rows = lax.all_gather(packed, "wide", axis=0, tiled=False)
        out_t, hidden_t, proj_t = [
            lax.all_gather(w.T, "wide", axis=0, tiled=False) for w in (w_out, w_hidden, w_proj)
        ]
    out_t = out_t.reshape(width, width)
    hidden_t = hidden_t.reshape(hidden, width)
    proj_t = proj_t.reshape(width, hidden)
    joined_t = joined_t.reshape(HEADS * (3 * head_dim + SPARE), width)
    gain_one_f, bias_one_f, b_query_f, b_value_f, b_out_f, gain_two_f, bias_two_f, b_hidden_f, b_proj_f = [
        vector_rows[:, n, : v.shape[0]].reshape(-1).astype(F32) for n, v in enumerate(vectors)
    ]

    live = keep[0]
    seg = segment[0]
    index = jnp.arange(count)
    allowed = (seg[:, None] == seg[None, :]) & (
        (live[:, None] > 0) | (index[:, None] == index[None, :])
    )
    mask = jnp.where(allowed, 0.0, MASKED).astype(BF16)

    x = tokens.astype(F32)
    xhat_one, factor_one = norm(x)
    h_one = (xhat_one * gain_one_f + bias_one_f).astype(BF16)
    block = 3 * head_dim + SPARE
    offsets = jnp.concatenate(
        [
            b_query_f.reshape(HEADS, head_dim),
            jnp.zeros((HEADS, head_dim), F32),
            b_value_f.reshape(HEADS, head_dim),
            jnp.zeros((HEADS, SPARE), F32),
        ],
        1,
    )
    row = jnp.arange(block)[None, :, None]
    qkv = dims(joined_t, h_one, 1, 1).reshape(HEADS, block, count) + offsets[:, :, None]
    qkv = jnp.where(row < 3 * head_dim, qkv, jnp.where(row == 3 * head_dim, 1.0, 0.0)).astype(BF16)
    o_t, lse = attention(qkv, mask)
    o_flat = o_t.reshape(width, count)
    x_one = x + dims(o_flat, out_t, 0, 1) + b_out_f
    xhat_two, factor_two = norm(x_one)
    h_two = (xhat_two * gain_two_f + bias_two_f).astype(BF16)
    upper = dims(h_two, hidden_t, 1, 1) + b_hidden_f
    act = jax.nn.gelu(upper, approximate=False).astype(BF16)
    mixed = (x_one + dims(act, proj_t, 1, 1) + b_proj_f).astype(BF16)

    d_y = cotangent.astype(F32) * live.astype(F32)[:, None]
    d_m = d_y.astype(BF16)
    grad_proj = dims(d_m, act, 0, 0).astype(BF16)
    d_upper = (dims(d_m, proj_t, 1, 0) * gelu_slope(upper)).astype(BF16)
    grad_hidden = dims(d_upper, h_two, 0, 0).astype(BF16)
    d_two, grad_gain_two, grad_bias_two = norm_back(
        dims(d_upper, hidden_t, 1, 0), xhat_two, factor_two, gain_two_f
    )
    d_x_one = d_y + d_two
    d_attn = d_x_one.astype(BF16)
    grad_out = dims(d_attn, o_flat, 0, 1).astype(BF16)
    d_o = dims(out_t, d_attn, 0, 1).astype(BF16).reshape(HEADS, head_dim, count)
    late = [
        g.reshape(chips, -1, g.shape[-1]) for g in (grad_out, grad_hidden, grad_proj)
    ]
    if own_copies:
        late = scatter(late, 2)
    d_qkv = attention_back(qkv, mask, o_t, d_o, lse)
    d_flat = d_qkv.reshape(HEADS * block, count)
    grad_qkv = dims(d_flat, h_one, 1, 0).reshape(HEADS, block, width)
    bias_sums = jnp.sum(d_qkv.astype(F32), -1)
    d_one, grad_gain_one, grad_bias_one = norm_back(
        dims(d_flat, joined_t, 0, 0), xhat_one, factor_one, gain_one_f
    )
    grad_tokens = d_x_one + d_one

    sums = (
        grad_gain_one,
        grad_bias_one,
        bias_sums[:, :head_dim].reshape(-1),
        bias_sums[:, 2 * head_dim : 3 * head_dim].reshape(-1),
        row_sums(d_attn),
        grad_gain_two,
        grad_bias_two,
        row_sums(d_upper),
        row_sums(d_m),
    )
    sums = jnp.stack(
        [jnp.pad(s.reshape(chips, -1), ((0, 0), (0, width - s.size // chips))) for s in sums], 1
    )
    sums = jnp.pad(sums, ((0, 0), (0, SPARE - sums.shape[1]), (0, 0)))
    part = width // chips
    if own_copies:
        early = jnp.concatenate([grad_qkv[:, : 3 * head_dim], sums], 1).astype(BF16)
        (early,) = scatter([early], 3)
        grads = [early[n * head_dim : (n + 1) * head_dim] for n in range(3)]
        vector_grads = early[3 * head_dim :]
    else:
        grads = [
            grad_qkv[:, n * head_dim : (n + 1) * head_dim].reshape(chips, part, width)
            for n in range(3)
        ]
        *grads, vector_grads = [
            lax.psum(
                lax.psum_scatter(g.astype(F32), "wide", scatter_dimension=0, tiled=False).astype(
                    BF16
                ),
                "narrow",
            ).astype(F32)
            for g in grads + [sums]
        ]
        late = [
            lax.psum(
                lax.psum_scatter(g.astype(F32), "wide", scatter_dimension=0, tiled=False).astype(
                    BF16
                ),
                "narrow",
            ).astype(F32)
            for g in late
        ]
    g_query, g_key, g_value = [g.T for g in grads]
    g_out, g_hidden, g_proj = [g.T for g in late]
    g_vec = [vector_grads[n, : v.shape[0]] for n, v in enumerate(vectors)]
    return (
        mixed, grad_tokens, g_vec[0], g_vec[1], g_query, g_vec[2], g_key, g_value, g_vec[3],
        g_out, g_vec[4], g_vec[5], g_vec[6], g_hidden, g_vec[7], g_proj, g_vec[8],
    )


def solution(mesh):
    both, wide = P(("wide", "narrow"), None), P("wide")
    weight = P(None, "wide")
    return jax.shard_map(
        functools.partial(shards, mesh.shape["wide"], mesh.shape["narrow"]),
        mesh=mesh,
        in_specs=(
            both, both, both, both, wide, wide, weight, wide, weight, weight, wide, weight, wide,
            wide, wide, weight, wide, weight, wide,
        ),
        out_specs=(
            both, both, wide, wide, weight, wide, weight, weight, wide, weight, wide, wide, wide,
            weight, wide, weight, wide,
        ),
        check_vma=False,
    )
```

time: 1370 us -> 582 us (0.42)
  waiting for transfers between devices: 763 us -> 0 us
  Pallas kernels: 0 us -> 385 us
  matrix products: 294 us -> 109 us
  blocking collectives: 130 us -> 0 us
  other arithmetic: 121 us -> 33.1 us
  between operations: 17.3 us -> 1.34 us
    reduce_scatter x6 -> x0, waiting for transfers between devices: 561 us -> none  [the longest x1 175 us: shards(): lax.psum_scatter(grad_w_hidden, 'wide', scatter_dimension=1, tiled=True)]
    pallas_call x0 -> x6, Pallas kernels: none -> 385 us  [the longest x2 146 us: gather(): pl.pallas_call(functools.partial(gather_kernel, chips, len(arrays)), out_...]
    dot_general x24 -> x12, matrix products: 294 us -> 109 us  [dims(): lax.dot_general(left, right, (((a,), (b,)), ((), ())), preferred_element_...]
    all_gather x6 -> x0, waiting for transfers between devices: 184 us -> none  [the longest x1 77 us: shards(): lax.all_gather(w_hidden, 'wide', axis=1, tiled=True)]
    unnamed x2 -> x0, blocking collectives: 114 us -> none
    convert_element_type x32 -> x5, other arithmetic: 82.6 us -> 5.33 us  [the longest x1 2.56 us: shards(): mask = jnp.where(allowed, 0.0, MASKED).astype(BF16)]
    psum x1 -> x0, blocking collectives: 16.6 us -> none  [shards(): lax.psum(shares[0].astype(jnp.bfloat16), 'narrow').astype(jnp.float32)]
    reduce_sum x5, other arithmetic: 25.2 us -> 9.96 us  [the longest x1 5.46 us: row_sums(): return jnp.sum(values.astype(F32), 0)]
  transfers between devices with their start and end apart: 13 -> 0, of which waited for: 10 -> 0; matrix products, arithmetic and copies ran while one was open for 29% -> 0% of each run, Pallas kernels for 0% -> 0%
where the time goes in v1:
time: 582 us; the launch traced here: 571 us
  Pallas kernels  385 us (66%)
  matrix products  109 us (19%)
  local copies, waits for them, and re-layouts  42.7 us (7%)
  other arithmetic  33.1 us (6%)
    pallas_call x2, Pallas kernels, gather(): pl.pallas_call(functools.partial(gather_kernel, chips, len(arrays)), out_...  146 us
    pallas_call x2, Pallas kernels, scatter(): pl.pallas_call(functools.partial(scatter_kernel, arrays[0].shape[0], len(...  139 us
    dot_general x12, matrix products, dims(): lax.dot_general(left, right, (((a,), (b,)), ((), ())), preferred_element_...  109 us
    pallas_call x1, Pallas kernels, attention_back(): pl.pallas_call(body, grid=(HEADS,), out_shape=jax.ShapeDtypeStruct((HEADS...  51 us
    pallas_call x1, Pallas kernels, attention(): pl.pallas_call(body, grid=(HEADS,), out_shape=[jax.ShapeDtypeStruct((HEAD...  48 us
    unnamed x61, local copies, waits for them, and re-layouts  13.8 us

profile of v1, /device:TPU:9, one launch (start us, length us, event | category | flops | bytes accessed | tf_op | source)
XLA Modules:
  0.0 570.8 jit_solution(6850276366891714760)
XLA Ops:
  0.8 0.7 compare_reduce_fusion
  7.6 0.7 convert_element_type.204
  8.3 1.7 fusion.44.refs_0_
  10.0 1.7 copy.69
  12.5 1.7 copy.73
  14.2 2.6 select_convert_fusion.1.mask_ref
  16.8 48.1 %shard_map.314 = bf16[16,160,768]{2,1,0:T(8,128)(2,1)} custom-call(bf16[160,768]{1,0:T(8,128)(2,1)} %fusion.44.refs_0_), custom_call_target="tpu_custom_call" | custom-call | tf_op jit(solution)/shard_map/pallas_call | solution.py:192
  64.8 0.9 convert_reduce_fusion.1
  65.8 0.9 fusion.49
  66.8 1.2 convert_reduce_fusion.2
  68.4 8.9 %select_convert_fusion.qkv_ref = bf16[16,160,1024]{2,1,0:T(8,128)(2,1)} fusion(bf16[160]{0:T(256)(128)(2,1)S(1)} %compare_select_fusion, f32[16,160]{1,0:T(8,128)S(1)} %maximum_maximum_fusion, pred[160]{0:T(512)(128)(4,1)S(1)} %iota_compare_fusion.3, bf16[16,160,768]{2,1,0:T(8,128)(2,1)} %shard_map.314, bf16[1024,768]{0,1:T(8,128)(2,1)S(1)} %copy.69, ...), kind=kOutput, calls=%fused_computation.26 | convolution fusion | flops 4036493312 | bytes 10772960 | tf_op jit(solution)/shard_map/dot_general | solution.py:22
  77.3 48.0 %shard_map.315 = (bf16[16,48,1024]{2,1,0:T(8,128)(2,1)}, f32[16,1,1024]{2,1,0:T(1,128)}) custom-call(bf16[16,160,1024]{2,1,0:T(8,128)(2,1)} %select_convert_fusion.qkv_ref, bf16[1024,1024]{1,0:T(8,128)(2,1)} %select_convert_fusion.1.mask_ref), custom_call_target="tpu_custom_call" | custom-call | tf_op jit(solution)/shard_map/pallas_call | solution.py:423
  125.3 98.2 %shard_map.316 = (bf16[16,48,768]{2,1,0:T(8,128)(2,1)}, bf16[16,192,768]{2,1,0:T(8,128)(2,1)}, bf16[16,48,3072]{2,1,0:T(8,128)(2,1)}) custom-call(bf16[48,768]{1,0:T(8,128)(2,1)} %bitcast.103, bf16[192,768]{1,0:T(8,128)(2,1)} %bitcast.97, bf16[48,3072]{1,0:T(8,128)(2,1)} %bitcast.98), custom_call_target="tpu_custom_call" | custom-call | tf_op jit(solution)/shard_map/pallas_call | solution.py:192
  223.5 3.3 fusion.51
  227.3 34.8 %fusion.2 = (bf16[1024,3072]{1,0:T(8,128)(2,1)S(1)}, f32[1024,3072]{1,0:T(8,128)}) fusion(f32[3072]{0:T(1024)S(1)} %reshape.242, bf16[3072,768]{1,0:T(8,128)(2,1)S(1)} %bitcast.112, f32[1024,768]{0,1:T(8,128)S(1)} %get-tuple-element.115, f32[768]{0:T(1024)S(1)} %reshape.241, f32[768]{0:T(1024)S(1)} %reshape.240, f32[1024]{0:T(1024)S(1)} %add_rsqrt_fusion, ...), kind=kOutput, calls=%fused_computation.4 | convolution fusion | flops 5043388416 | bytes 26765312 | tf_op jit(solution)/shard_map/dot_general | solution.py:22
  262.1 12.3 %fusion.54 = (bf16[3072]{0:T(1024)(128)(2,1)S(1)}, bf16[1024,3072]{1,0:T(8,128)(2,1)S(1)}) fusion(f32[1024,3072]{1,0:T(8,128)} %get-tuple-element.117, f32[3072]{0:T(1024)S(1)} %reshape.242, bf16[768,3072]{1,0:T(8,128)(2,1)S(1)} %bitcast.116, bf16[1024,768]{0,1:T(8,128)(2,1)S(1)} %copy.73, f32[1024]{0:T(1024)S(1)} %bitcast.106), kind=kOutput, calls=%fused_computation.126 | convolution fusion | flops 4871943168 | bytes 25188352 | tf_op jit(solution)/shard_map/dot_general | solution.py:22
  274.5 5.1 add_convert_fusion
  279.6 6.8 %convolution_convert_fusion = bf16[768,3072]{1,0:T(8,128)(2,1)} fusion(bf16[1024,3072]{1,0:T(8,128)(2,1)S(1)} %get-tuple-element.116, bf16[1024,768]{0,1:T(8,128)(2,1)S(1)} %copy.73, f32[1024]{0:T(1024)S(1)} %bitcast.107), kind=kOutput, calls=%fused_computation.30 | convolution fusion | flops 4836556800 | bytes 12587008 | tf_op jit(solution)/shard_map/dot_general | solution.py:22
  286.3 6.7 %fusion.53 = (bf16[768]{0:T(1024)(128)(2,1)S(1)}, f32[1024,768]{1,0:T(8,128)}) fusion(bf16[1024,3072]{1,0:T(8,128)(2,1)S(1)} %get-tuple-element.123, bf16[3072,768]{1,0:T(8,128)(2,1)S(1)} %bitcast.113), kind=kOutput, calls=%fused_computation.125 | convolution fusion | flops 4832623616 | bytes 14157312 | tf_op jit(solution)/shard_map/dot_general | solution.py:22
  293.1 1.6 copy.88
  296.1 3.9 copy.74
  300.0 3.0 multiply_reduce_fusion
  303.0 0.7 copy-done.22
  303.7 7.4 %convolution_convert_fusion.1 = bf16[3072,768]{1,0:T(8,128)(2,1)} fusion(bf16[1024,3072]{1,0:T(8,128)(2,1)S(1)} %copy-done.22, f32[1024,768]{0,1:T(8,128)S(1)} %copy-done.3, f32[768]{0:T(1024)S(1)} %reshape.241, f32[768]{0:T(1024)S(1)} %reshape.240, f32[1024]{0:T(1024)S(1)} %add_rsqrt_fusion, f32[1024]{0:T(1024)S(1)} %broadcast_multiply_fusion.4), kind=kOutput, calls=%fused_computation.31 | convolution fusion | flops 4838129664 | bytes 14170112 | tf_op jit(solution)/shard_map/dot_general | solution.py:22
  311.2 5.5 convert_reduce_fusion.8
  318.9 4.9 convolution_convert_fusion.2
  323.8 51.0 %shard_map.317 = bf16[16,160,1024]{2,1,0:T(8,128)(2,1)} custom-call(bf16[16,160,1024]{2,1,0:T(8,128)(2,1)} %select_convert_fusion.qkv_ref, bf16[1024,1024]{1,0:T(8,128)(2,1)} %select_convert_fusion.1.mask_ref, bf16[16,48,1024]{2,1,0:T(8,128)(2,1)} %get-tuple-element.25.out_ref, bf16[16,48,1024]{2,1,0:T(8,128)(2,1)} %bitcast.93, ...), custom_call_target="tpu_custom_call" | custom-call | tf_op jit(solution)/shard_map/pallas_call | solution.py:445
  374.8 8.6 %fusion.52 = (bf16[768]{0:T(1024)(128)(2,1)S(1)}, f32[1024,768]{1,0:T(8,128)}) fusion(bf16[16,160,1024]{2,1,0:T(8,128)(2,1)} %shard_map.317, bf16[16,160,768]{2,1,0:T(8,128)(2,1)S(1)} %copy-done.7), kind=kOutput, calls=%fused_computation.124 | convolution fusion | flops 4027317504 | bytes 12322304 | tf_op jit(solution)/shard_map/dot_general | solution.py:22
  383.5 3.4 reduce
  386.9 7.8 %fusion.41 = bf16[16,160,768]{2,1,0:T(8,128)(2,1)S(1)} fusion(bf16[16,160,1024]{2,1,0:T(8,128)(2,1)} %shard_map.317, bf16[1024,768]{0,1:T(8,128)(2,1)S(1)} %copy-done.1, f32[768]{0:T(1024)S(1)} %copy-done.20, f32[768]{0:T(1024)S(1)} %copy-done.15, f32[1024]{0:T(1024)S(1)} %copy-done.17, f32[1024]{0:T(1024)S(1)} %copy-done.13), kind=kOutput, calls=%fused_computation.73 | convolution fusion | flops 4031250432 | bytes 10762240 | tf_op jit(solution)/shard_map/dot_general | solution.py:22
  394.8 2.0 copy-done.4
  396.8 0.7 copy.80
  398.1 0.7 copy.81
  398.8 2.5 convolution_convert_fusion.3
  401.3 98.8 %shard_map.319 = (f32[48,768]{1,0:T(8,128)}, f32[192,768]{1,0:T(8,128)}, f32[48,3072]{1,0:T(8,128)}) custom-call(bf16[16,48,768]{2,1,0:T(8,128)(2,1)} %bitcast.94, bf16[16,192,768]{2,1,0:T(8,128)(2,1)} %bitcast.90, bf16[16,48,3072]{2,1,0:T(8,128)(2,1)} %bitcast.89), custom_call_target="tpu_custom_call" | custom-call | tf_op jit(solution)/shard_map/pallas_call | solution.py:351
  500.1 3.6 copy.75
  503.7 2.9 fusion.32
  506.7 5.5 fusion.31
  512.2 3.7 copy.89
  516.6 3.5 stack.89
  520.1 3.0 fusion.19.refs_0_
  523.1 40.6 %shard_map.318 = f32[160,768]{1,0:T(8,128)} custom-call(bf16[16,160,768]{2,1,0:T(8,128)(2,1)} %fusion.19.refs_0_), custom_call_target="tpu_custom_call" | custom-call | tf_op jit(solution)/shard_map/pallas_call | solution.py:351
  563.7 1.3 slice.117
  565.0 1.5 slice_bitcast_fusion.3
  566.5 1.8 slice_bitcast_fusion
  568.3 0.7 copy.102
  569.0 0.8 copy.103
  569.8 0.8 copy.104
  (124 shorter events, 13.4 us)
Async XLA Ops:
  11.7 211.8 %copy-start = (bf16[1024,768]{0,1:T(8,128)(2,1)}, bf16[1024,768]{0,1:T(8,128)(2,1)S(1)}, u32[]{:S(2)}) copy-start(bf16[1024,768]{0,1:T(8,128)(2,1)S(1)} %copy.69) | copy-start | bytes 4718596
  11.7 2.5 copy-start.18
  12.0 56.4 %copy-start.12 = (f32[1024]{0:T(1024)}, f32[1024]{0:T(1024)S(1)}, u32[]{:S(2)}) copy-start(f32[1024]{0:T(1024)S(1)} %broadcast_multiply_fusion.5) | copy-start | bytes 12292
  12.5 55.9 %copy-start.16 = (f32[1024]{0:T(1024)}, f32[1024]{0:T(1024)S(1)}, u32[]{:S(2)}) copy-start(f32[1024]{0:T(1024)S(1)} %add_rsqrt_fusion.1) | copy-start | bytes 12292
  14.2 265.3 %copy-start.6 = (bf16[1024,768]{0,1:T(8,128)(2,1)}, bf16[1024,768]{0,1:T(8,128)(2,1)S(1)}, u32[]{:S(2)}) copy-start(bf16[1024,768]{0,1:T(8,128)(2,1)S(1)} %copy.73) | copy-start | bytes 4718596
  68.2 9.1 %copy-start.14 = (f32[768]{0:T(1024)}, f32[768]{0:T(1024)S(1)}, u32[]{:S(2)}) copy-start(f32[768]{0:T(1024)S(1)} %reshape.235) | copy-start | bytes 9220
  68.3 9.0 %copy-start.19 = (f32[768]{0:T(1024)}, f32[768]{0:T(1024)S(1)}, u32[]{:S(2)}) copy-start(f32[768]{0:T(1024)S(1)} %reshape.236) | copy-start | bytes 9220
  223.5 3.8 slice-start.1
  223.5 3.8 slice-start.2
  223.5 38.6 %slice-start.3 = ((s8[4718592]{0:T(1024)(128)(4,1)}), s8[4194304]{0:T(1024)(128)(4,1)S(1)}, s32[]{:S(2)}) async-start(s8[4718592]{0:T(1024)(128)(4,1)} %bitcast.114), calls=%async_computation.3 | async-start | bytes 8388608
  226.9 47.6 %copy-start.2 = (f32[1024,768]{0,1:T(8,128)}, f32[1024,768]{0,1:T(8,128)S(1)}, u32[]{:S(2)}) copy-start(f32[1024,768]{0,1:T(8,128)S(1)} %get-tuple-element.115) | copy-start | bytes 9437188
  227.3 34.8 %slice-start.4 = ((s8[4718592]{0:T(1024)(128)(4,1)}), s8[524288]{0:T(1024)(128)(4,1)S(1)}, s32[]{:S(2)}) async-start(s8[4718592]{0:T(1024)(128)(4,1)} %bitcast.114), calls=%async_computation.4 | async-start | bytes 1048576
  274.5 11.9 %copy-start.21 = (bf16[1024,3072]{1,0:T(8,128)(2,1)}, bf16[1024,3072]{1,0:T(8,128)(2,1)S(1)}, u32[]{:S(2)}) copy-start(bf16[1024,3072]{1,0:T(8,128)(2,1)S(1)} %get-tuple-element.123) | copy-start | bytes 18874372
  296.1 3.9 copy-start.3
  300.0 3.7 copy-start.22
  323.8 51.0 %copy-start.7 = (bf16[16,160,768]{2,1,0:T(8,128)(2,1)S(1)}, bf16[16,160,768]{2,1,0:T(8,128)(2,1)}, u32[]{:S(2)}) copy-start(bf16[16,160,768]{2,1,0:T(8,128)(2,1)} %shard_map.314) | copy-start | bytes 11796484
  383.4 3.5 copy-start.1
  383.4 3.5 copy-start.13
  383.4 3.5 copy-start.15
  383.4 3.5 copy-start.17
  383.4 3.5 copy-start.20
  394.7 2.0 copy-start.4
  394.7 4.1 copy-start.5
  394.7 4.1 copy-start.8
  512.2 7.9 %slice-start = ((bf16[16,160,768]{2,1,0:T(8,128)(2,1)}), bf16[16,144,768]{2,1,0:T(8,128)(2,1)S(1)}, s32[]{:S(2)}) async-start(bf16[16,160,768]{2,1,0:T(8,128)(2,1)} %copy-done.4), calls=%async_computation | async-start | bytes 7077888 | tf_op jit(solution)/shard_map/slice | solution.py:624
  523.1 45.2 %copy-start.11 = (f32[48,768]{1,0:T(8,128)S(1)}, f32[48,768]{1,0:T(8,128)}, u32[]{:S(2)}) copy-start(f32[48,768]{1,0:T(8,128)} %get-tuple-element.30) | copy-start | bytes 442372
  523.1 45.9 %copy-start.10 = (f32[192,768]{1,0:T(8,128)S(1)}, f32[192,768]{1,0:T(8,128)}, u32[]{:S(2)}) copy-start(f32[192,768]{1,0:T(8,128)} %get-tuple-element.31) | copy-start | bytes 1769476
  523.1 46.7 %copy-start.9 = (f32[48,3072]{1,0:T(8,128)S(1)}, f32[48,3072]{1,0:T(8,128)}, u32[]{:S(2)}) copy-start(f32[48,3072]{1,0:T(8,128)} %get-tuple-element.32) | copy-start | bytes 1769476

commit v2 on v1

--- a/solution.py
+++ b/solution.py
@@ -15,7 +15,10 @@
 LOG2E = math.log2(math.e)
 MASKED = -1e30
 SPARE = 16
-CHUNK = 256
+SEGS = 4
+GATHER_STEPS = (0, 3, 6, 10, 14)
+SCATTER_STEPS = (0, 2, 6, 9, 12, 15)
+CHUNK = 512
 
 
 def dims(left, right, a, b):
@@ -360,42 +363,76 @@
     )(*arrays)
 
 
-def forward_head(qkv, mask, out, lse, head_dim):
+def forward_head(qkv, extra, pad, out, lse, head_dim):
     count = qkv.shape[-1]
     factor = head_dim**-0.5 * LOG2E
-    keys = qkv[0, head_dim : 2 * head_dim, :]
+    keys = jnp.concatenate([qkv[0, head_dim : 2 * head_dim, :], extra[1]], 0).T
     value = qkv[0, 2 * head_dim : 3 * head_dim + SPARE, :]
 
     for start in range(0, count, CHUNK):
         part = pl.ds(start, CHUNK)
-        raw = dims(keys, qkv[0, :head_dim, part], 0, 0) * factor + mask[:, part].astype(F32)
-        top = jnp.max(raw, 0, keepdims=True)
-        probs = jnp.exp2(raw - top).astype(BF16)
+        query = qkv[0, :head_dim, part]
+        own_key = qkv[0, head_dim : 2 * head_dim, part]
+        own = jnp.sum(query.astype(F32) * own_key.astype(F32), 0, keepdims=True) + pad[:, part]
+        raw = dims(keys, jnp.concatenate([query, extra[0, :, part]], 0), 1, 0)
+        top = jnp.maximum(jnp.max(raw, 0, keepdims=True), own)
+        probs = jnp.exp2((raw - top) * factor).astype(BF16)
+        own = jnp.exp2((own - top) * factor)
         both = dims(value, probs, 1, 0)
-        total = both[head_dim : head_dim + 1]
-        out[0, :, part] = (both[:head_dim] / total).astype(BF16)
-        lse[0, :, part] = top + jnp.log2(total)
-
-
-def backward_head(qkv, mask, out, d_out, lse, grad, d_key, d_value, head_dim):
+        total = both[head_dim : head_dim + 1] + own
+        own_value = qkv[0, 2 * head_dim : 3 * head_dim, part].astype(F32)
+        out[0, :, part] = ((both[:head_dim] + own * own_value) / total).astype(BF16)
+        lse[0, :, part] = top + jnp.log2(total) * (1.0 / factor)
+
+
+def split_rows(row):
+    high = row.astype(BF16)
+    rest = row - high.astype(F32)
+    middle = rest.astype(BF16)
+    low = (rest - middle.astype(F32)).astype(BF16)
+    return [high, middle, low]
+
+
+def backward_head(qkv, extra, pad, out, d_out, lse, grad, d_key, d_value, head_dim):
     count = qkv.shape[-1]
     scale = head_dim**-0.5
     factor = scale * LOG2E
     keys = qkv[0, head_dim : 2 * head_dim, :]
-    value = qkv[0, 2 * head_dim : 3 * head_dim, :]
+    keys_t = jnp.concatenate([keys, extra[1]], 0).T
+    row = lax.broadcasted_iota(jnp.int32, (SPARE, count), 0)
+    ones = jnp.where(row < 3, 1.0, 0.0).astype(BF16)
+    value_t = jnp.concatenate([qkv[0, 2 * head_dim : 3 * head_dim, :], ones], 0).T
 
     for start in range(0, count, CHUNK):
         part = pl.ds(start, CHUNK)
         query = qkv[0, :head_dim, part]
         d_part = d_out[0, :, part]
-        probs = jnp.exp2(
-            dims(keys, query, 0, 0) * factor + (mask[:, part].astype(F32) - lse[0, :, part])
-        )
-        share = jnp.sum(d_part.astype(F32) * out[0, :, part].astype(F32), 0, keepdims=True)
-        d_probs = dims(value, d_part, 0, 0)
-        d_scores = (probs * (d_probs - share)).astype(BF16)
+        d_full = d_part.astype(F32)
+        share = jnp.sum(d_full * out[0, :, part].astype(F32), 0, keepdims=True)
+        row = lax.broadcasted_iota(jnp.int32, (SPARE, CHUNK), 0)
+
+        def spread(values, at, base):
+            for n, piece in enumerate(split_rows(values)):
+                base = jnp.where(row == at + n, -piece.astype(F32), base)
+            return base.astype(BF16)
+
+        base = extra[0, :, part].astype(F32)
+        query_x = jnp.concatenate([query, spread(lse[0, :, part], 5, base)], 0)
+        d_part_x = jnp.concatenate([d_part, spread(share, 0, jnp.zeros_like(base))], 0)
+        probs = jnp.exp2(dims(keys_t, query_x, 1, 0) * factor)
+        d_scores = (probs * dims(value_t, d_part_x, 1, 0)).astype(BF16)
         probs_low = probs.astype(BF16)
-        grad[0, :head_dim, part] = (dims(keys, d_scores, 1, 0) * scale).astype(BF16)
+
+        own_key = qkv[0, head_dim : 2 * head_dim, part].astype(F32)
+        own_value = qkv[0, 2 * head_dim : 3 * head_dim, part].astype(F32)
+        query_f = query.astype(F32)
+        own = jnp.sum(query_f * own_key, 0, keepdims=True) + pad[:, part]
+        own = jnp.exp2((own - lse[0, :, part]) * factor)
+        own_ds = own * (jnp.sum(d_full * own_value, 0, keepdims=True) - share)
+
+        grad[0, :head_dim, part] = (
+            (dims(keys, d_scores, 1, 0) + own_ds * own_key) * scale
+        ).astype(BF16)
         more_value = dims(d_part, probs_low, 1, 1)
         more_key = dims(query, d_scores, 1, 1)
         if start == 0:
@@ -404,8 +441,12 @@
         else:
             d_value[...] += more_value
             d_key[...] += more_key
-    grad[0, head_dim : 2 * head_dim, :] = (d_key[...] * scale).astype(BF16)
-    grad[0, 2 * head_dim : 3 * head_dim, :] = d_value[...].astype(BF16)
+        grad[0, head_dim : 2 * head_dim, part] = (own_ds * query_f).astype(BF16)
+        grad[0, 2 * head_dim : 3 * head_dim, part] = (own * d_full).astype(BF16)
+    for slot, total, factor_out in ((1, d_key, scale), (2, d_value, 1.0)):
+        rows = pl.ds(slot * head_dim, head_dim)
+        whole = total[...]
+        grad[0, rows, :] = ((whole + grad[0, rows, :].astype(F32)) * factor_out).astype(BF16)
     grad[0, 3 * head_dim :, :] = jnp.zeros((SPARE, count), BF16)
 
 
@@ -413,12 +454,40 @@
     return pl.BlockSpec((1, rows, count), lambda h: (h, 0, 0))
 
 
-def attention(qkv, mask):
+def same(*shape):
+    return pl.BlockSpec(shape, lambda h: (0,) * len(shape))
+
+
+def run_stages(plan, when, chips):
+    me, core = lax.axis_index("wide"), lax.axis_index("narrow")
+    axes = chip_axes(chips)
+    h = pl.program_id(0)
+
+    @pl.when(h == 0)
+    def _():
+        greet(me, core, axes)
+
+    for c in range(2):
+        for stage, step in zip(plan(me, c, axes), when):
+            @pl.when((core == c) & (h == step))
+            def _(stage=stage):
+                stage()
+
+
+def attention(qkv, extra, pad, weights=(), chips=0, ident=None):
     rows, count = qkv.shape[1:]
     head_dim = (rows - SPARE) // 3
-
-    def body(qkv_ref, mask_ref, out, lse):
-        forward_head(qkv_ref, mask_ref, out, lse, head_dim)
+    n = len(weights)
+
+    def body(*refs):
+        (qkv_ref, extra_ref, pad_ref), ins = refs[:3], refs[3 : 3 + n]
+        (out, lse), outs, sems = refs[3 + n : 5 + n], refs[5 + n : 5 + 2 * n], refs[5 + 2 * n :]
+        if n:
+            run_stages(
+                lambda me, c, axes: gather_plan(ins, outs, sems, me, c, axes),
+                GATHER_STEPS, chips,
+            )
+        forward_head(qkv_ref, extra_ref, pad_ref, out, lse, head_dim)
 
     return pl.pallas_call(
         body,
@@ -426,37 +495,75 @@
         out_shape=[
             jax.ShapeDtypeStruct((HEADS, head_dim, count), BF16),
             jax.ShapeDtypeStruct((HEADS, 1, count), F32),
-        ],
-        in_specs=[head_spec(rows, count), pl.BlockSpec((count, count), lambda h: (0, 0))],
-        out_specs=[head_spec(head_dim, count), head_spec(1, count)],
-        compiler_params=pltpu.CompilerParams(vmem_limit_bytes=60 * 2**20),
-    )(qkv, mask)
-
-
-def attention_back(qkv, mask, out, d_out, lse):
+        ]
+        + [jax.ShapeDtypeStruct((chips,) + a.shape, a.dtype) for a in weights],
+        in_specs=[head_spec(rows, count), same(2, SPARE, count), same(1, count)]
+        + [same(*a.shape) for a in weights],
+        out_specs=[head_spec(head_dim, count), head_spec(1, count)]
+        + [pl.BlockSpec(memory_space=pl.ANY)] * n,
+        scratch_shapes=gather_sems(chips, n) if n else [],
+        compiler_params=pltpu.CompilerParams(
+            vmem_limit_bytes=60 * 2**20, collective_id=ident, has_side_effects=n > 0
+        ),
+    )(qkv, extra, pad, *weights)
+
+
+def attention_back(qkv, extra, pad, out, d_out, lse, grads=(), chips=0, ident=None):
     rows, count = qkv.shape[1:]
     head_dim = (rows - SPARE) // 3
-
-    def body(qkv_ref, mask_ref, out_ref, d_out_ref, lse_ref, grad, d_key, d_value):
-        backward_head(
-            qkv_ref, mask_ref, out_ref, d_out_ref, lse_ref, grad, d_key, d_value, head_dim
-        )
-
+    n = len(grads)
+
+    def body(*refs):
+        ins, refs = refs[:6], refs[6:]
+        g_ins, grad, g_outs, rest = refs[:n], refs[n], refs[n + 1 : 2 * n + 1], refs[2 * n + 1 :]
+        d_key, d_value = rest[:2]
+        if n:
+            parts, sems = scatter_parts(n, rest[2:])
+            run_stages(
+                lambda me, c, axes: scatter_plan(g_ins, g_outs, *parts, sems, me, c, axes),
+                SCATTER_STEPS, chips,
+            )
+        backward_head(*ins, grad, d_key, d_value, head_dim)
+
+    any_space = pl.BlockSpec(memory_space=pl.ANY)
     return pl.pallas_call(
         body,
         grid=(HEADS,),
-        out_shape=jax.ShapeDtypeStruct((HEADS, rows, count), BF16),
+        out_shape=[jax.ShapeDtypeStruct((HEADS, rows, count), BF16)]
+        + [jax.ShapeDtypeStruct(a.shape[1:], F32) for a in grads],
         in_specs=[
             head_spec(rows, count),
-            pl.BlockSpec((count, count), lambda h: (0, 0)),
+            same(2, SPARE, count),
+            same(1, count),
             head_spec(head_dim, count),
             head_spec(head_dim, count),
             head_spec(1, count),
-        ],
-        out_specs=head_spec(rows, count),
-        scratch_shapes=[pltpu.VMEM((head_dim, count), F32)] * 2,
-        compiler_params=pltpu.CompilerParams(vmem_limit_bytes=60 * 2**20),
-    )(qkv, mask, out, d_out, lse)
+        ]
+        + [any_space] * n,
+        out_specs=[head_spec(rows, count)] + [any_space] * n,
+        scratch_shapes=[pltpu.VMEM((head_dim, count), F32)] * 2
+        + (scatter_scratch(grads) if n else []),
+        compiler_params=pltpu.CompilerParams(
+            vmem_limit_bytes=60 * 2**20, collective_id=ident, has_side_effects=n > 0
+        ),
+    )(qkv, extra, pad, out, d_out, lse, *grads)
+
+
+def masking_rows(seg, live):
+    n = jnp.arange(SPARE)[:, None]
+    seg, live = seg[None], live[None]
+    group = n < SEGS
+    query = jnp.where(group, seg == n, n == SEGS).astype(F32)
+    keys = jnp.where(
+        group,
+        jnp.where(seg == n, 0.0, MASKED),
+        jnp.where(
+            n == SEGS,
+            jnp.where(live > 0, 0.0, MASKED),
+            jnp.where((n > SEGS) & (n < SEGS + 4), 1.0, 0.0),
+        ),
+    )
+    return jnp.stack([query, keys]).astype(BF16), jnp.where(live > 0, MASKED, 0.0).astype(F32)
 
 
 def norm(values):
@@ -475,10 +582,10 @@
     return factor * inner, jnp.sum(grad * normed, 0), jnp.sum(grad, 0)
 
 
-def gelu_slope(values):
+def gelu_pair(values):
     cdf = 0.5 * (1.0 + lax.erf(values * (1.0 / math.sqrt(2.0))))
     pdf = jnp.exp(-0.5 * values * values) * (1.0 / math.sqrt(2.0 * math.pi))
-    return cdf + values * pdf
+    return values * cdf, cdf + values * pdf
 
 
 def row_sums(values):
@@ -523,7 +630,6 @@
     if own_copies:
         first = jnp.concatenate([w_query.T, w_key.T, w_value.T, packed], 0)
         (first,) = gather([first], chips, 0)
-        out_t, hidden_t, proj_t = gather([w_out.T, w_hidden.T, w_proj.T], chips, 1)
         joined_t = first
         vector_rows = first[:, 3 * head_dim :, :]
     else:
@@ -537,9 +643,6 @@
         out_t, hidden_t, proj_t = [
             lax.all_gather(w.T, "wide", axis=0, tiled=False) for w in (w_out, w_hidden, w_proj)
         ]
-    out_t = out_t.reshape(width, width)
-    hidden_t = hidden_t.reshape(hidden, width)
-    proj_t = proj_t.reshape(width, hidden)
     joined_t = joined_t.reshape(HEADS * (3 * head_dim + SPARE), width)
     gain_one_f, bias_one_f, b_query_f, b_value_f, b_out_f, gain_two_f, bias_two_f, b_hidden_f, b_proj_f = [
         vector_rows[:, n, : v.shape[0]].reshape(-1).astype(F32) for n, v in enumerate(vectors)
@@ -547,11 +650,7 @@
 
     live = keep[0]
     seg = segment[0]
-    index = jnp.arange(count)
-    allowed = (seg[:, None] == seg[None, :]) & (
-        (live[:, None] > 0) | (index[:, None] == index[None, :])
-    )
-    mask = jnp.where(allowed, 0.0, MASKED).astype(BF16)
+    extra, pad = masking_rows(seg, live)
 
     x = tokens.astype(F32)
     xhat_one, factor_one = norm(x)
@@ -569,19 +668,27 @@
     row = jnp.arange(block)[None, :, None]
     qkv = dims(joined_t, h_one, 1, 1).reshape(HEADS, block, count) + offsets[:, :, None]
     qkv = jnp.where(row < 3 * head_dim, qkv, jnp.where(row == 3 * head_dim, 1.0, 0.0)).astype(BF16)
-    o_t, lse = attention(qkv, mask)
+    if own_copies:
+        o_t, lse, out_t, hidden_t, proj_t = attention(
+            qkv, extra, pad, (w_out.T, w_hidden.T, w_proj.T), chips, 1
+        )
+    else:
+        o_t, lse = attention(qkv, extra, pad)
+    out_t = out_t.reshape(width, width)
+    hidden_t = hidden_t.reshape(hidden, width)
+    proj_t = proj_t.reshape(width, hidden)
     o_flat = o_t.reshape(width, count)
     x_one = x + dims(o_flat, out_t, 0, 1) + b_out_f
     xhat_two, factor_two = norm(x_one)
     h_two = (xhat_two * gain_two_f + bias_two_f).astype(BF16)
     upper = dims(h_two, hidden_t, 1, 1) + b_hidden_f
-    act = jax.nn.gelu(upper, approximate=False).astype(BF16)
+    act, slope = [v.astype(BF16) for v in gelu_pair(upper)]
     mixed = (x_one + dims(act, proj_t, 1, 1) + b_proj_f).astype(BF16)
 
     d_y = cotangent.astype(F32) * live.astype(F32)[:, None]
     d_m = d_y.astype(BF16)
     grad_proj = dims(d_m, act, 0, 0).astype(BF16)
-    d_upper = (dims(d_m, proj_t, 1, 0) * gelu_slope(upper)).astype(BF16)
+    d_upper = (dims(d_m, proj_t, 1, 0) * slope.astype(F32)).astype(BF16)
     grad_hidden = dims(d_upper, h_two, 0, 0).astype(BF16)
     d_two, grad_gain_two, grad_bias_two = norm_back(
         dims(d_upper, hidden_t, 1, 0), xhat_two, factor_two, gain_two_f
@@ -594,8 +701,9 @@
         g.reshape(chips, -1, g.shape[-1]) for g in (grad_out, grad_hidden, grad_proj)
     ]
     if own_copies:
-        late = scatter(late, 2)
-    d_qkv = attention_back(qkv, mask, o_t, d_o, lse)
+        d_qkv, *late = attention_back(qkv, extra, pad, o_t, d_o, lse, late, chips, 2)
+    else:
+        (d_qkv,) = attention_back(qkv, extra, pad, o_t, d_o, lse)
     d_flat = d_qkv.reshape(HEADS * block, count)
     grad_qkv = dims(d_flat, h_one, 1, 0).reshape(HEADS, block, width)
     bias_sums = jnp.sum(d_qkv.astype(F32), -1)

time: 582 us -> 487 us (0.84)
  Pallas kernels: 385 us -> 312 us
  matrix products: 109 us -> 89.2 us
    pallas_call x2 -> x1, Pallas kernels: 146 us -> 48.1 us  [gather(): pl.pallas_call(functools.partial(gather_kernel, chips, len(arrays)), out_...]
    pallas_call x2 -> x1, Pallas kernels: 139 us -> 42.7 us  [scatter(): pl.pallas_call(functools.partial(scatter_kernel, arrays[0].shape[0], len(...]
    pallas_call x1, Pallas kernels: 51 us -> 118 us  [attention_back(): pl.pallas_call(body, grid=(HEADS,), out_shape=[jax.ShapeDtypeStruct((HEAD...]
    pallas_call x1, Pallas kernels: 48 us -> 104 us  [attention(): pl.pallas_call(body, grid=(HEADS,), out_shape=[jax.ShapeDtypeStruct((HEAD...]
    dot_general x12, matrix products: 109 us -> 89.2 us  [dims(): lax.dot_general(left, right, (((a,), (b,)), ((), ())), preferred_element_...]
    unnamed x61 -> x33, local copies, waits for them, and re-layouts: 13.8 us -> 13.9 us
where the time goes in v2:
time: 487 us; the launch traced here: 480 us
  Pallas kernels  312 us (64%)
  matrix products  89.2 us (18%)
  local copies, waits for them, and re-layouts  42.5 us (9%)
  other arithmetic  34.8 us (7%)
    pallas_call x1, Pallas kernels, attention_back(): pl.pallas_call(body, grid=(HEADS,), out_shape=[jax.ShapeDtypeStruct((HEAD...  118 us
    pallas_call x1, Pallas kernels, attention(): pl.pallas_call(body, grid=(HEADS,), out_shape=[jax.ShapeDtypeStruct((HEAD...  104 us
    dot_general x12, matrix products, dims(): lax.dot_general(left, right, (((a,), (b,)), ((), ())), preferred_element_...  89.2 us
    pallas_call x1, Pallas kernels, gather(): pl.pallas_call(functools.partial(gather_kernel, chips, len(arrays)), out_...  48.1 us
    pallas_call x1, Pallas kernels, scatter(): pl.pallas_call(functools.partial(scatter_kernel, arrays[0].shape[0], len(...  42.7 us
    unnamed x33, local copies, waits for them, and re-layouts  13.9 us

profile of v2, /device:TPU:9, one launch (start us, length us, event | category | flops | bytes accessed | tf_op | source)
XLA Modules:
  0.0 480.3 jit_solution(14629472333572129062)
XLA Ops:
  0.8 0.7 pad.76
  6.9 0.7 convert_element_type.218
  7.6 1.3 compare_select_fusion
  8.9 0.8 select_convert_fusion.1
  9.7 0.8 convert_convert_fusion
  11.1 1.7 fusion.31.refs_0_
  12.7 1.7 copy.69
  15.2 1.7 copy.73
  16.9 48.1 %shard_map.314 = bf16[16,160,768]{2,1,0:T(8,128)(2,1)} custom-call(bf16[160,768]{1,0:T(8,128)(2,1)} %fusion.31.refs_0_), custom_call_target="tpu_custom_call" | custom-call | tf_op jit(solution)/shard_map/pallas_call | solution.py:195
  65.0 0.9 convert_reduce_fusion.1
  66.0 0.9 fusion.37
  66.9 1.3 convert_reduce_fusion.2
  68.7 8.9 %select_convert_fusion.refs_0_ = bf16[16,160,1024]{2,1,0:T(8,128)(2,1)} fusion(bf16[160]{0:T(256)(128)(2,1)S(1)} %compare_select_fusion.2, f32[16,160]{1,0:T(8,128)S(1)} %maximum_maximum_fusion, pred[160]{0:T(512)(128)(4,1)S(1)} %iota_compare_fusion.3, bf16[16,160,768]{2,1,0:T(8,128)(2,1)} %shard_map.314, bf16[1024,768]{0,1:T(8,128)(2,1)S(1)} %copy.69, ...), kind=kOutput, calls=%fused_computation.9 | convolution fusion | flops 4036493312 | bytes 10772960 | tf_op jit(solution)/shard_map/dot_general | solution.py:25
  77.6 103.6 %shard_map.315 = (bf16[16,48,1024]{2,1,0:T(8,128)(2,1)}, f32[16,1,1024]{2,1,0:T(1,128)}, bf16[16,48,768]{2,1,0:T(8,128)(2,1)}, bf16[16,192,768]{2,1,0:T(8,128)(2,1)}, bf16[16,48,3072]{2,1,0:T(8,128)(2,1)}) custom-call(bf16[16,160,1024]{2,1,0:T(8,128)(2,1)} %select_convert_fusion.refs_0_, bf16[2,16,1024]{2,1,0:T(8,128)(2,1)} %pad_maximum_fusion.refs_1_, ...), custom_call_target="tpu_custom_call" | custom-call | tf_op jit(solution)/shard_map/pallas_call | solution.py:492
  181.2 3.3 fusion.39
  185.0 9.3 %multiply_convert_fusion.1 = (bf16[1024,3072]{1,0:T(8,128)(2,1)S(1)}, f32[1024,3072]{1,0:T(8,128)}) fusion(f32[3072]{0:T(1024)S(1)} %reshape.449, bf16[3072,768]{1,0:T(8,128)(2,1)S(1)} %bitcast.115, f32[1024,768]{0,1:T(8,128)S(1)} %get-tuple-element.119, f32[768]{0:T(1024)S(1)} %reshape.448, f32[768]{0:T(1024)S(1)} %reshape.447, ...), kind=kOutput, calls=%fused_computation.7 | convolution fusion | flops 4854644736 | bytes 26765312 | tf_op jit(solution)/shard_map/dot_general | solution.py:25
  194.3 12.3 %fusion.42 = (bf16[3072]{0:T(1024)(128)(2,1)S(1)}, bf16[1024,3072]{1,0:T(8,128)(2,1)S(1)}) fusion(f32[1024,3072]{1,0:T(8,128)} %get-tuple-element.121, f32[3072]{0:T(1024)S(1)} %reshape.449, bf16[768,3072]{1,0:T(8,128)(2,1)S(1)} %bitcast.119, bf16[1024,768]{0,1:T(8,128)(2,1)S(1)} %copy.73, f32[1024]{0:T(1024)S(1)} %bitcast.106), kind=kOutput, calls=%fused_computation.114 | convolution fusion | flops 4878234624 | bytes 25188352 | tf_op jit(solution)/shard_map/dot_general | solution.py:25
  206.6 6.3 %add_convert_fusion = bf16[1024,768]{0,1:T(8,128)(2,1)} fusion(f32[1024,768]{0,1:T(8,128)S(1)} %get-tuple-element.119, bf16[1024,3072]{1,0:T(8,128)(2,1)S(1)} %get-tuple-element.120, bf16[768,3072]{1,0:T(8,128)(2,1)S(1)} %bitcast.120, f32[768]{0:T(1024)S(1)} %reshape.450), kind=kOutput, calls=%fused_computation.39 | convolution fusion | flops 4834197504 | bytes 15731712 | tf_op jit(solution)/shard_map/dot_general | solution.py:25
  212.9 7.0 %convolution_convert_fusion = bf16[768,3072]{1,0:T(8,128)(2,1)} fusion(bf16[1024,3072]{1,0:T(8,128)(2,1)S(1)} %get-tuple-element.120, bf16[1024,768]{0,1:T(8,128)(2,1)S(1)} %copy.73, f32[1024]{0:T(1024)S(1)} %bitcast.107), kind=kOutput, calls=%fused_computation.13 | convolution fusion | flops 4836556800 | bytes 12587008 | tf_op jit(solution)/shard_map/dot_general | solution.py:25
  219.9 6.7 %fusion.41 = (bf16[768]{0:T(1024)(128)(2,1)S(1)}, f32[1024,768]{1,0:T(8,128)}) fusion(bf16[1024,3072]{1,0:T(8,128)(2,1)S(1)} %get-tuple-element.127, bf16[3072,768]{1,0:T(8,128)(2,1)S(1)} %bitcast.116), kind=kOutput, calls=%fused_computation.113 | convolution fusion | flops 4832623616 | bytes 14157312 | tf_op jit(solution)/shard_map/dot_general | solution.py:25
  226.6 2.6 copy.88
  230.7 3.5 copy.74
  234.2 4.0 multiply_reduce_fusion
  238.2 10.5 %convolution_convert_fusion.1 = bf16[3072,768]{1,0:T(8,128)(2,1)} fusion(bf16[1024,3072]{1,0:T(8,128)(2,1)} %copy-done.8, f32[1024,768]{0,1:T(8,128)S(1)} %copy-done.1, f32[768]{0:T(1024)S(1)} %reshape.448, f32[768]{0:T(1024)S(1)} %reshape.447, f32[1024]{0:T(1024)S(1)} %add_rsqrt_fusion, f32[1024]{0:T(1024)S(1)} %broadcast_multiply_fusion.4), kind=kOutput, calls=%fused_computation.14 | convolution fusion | flops 4838129664 | bytes 14170112 | tf_op jit(solution)/shard_map/dot_general | solution.py:25
  248.8 6.0 %convert_reduce_fusion.8 = (bf16[768]{0:T(1024)(128)(2,1)S(1)}, f32[1024,768]{0,1:T(8,128)}, bf16[768]{0:T(1024)(128)(2,1)S(1)}) fusion(f32[1024]{0:T(1024)S(1)} %broadcast_multiply_fusion.2, f32[1024,768]{0,1:T(8,128)} %copy-done, f32[1024]{0:T(1024)S(1)} %broadcast_multiply_fusion.4, f32[1024]{0:T(1024)S(1)} %broadcast_multiply_fusion.3, ...), kind=kLoop, calls=%fused_computation.105 | loop fusion | flops 11008512 | bytes 11036672 | tf_op jit(solution)/shard_map/reduce_sum | solution.py:592
  255.0 0.7 copy.84
  256.9 4.9 %convolution_convert_fusion.2 = bf16[768,1024]{1,0:T(8,128)(2,1)} fusion(bf16[768,768]{1,0:T(8,128)(2,1)} %bitcast.122, f32[1024,768]{0,1:T(8,128)} %get-tuple-element.99), kind=kOutput, calls=%fused_computation.46 | convolution fusion | flops 1209532416 | bytes 5898240 | tf_op jit(solution)/shard_map/dot_general | solution.py:25
  261.9 2.5 convolution_convert_fusion.3
  264.4 118.0 %shard_map.316 = (bf16[16,160,1024]{2,1,0:T(8,128)(2,1)}, f32[48,768]{1,0:T(8,128)}, f32[192,768]{1,0:T(8,128)}, f32[48,3072]{1,0:T(8,128)}) custom-call(bf16[16,160,1024]{2,1,0:T(8,128)(2,1)} %select_convert_fusion.refs_0_, bf16[2,16,1024]{2,1,0:T(8,128)(2,1)} %pad_maximum_fusion.refs_1_, f32[1,1024]{1,0:T(1,128)} %get-tuple-element.116.refs_2_, ...), custom_call_target="tpu_custom_call" | custom-call | tf_op jit(solution)/shard_map/pallas_call | solution.py:529
  382.3 9.7 %fusion.40 = (bf16[768]{0:T(1024)(128)(2,1)S(1)}, f32[1024,768]{1,0:T(8,128)}) fusion(bf16[16,160,1024]{2,1,0:T(8,128)(2,1)} %get-tuple-element.31, bf16[16,160,768]{2,1,0:T(8,128)(2,1)} %shard_map.314), kind=kOutput, calls=%fused_computation.112 | convolution fusion | flops 4027317504 | bytes 12322304 | tf_op jit(solution)/shard_map/dot_general | solution.py:25
  392.2 3.3 reduce
  395.5 7.8 %fusion.28 = bf16[16,160,768]{2,1,0:T(8,128)(2,1)S(1)} fusion(bf16[16,160,1024]{2,1,0:T(8,128)(2,1)} %get-tuple-element.31, bf16[1024,768]{0,1:T(8,128)(2,1)S(1)} %copy.69, f32[768]{0:T(1024)S(1)} %reshape.443, f32[768]{0:T(1024)S(1)} %reshape.442, f32[1024]{0:T(1024)S(1)} %add_rsqrt_fusion.1, f32[1024]{0:T(1024)S(1)} %broadcast_multiply_fusion.5), kind=kOutput, calls=%fused_computation.52 | convolution fusion | flops 4031250432 | bytes 10762240 | tf_op jit(solution)/shard_map/dot_general | solution.py:25
  403.3 1.9 copy-done.2
  405.2 0.7 copy.80
  407.2 3.6 copy.75
  410.8 2.9 fusion.19
  413.9 5.6 %fusion.18 = f32[1024,768]{0,1:T(8,128)} fusion(f32[1024,768]{0,1:T(8,128)} %get-tuple-element.99, bf16[1024,768]{0,1:T(8,128)(2,1)S(1)} %copy.69, f32[1024,768]{0,1:T(8,128)} %copy.75, f32[1024]{0:T(1024)S(1)} %broadcast_multiply_fusion, f32[1024]{0:T(1024)S(1)} %broadcast_multiply_fusion.1, f32[768]{0:T(1024)S(1)} %reshape.442, ...), kind=kLoop, calls=%fused_computation.30 | loop fusion | flops 7077888 | bytes 11029504 | tf_op jit(solution)/shard_map/add | solution.py:713
  419.4 3.7 copy.89
  423.1 0.7 copy.79
  423.8 3.5 stack.96
  427.3 3.0 fusion.6.refs_0_
  430.3 42.7 %shard_map.317 = f32[160,768]{1,0:T(8,128)} custom-call(bf16[16,160,768]{2,1,0:T(8,128)(2,1)} %fusion.6.refs_0_), custom_call_target="tpu_custom_call" | custom-call | tf_op jit(solution)/shard_map/pallas_call | solution.py:354
  473.0 1.3 slice.117
  474.3 1.5 slice_bitcast_fusion.3
  475.8 1.8 slice_bitcast_fusion
  477.6 0.7 copy.102
  478.3 0.8 copy.103
  479.1 0.8 copy.104
  (99 shorter events, 12.7 us)
Async XLA Ops:
  181.1 3.8 slice-start.1
  181.1 3.8 slice-start.2
  184.5 22.1 %copy-start = (f32[1024,768]{0,1:T(8,128)}, f32[1024,768]{0,1:T(8,128)S(1)}, u32[]{:S(2)}) copy-start(f32[1024,768]{0,1:T(8,128)S(1)} %get-tuple-element.119) | copy-start | bytes 9437188
  184.5 9.7 %slice-start.3 = ((s8[4718592]{0:T(1024)(128)(4,1)}), s8[4194304]{0:T(1024)(128)(4,1)S(1)}, s32[]{:S(2)}) async-start(s8[4718592]{0:T(1024)(128)(4,1)} %bitcast.117), calls=%async_computation.3 | async-start | bytes 8388608
  185.0 9.3 %slice-start.4 = ((s8[4718592]{0:T(1024)(128)(4,1)}), s8[524288]{0:T(1024)(128)(4,1)S(1)}, s32[]{:S(2)}) async-start(s8[4718592]{0:T(1024)(128)(4,1)} %bitcast.117), calls=%async_computation.4 | async-start | bytes 1048576
  206.6 13.3 %copy-start.8 = (bf16[1024,3072]{1,0:T(8,128)(2,1)}, bf16[1024,3072]{1,0:T(8,128)(2,1)S(1)}, u32[]{:S(2)}) copy-start(bf16[1024,3072]{1,0:T(8,128)(2,1)S(1)} %get-tuple-element.127) | copy-start | bytes 18874372
  234.2 4.0 copy-start.1
  256.9 5.0 %copy-start.3 = (f32[1024,768]{0,1:T(8,128)S(1)}, f32[1024,768]{0,1:T(8,128)}, u32[]{:S(2)}) copy-start(f32[1024,768]{0,1:T(8,128)} %get-tuple-element.99) | copy-start | bytes 9437188
  256.9 5.0 %copy-start.4 = (bf16[16,48,1024]{2,1,0:T(8,128)(2,1)S(1)}, bf16[16,48,1024]{2,1,0:T(8,128)(2,1)}, u32[]{:S(2)}) copy-start(bf16[16,48,1024]{2,1,0:T(8,128)(2,1)} %get-tuple-element.26.refs_3_) | copy-start | bytes 4718596
  403.2 1.9 copy-start.2
  419.4 7.9 %slice-start = ((bf16[16,160,768]{2,1,0:T(8,128)(2,1)}), bf16[16,144,768]{2,1,0:T(8,128)(2,1)S(1)}, s32[]{:S(2)}) async-start(bf16[16,160,768]{2,1,0:T(8,128)(2,1)} %copy-done.2), calls=%async_computation | async-start | bytes 7077888 | tf_op jit(solution)/shard_map/slice | solution.py:732
  430.3 47.3 %copy-start.7 = (f32[48,768]{1,0:T(8,128)S(1)}, f32[48,768]{1,0:T(8,128)}, u32[]{:S(2)}) copy-start(f32[48,768]{1,0:T(8,128)} %get-tuple-element.32) | copy-start | bytes 442372
  430.3 48.0 %copy-start.6 = (f32[192,768]{1,0:T(8,128)S(1)}, f32[192,768]{1,0:T(8,128)}, u32[]{:S(2)}) copy-start(f32[192,768]{1,0:T(8,128)} %get-tuple-element.33) | copy-start | bytes 1769476
  430.3 48.8 %copy-start.5 = (f32[48,3072]{1,0:T(8,128)S(1)}, f32[48,3072]{1,0:T(8,128)}, u32[]{:S(2)}) copy-start(f32[48,3072]{1,0:T(8,128)} %get-tuple-element.34) | copy-start | bytes 1769476

commit v3 on v2

--- a/solution.py
+++ b/solution.py
@@ -1,4 +1,5 @@
 import functools
+import itertools
 import math
 
 import jax
@@ -16,8 +17,8 @@
 MASKED = -1e30
 SPARE = 16
 SEGS = 4
-GATHER_STEPS = (0, 3, 6, 10, 14)
-SCATTER_STEPS = (0, 2, 6, 9, 12, 15)
+GATHER_STEPS = (1, HEADS)
+SCATTER_STEPS = (0, HEADS)
 CHUNK = 512
 
 
@@ -62,12 +63,26 @@
     pl.semaphore_wait(barrier, count)
 
 
-def held_blocks(me, axes, done):
-    ids = [me]
-    for a in done:
-        stride, size = axes[a]
-        ids = [i + (v - place(me, axes[a])) * stride for i in ids for v in range(size)]
-    return ids
+def moved(me, axes, order, steps, sign):
+    for a, step in zip(order, steps):
+        size = axes[a][1]
+        if step:
+            other = peer(me, axes[a], step if sign > 0 else size - step)
+            me = me + (other - me)
+    return me
+
+
+def grid_of(axes, order):
+    return [range(axes[a][1]) for a in order]
+
+
+def slots_of(axes, order):
+    slots = {}
+    for k in range(len(order)):
+        for steps in itertools.product(*grid_of(axes, order[: k + 1])):
+            if steps[-1]:
+                slots[steps] = len(slots)
+    return slots
 
 
 def half(ref, block, c):
@@ -83,92 +98,87 @@
 def gather_plan(ins, outs, sems, me, c, axes):
     order = axis_orders(axes)[c]
     send, recv, pass_send, pass_recv, own = sems
-    chips = outs[0].shape[0]
-    stages = []
-    count = [0]
-    passed = [0]
-    pending = []
-
-    def hand_over(ids, first=False):
-        for n, block in enumerate(ids):
-            for k, (src, dst) in enumerate(zip(ins, outs)):
-                slot = passed[0] + n * len(outs) + k
-                source = flat_half(src, c) if first else half(dst, block, c)
+    arrays = len(outs)
+    slots = slots_of(axes, order)
+
+    def block_of(steps):
+        return moved(me, axes, order, steps, -1)
+
+    def message(steps):
+        before = steps[:-1]
+        target = moved(me, axes, order[len(before) :], steps[-1:], 1)
+        block = block_of(before)
+        fresh = not any(before)
+        return [
+            pltpu.make_async_remote_copy(
+                flat_half(src, c) if fresh else half(dst, block, c),
+                half(dst, block, c),
+                send.at[slots[steps] * arrays + k],
+                recv.at[slots[steps] * arrays + k],
+                device_id=(target, c), device_id_type=MESH,
+            )
+            for k, (src, dst) in enumerate(zip(ins, outs))
+        ]
+
+    def send_on(steps):
+        for k in range(len(steps), len(order)):
+            lead = steps + (0,) * (k - len(steps))
+            for step in range(1, axes[order[k]][1]):
+                for copy in message(lead + (step,)):
+                    copy.start()
+
+    def hand_over(steps):
+        block = block_of(steps)
+        return [
+            pltpu.make_async_remote_copy(
+                half(dst, block, c), half(dst, block, c),
+                pass_send.at[slots[steps] * arrays + k], pass_recv.at[slots[steps] * arrays + k],
+                device_id=(me, 1 - c), device_id_type=MESH,
+            )
+            for k, dst in enumerate(outs)
+        ]
+
+    def keep_own():
+        return [pltpu.make_async_copy(s, d.at[me], own.at[k]) for k, (s, d) in enumerate(zip(ins, outs))]
+
+    def first():
+        send_on(())
+        for copy in keep_own():
+            copy.start()
+
+    def arrive(steps):
+        def run():
+            for copy in message(steps):
+                copy.wait_recv()
+            send_on(steps)
+            for copy in hand_over(steps):
+                copy.start()
+        return run
+
+    def last():
+        for copy in keep_own():
+            copy.wait()
+        for steps in slots:
+            for copy in message(steps):
+                copy.wait_send()
+            for copy in hand_over(steps):
+                copy.wait_send()
+        other = axis_orders(axes)[1 - c]
+        other_slots = slots_of(axes, other)
+        for steps, slot in other_slots.items():
+            block = moved(me, axes, other, steps, -1)
+            for k, dst in enumerate(outs):
+                n = slot * arrays + k
                 pltpu.make_async_remote_copy(
-                    source, half(dst, block, c), pass_send.at[slot], pass_recv.at[slot],
+                    half(dst, block, 1 - c), half(dst, block, 1 - c),
+                    pass_send.at[n], pass_recv.at[n],
                     device_id=(me, 1 - c), device_id_type=MESH,
-                ).start()
-        passed[0] += len(ids) * len(outs)
-
-    def copies(number):
-        axis = axes[order[number]]
-        ids = held_blocks(me, axes, order[:number])
-        base = sum(
-            (axes[order[m]][1] - 1) * math.prod(axes[a][1] for a in order[:m]) * len(outs)
-            for m in range(number)
-        )
-        out = []
-        slot = base
-        for step in range(1, axis[1]):
-            target = peer(me, axis, step)
-            source = peer(me, axis, axis[1] - step)
-            for block in ids:
-                for k, (src, dst) in enumerate(zip(ins, outs)):
-                    first = number == 0
-                    out.append((
-                        pltpu.make_async_remote_copy(
-                            flat_half(src, c) if first else half(dst, block, c),
-                            half(dst, block, c), send.at[slot], recv.at[slot],
-                            device_id=(target, c), device_id_type=MESH,
-                        ),
-                        block + (source - me),
-                    ))
-                    slot += 1
-        return out
-
-    def begin(number):
-        for copy, _ in copies(number):
-            copy.start()
-
-    def land(number):
-        got = copies(number)
-        for copy, _ in got:
-            copy.wait_recv()
-        return [block for _, block in got[:: len(outs)]]
-
-    def first():
-        for k, (src, dst) in enumerate(zip(ins, outs)):
-            pltpu.make_async_copy(src, dst.at[me], own.at[k]).start()
-        begin(0)
-
-    def middle(number):
-        def run():
-            blocks = land(number)
-            if number == 0:
-                for k, (src, dst) in enumerate(zip(ins, outs)):
-                    pltpu.make_async_copy(src, dst.at[me], own.at[k]).wait()
-            if number + 1 < len(order):
-                begin(number + 1)
-            hand_over(blocks)
-        return run
-
-    def last():
-        total = (chips - 1) * len(outs)
-        for number in range(len(order)):
-            for copy, _ in copies(number):
-                copy.wait_send()
-        for k in range(total):
-            dst = outs[k % len(outs)]
-            pltpu.make_async_remote_copy(
-                half(dst, me, c), half(dst, me, 1 - c), pass_send.at[k], pass_recv.at[k],
-                device_id=(me, 1 - c), device_id_type=MESH,
-            ).wait()
-
-    stages.append(first)
-    for number in range(len(order)):
-        stages.append(middle(number))
-    stages.append(last)
-    return stages
+                ).wait_recv()
+
+    def cost(steps):
+        return (sum(1 for s in steps if s), len(steps), steps)
+
+    return [first] + [arrive(steps) for steps in sorted(slots, key=cost)] + [last]
 
 
 def gather_sems(chips, arrays):
@@ -202,120 +212,141 @@
     )(*arrays)
 
 
-def phase_base(axes, order, number, arrays):
-    return sum(
-        (axes[order[m]][1] - 1) * math.prod(axes[a][1] for a in order[:m]) * arrays
-        for m in range(number)
-    )
-
-
 def scatter_plan(ins, outs, accs, halves, landed, results, sems, me, c, axes):
     order = axis_orders(axes)[c]
-    send, recv, swap_send, swap_recv, own, out_sem = sems
+    send, recv, swap_send, swap_recv, own, out_sem, last_send, last_recv = sems
     arrays = len(ins)
-
-    def swap():
-        copies = []
-        for k in range(arrays):
-            width = ins[k].shape[-1] // 2
-            copies.append((
-                pltpu.make_async_remote_copy(
-                    ins[k].at[:, :, pl.ds((1 - c) * width, width)], halves[k],
-                    swap_send.at[k], swap_recv.at[k],
-                    device_id=(me, 1 - c), device_id_type=MESH,
-                ),
-                pltpu.make_async_copy(
-                    ins[k].at[:, :, pl.ds(c * width, width)], accs[k], own.at[k]
-                ),
-            ))
-        return copies
-
-    def copies(number):
-        axis = axes[order[number]]
-        ids = held_blocks(me, axes, order[:number])
-        slot = phase_base(axes, order, number, 1)
-        out = []
-        for step in range(1, axis[1]):
-            target = peer(me, axis, step)
-            for block in ids:
-                for k in range(arrays):
-                    n = slot * arrays + k
-                    out.append((
-                        pltpu.make_async_remote_copy(
-                            accs[k].at[block + (target - me)], landed[k].at[slot],
-                            send.at[n], recv.at[n],
-                            device_id=(target, c), device_id_type=MESH,
-                        ),
-                        block, k, slot,
-                    ))
-                slot += 1
-        return out
-
-    def begin(number):
-        for copy, *_ in copies(number):
-            copy.start()
+    slots = slots_of(axes, order)
+    depth = len(order)
+
+    def all_steps(number):
+        steps = itertools.product(*grid_of(axes, order[:number]))
+        return sorted(steps, key=lambda t: (-sum(1 for s in t if s), [-s for s in reversed(t)]))
+
+    def owner(steps):
+        return moved(me, axes, order, steps, 1)
+
+    whole = all_steps(depth)
+
+    def swap(steps, core):
+        there = axis_orders(axes)[core]
+        names = all_steps_of(there)
+        n = names.index(steps)
+        block = moved(me, axes, there, steps, 1)
+        return [
+            pltpu.make_async_remote_copy(
+                half(ins[k], block, core), halves[k].at[block],
+                swap_send.at[n * arrays + k], swap_recv.at[n * arrays + k],
+                device_id=(me, 1 - c), device_id_type=MESH,
+            )
+            for k in range(arrays)
+        ]
+
+    def all_steps_of(there):
+        steps = itertools.product(*grid_of(axes, there))
+        return sorted(steps, key=lambda t: (-sum(1 for s in t if s), [-s for s in reversed(t)]))
+
+    def load(steps):
+        block = owner(steps)
+        n = whole.index(steps)
+        return [
+            pltpu.make_async_copy(half(ins[k], block, c), accs[k].at[block], own.at[n * arrays + k])
+            for k in range(arrays)
+        ]
+
+    def message(steps):
+        block = owner(steps)
+        target = moved(me, axes, order[len(steps) - 1 :], steps[-1:], 1)
+        slot = slots[steps]
+        return [
+            pltpu.make_async_remote_copy(
+                accs[k].at[block], landed[k].at[slot],
+                send.at[slot * arrays + k], recv.at[slot * arrays + k],
+                device_id=(target, c), device_id_type=MESH,
+            )
+            for k in range(arrays)
+        ]
+
+    def send_on(steps):
+        if steps and steps[-1]:
+            for copy in message(steps):
+                copy.start()
 
     def first():
-        for remote, local in swap():
-            remote.start()
-            local.start()
-
-    def add_pair():
-        for remote, local in swap():
-            local.wait()
-            remote.wait()
-        for k in range(arrays):
-            @pl.loop(0, accs[k].shape[0])
-            def _(block):
+        for steps in all_steps_of(axis_orders(axes)[1 - c]):
+            for copy in swap(steps, 1 - c):
+                copy.start()
+        for steps in whole:
+            for copy in load(steps):
+                copy.start()
+
+    def add_pair(steps):
+        def run():
+            for copy in load(steps):
+                copy.wait()
+            for copy in swap(steps, c):
+                copy.wait_recv()
+            block = owner(steps)
+            for k in range(arrays):
                 accs[k][block] = (
                     accs[k][block].astype(F32) + halves[k][block].astype(F32)
                 ).astype(BF16)
-        begin(len(order) - 1)
-
-    def add(number):
+            send_on(steps)
+        return run
+
+    def add(steps):
         def run():
-            got = copies(number)
-            for copy, *_ in got:
-                copy.wait()
-            groups = {}
-            for position, (_, block, k, slot) in enumerate(got):
-                ids = math.prod(axes[a][1] for a in order[:number])
-                groups.setdefault((position // arrays % ids, k), (block, []))[1].append(slot)
-            for (_, k), (block, slots) in groups.items():
+            got = [steps + (s,) for s in range(1, axes[order[len(steps)]][1])]
+            for came in got:
+                for copy in message(came):
+                    copy.wait_recv()
+            block = owner(steps)
+            for k in range(arrays):
                 total = accs[k][block].astype(F32)
-                for slot in slots:
-                    total = total + landed[k][slot].astype(F32)
-                if number:
+                for came in got:
+                    total = total + landed[k][slots[came]].astype(F32)
+                if steps:
                     accs[k][block] = total.astype(BF16)
                 else:
                     width = total.shape[-1]
                     results[k][:, pl.ds(c * width, width)] = total
-            if number:
-                begin(number - 1)
+            if steps:
+                send_on(steps)
             else:
-                for copy in finals():
+                for copy in finals(c):
                     copy.start()
         return run
 
-    def finals():
+    def finals(core):
         return [
             pltpu.make_async_remote_copy(
-                flat_half(results[k], c), flat_half(results[k], c),
-                swap_send.at[arrays + k], swap_recv.at[arrays + k],
+                flat_half(results[k], core), flat_half(results[k], core),
+                last_send.at[k], last_recv.at[k],
                 device_id=(me, 1 - c), device_id_type=MESH,
             )
             for k in range(arrays)
         ]
 
     def last():
+        for steps in slots:
+            for copy in message(steps):
+                copy.wait_send()
+        for steps in all_steps_of(axis_orders(axes)[1 - c]):
+            for copy in swap(steps, 1 - c):
+                copy.wait_send()
         outgoing = [pltpu.make_async_copy(results[k], outs[k], out_sem.at[k]) for k in range(arrays)]
-        for copy, out in zip(finals(), outgoing):
-            copy.wait()
+        for copy in finals(c):
+            copy.wait_send()
+        for copy, out in zip(finals(1 - c), outgoing):
+            copy.wait_recv()
             out.start()
         for out in outgoing:
             out.wait()
 
-    return [first, add_pair] + [add(n) for n in reversed(range(len(order)))] + [last]
+    events = [first] + [add_pair(steps) for steps in whole]
+    for number in reversed(range(depth)):
+        events += [add(steps) for steps in all_steps(number)]
+    return events + [last]
 
 
 def scatter_scratch(arrays):
@@ -326,9 +357,8 @@
         scratch += [pltpu.VMEM((rows, a.shape[1], a.shape[2] // 2), BF16) for a in arrays]
     scratch += [pltpu.VMEM(a.shape[1:], F32) for a in arrays]
     dma = pltpu.SemaphoreType.DMA
-    return scratch + [dma(((chips - 1) * number,)) for _ in range(2)] + [
-        dma((n,)) for n in (2 * number, 2 * number, number, number)
-    ]
+    sizes = (chips - 1,) * 2 + (chips,) * 3 + (1,) * 3
+    return scratch + [dma((n * number,)) for n in sizes]
 
 
 def scatter_parts(arrays, refs):
@@ -458,6 +488,11 @@
     return pl.BlockSpec(shape, lambda h: (0,) * len(shape))
 
 
+def spread_over(number, begin, end):
+    inner = number - 2
+    return [0] + [begin + n * (end - begin) // inner for n in range(inner)] + [HEADS - 1]
+
+
 def run_stages(plan, when, chips):
     me, core = lax.axis_index("wide"), lax.axis_index("narrow")
     axes = chip_axes(chips)
@@ -468,7 +503,8 @@
         greet(me, core, axes)
 
     for c in range(2):
-        for stage, step in zip(plan(me, c, axes), when):
+        stages = plan(me, c, axes)
+        for stage, step in zip(stages, spread_over(len(stages), *when)):
             @pl.when((core == c) & (h == step))
             def _(stage=stage):
                 stage()

time: 487 us -> 413 us (0.85)
  the two profiles are of different devices: /device:TPU:9 before, /device:TPU:0 now
where the time goes in v3:
time: 413 us; the launch traced here: 407 us
  Pallas kernels  239 us (58%)
  matrix products  89.4 us (22%)
  local copies, waits for them, and re-layouts  42.5 us (10%)
  other arithmetic  34.8 us (8%)
    pallas_call x1, Pallas kernels, attention_back(): pl.pallas_call(body, grid=(HEADS,), out_shape=[jax.ShapeDtypeStruct((HEAD...  103 us
    dot_general x12, matrix products, dims(): lax.dot_general(left, right, (((a,), (b,)), ((), ())), preferred_element_...  89.4 us
    pallas_call x1, Pallas kernels, attention(): pl.pallas_call(body, grid=(HEADS,), out_shape=[jax.ShapeDtypeStruct((HEAD...  76.4 us
    pallas_call x1, Pallas kernels, gather(): pl.pallas_call(functools.partial(gather_kernel, chips, len(arrays)), out_...  30.5 us
    pallas_call x1, Pallas kernels, scatter(): pl.pallas_call(functools.partial(scatter_kernel, arrays[0].shape[0], len(...  28.9 us
    unnamed x33, local copies, waits for them, and re-layouts  13.9 us
    another operation x19, local copies, waits for them, and re-layouts, shards(): jnp.stack([jnp.pad(s.reshape(chips, -1), ((0, 0), (0, width - s.size // c...  9.49 us

profile of v3, /device:TPU:0, one launch (start us, length us, event | category | flops | bytes accessed | tf_op | source)
XLA Modules:
  0.0 406.6 jit_solution(16768209473921629113)
XLA Ops:
  0.8 0.7 pad.76
  6.9 0.7 convert_element_type.218
  7.6 1.3 compare_select_fusion
  8.9 0.8 select_convert_fusion.1
  9.7 0.8 convert_convert_fusion
  11.1 1.7 fusion.31.refs_0_
  12.7 1.7 copy.69
  15.2 1.7 copy.73
  16.9 30.5 %shard_map.314 = bf16[16,160,768]{2,1,0:T(8,128)(2,1)} custom-call(bf16[160,768]{1,0:T(8,128)(2,1)} %fusion.31.refs_0_), custom_call_target="tpu_custom_call" | custom-call | tf_op jit(solution)/shard_map/pallas_call | solution.py:205
  47.5 0.9 convert_reduce_fusion.1
  48.4 0.9 fusion.37
  49.4 1.3 convert_reduce_fusion.2
  51.1 8.9 %select_convert_fusion.refs_0_ = bf16[16,160,1024]{2,1,0:T(8,128)(2,1)} fusion(bf16[160]{0:T(256)(128)(2,1)S(1)} %compare_select_fusion.2, f32[16,160]{1,0:T(8,128)S(1)} %maximum_maximum_fusion, pred[160]{0:T(512)(128)(4,1)S(1)} %iota_compare_fusion.3, bf16[16,160,768]{2,1,0:T(8,128)(2,1)} %shard_map.314, bf16[1024,768]{0,1:T(8,128)(2,1)S(1)} %copy.69, ...), kind=kOutput, calls=%fused_computation.9 | convolution fusion | flops 4036493312 | bytes 10772960 | tf_op jit(solution)/shard_map/dot_general | solution.py:26
  60.0 76.4 %shard_map.315 = (bf16[16,48,1024]{2,1,0:T(8,128)(2,1)}, f32[16,1,1024]{2,1,0:T(1,128)}, bf16[16,48,768]{2,1,0:T(8,128)(2,1)}, bf16[16,192,768]{2,1,0:T(8,128)(2,1)}, bf16[16,48,3072]{2,1,0:T(8,128)(2,1)}) custom-call(bf16[16,160,1024]{2,1,0:T(8,128)(2,1)} %select_convert_fusion.refs_0_, bf16[2,16,1024]{2,1,0:T(8,128)(2,1)} %pad_maximum_fusion.refs_1_, ...), custom_call_target="tpu_custom_call" | custom-call | tf_op jit(solution)/shard_map/pallas_call | solution.py:528
  136.5 3.3 fusion.39
  140.3 9.3 %multiply_convert_fusion.1 = (bf16[1024,3072]{1,0:T(8,128)(2,1)S(1)}, f32[1024,3072]{1,0:T(8,128)}) fusion(f32[3072]{0:T(1024)S(1)} %reshape.449, bf16[3072,768]{1,0:T(8,128)(2,1)S(1)} %bitcast.115, f32[1024,768]{0,1:T(8,128)S(1)} %get-tuple-element.119, f32[768]{0:T(1024)S(1)} %reshape.448, f32[768]{0:T(1024)S(1)} %reshape.447, ...), kind=kOutput, calls=%fused_computation.7 | convolution fusion | flops 4854644736 | bytes 26765312 | tf_op jit(solution)/shard_map/dot_general | solution.py:26
  149.6 12.3 %fusion.42 = (bf16[3072]{0:T(1024)(128)(2,1)S(1)}, bf16[1024,3072]{1,0:T(8,128)(2,1)S(1)}) fusion(f32[1024,3072]{1,0:T(8,128)} %get-tuple-element.121, f32[3072]{0:T(1024)S(1)} %reshape.449, bf16[768,3072]{1,0:T(8,128)(2,1)S(1)} %bitcast.119, bf16[1024,768]{0,1:T(8,128)(2,1)S(1)} %copy.73, f32[1024]{0:T(1024)S(1)} %bitcast.106), kind=kOutput, calls=%fused_computation.114 | convolution fusion | flops 4878234624 | bytes 25188352 | tf_op jit(solution)/shard_map/dot_general | solution.py:26
  161.9 6.3 %add_convert_fusion = bf16[1024,768]{0,1:T(8,128)(2,1)} fusion(f32[1024,768]{0,1:T(8,128)S(1)} %get-tuple-element.119, bf16[1024,3072]{1,0:T(8,128)(2,1)S(1)} %get-tuple-element.120, bf16[768,3072]{1,0:T(8,128)(2,1)S(1)} %bitcast.120, f32[768]{0:T(1024)S(1)} %reshape.450), kind=kOutput, calls=%fused_computation.39 | convolution fusion | flops 4834197504 | bytes 15731712 | tf_op jit(solution)/shard_map/dot_general | solution.py:26
  168.2 7.0 %convolution_convert_fusion = bf16[768,3072]{1,0:T(8,128)(2,1)} fusion(bf16[1024,3072]{1,0:T(8,128)(2,1)S(1)} %get-tuple-element.120, bf16[1024,768]{0,1:T(8,128)(2,1)S(1)} %copy.73, f32[1024]{0:T(1024)S(1)} %bitcast.107), kind=kOutput, calls=%fused_computation.13 | convolution fusion | flops 4836556800 | bytes 12587008 | tf_op jit(solution)/shard_map/dot_general | solution.py:26
  175.2 6.7 %fusion.41 = (bf16[768]{0:T(1024)(128)(2,1)S(1)}, f32[1024,768]{1,0:T(8,128)}) fusion(bf16[1024,3072]{1,0:T(8,128)(2,1)S(1)} %get-tuple-element.127, bf16[3072,768]{1,0:T(8,128)(2,1)S(1)} %bitcast.116), kind=kOutput, calls=%fused_computation.113 | convolution fusion | flops 4832623616 | bytes 14157312 | tf_op jit(solution)/shard_map/dot_general | solution.py:26
  181.9 2.6 copy.88
  186.0 3.5 copy.74
  189.5 4.0 multiply_reduce_fusion
  193.5 10.7 %convolution_convert_fusion.1 = bf16[3072,768]{1,0:T(8,128)(2,1)} fusion(bf16[1024,3072]{1,0:T(8,128)(2,1)} %copy-done.8, f32[1024,768]{0,1:T(8,128)S(1)} %copy-done.1, f32[768]{0:T(1024)S(1)} %reshape.448, f32[768]{0:T(1024)S(1)} %reshape.447, f32[1024]{0:T(1024)S(1)} %add_rsqrt_fusion, f32[1024]{0:T(1024)S(1)} %broadcast_multiply_fusion.4), kind=kOutput, calls=%fused_computation.14 | convolution fusion | flops 4838129664 | bytes 14170112 | tf_op jit(solution)/shard_map/dot_general | solution.py:26
  204.3 6.0 %convert_reduce_fusion.8 = (bf16[768]{0:T(1024)(128)(2,1)S(1)}, f32[1024,768]{0,1:T(8,128)}, bf16[768]{0:T(1024)(128)(2,1)S(1)}) fusion(f32[1024]{0:T(1024)S(1)} %broadcast_multiply_fusion.2, f32[1024,768]{0,1:T(8,128)} %copy-done, f32[1024]{0:T(1024)S(1)} %broadcast_multiply_fusion.4, f32[1024]{0:T(1024)S(1)} %broadcast_multiply_fusion.3, ...), kind=kLoop, calls=%fused_computation.105 | loop fusion | flops 11008512 | bytes 11036672 | tf_op jit(solution)/shard_map/reduce_sum | solution.py:628
  210.5 0.7 copy.84
  212.4 4.9 %convolution_convert_fusion.2 = bf16[768,1024]{1,0:T(8,128)(2,1)} fusion(bf16[768,768]{1,0:T(8,128)(2,1)} %bitcast.122, f32[1024,768]{0,1:T(8,128)} %get-tuple-element.99), kind=kOutput, calls=%fused_computation.46 | convolution fusion | flops 1209532416 | bytes 5898240 | tf_op jit(solution)/shard_map/dot_general | solution.py:26
  217.4 2.5 convolution_convert_fusion.3
  219.9 102.8 %shard_map.316 = (bf16[16,160,1024]{2,1,0:T(8,128)(2,1)}, f32[48,768]{1,0:T(8,128)}, f32[192,768]{1,0:T(8,128)}, f32[48,3072]{1,0:T(8,128)}) custom-call(bf16[16,160,1024]{2,1,0:T(8,128)(2,1)} %select_convert_fusion.refs_0_, bf16[2,16,1024]{2,1,0:T(8,128)(2,1)} %pad_maximum_fusion.refs_1_, f32[1,1024]{1,0:T(1,128)} %get-tuple-element.116.refs_2_, ...), custom_call_target="tpu_custom_call" | custom-call | tf_op jit(solution)/shard_map/pallas_call | solution.py:565
  322.6 9.7 %fusion.40 = (bf16[768]{0:T(1024)(128)(2,1)S(1)}, f32[1024,768]{1,0:T(8,128)}) fusion(bf16[16,160,1024]{2,1,0:T(8,128)(2,1)} %get-tuple-element.31, bf16[16,160,768]{2,1,0:T(8,128)(2,1)} %shard_map.314), kind=kOutput, calls=%fused_computation.112 | convolution fusion | flops 4027317504 | bytes 12322304 | tf_op jit(solution)/shard_map/dot_general | solution.py:26
  332.5 3.3 reduce
  335.8 7.8 %fusion.28 = bf16[16,160,768]{2,1,0:T(8,128)(2,1)S(1)} fusion(bf16[16,160,1024]{2,1,0:T(8,128)(2,1)} %get-tuple-element.31, bf16[1024,768]{0,1:T(8,128)(2,1)S(1)} %copy.69, f32[768]{0:T(1024)S(1)} %reshape.443, f32[768]{0:T(1024)S(1)} %reshape.442, f32[1024]{0:T(1024)S(1)} %add_rsqrt_fusion.1, f32[1024]{0:T(1024)S(1)} %broadcast_multiply_fusion.5), kind=kOutput, calls=%fused_computation.52 | convolution fusion | flops 4031250432 | bytes 10762240 | tf_op jit(solution)/shard_map/dot_general | solution.py:26
  343.6 1.9 copy-done.2
  345.5 0.7 copy.80
  346.8 0.7 copy.81
  347.5 3.6 copy.75
  351.1 2.9 fusion.19
  354.2 5.6 %fusion.18 = f32[1024,768]{0,1:T(8,128)} fusion(f32[1024,768]{0,1:T(8,128)} %get-tuple-element.99, bf16[1024,768]{0,1:T(8,128)(2,1)S(1)} %copy.69, f32[1024,768]{0,1:T(8,128)} %copy.75, f32[1024]{0:T(1024)S(1)} %broadcast_multiply_fusion, f32[1024]{0:T(1024)S(1)} %broadcast_multiply_fusion.1, f32[768]{0:T(1024)S(1)} %reshape.442, ...), kind=kLoop, calls=%fused_computation.30 | loop fusion | flops 7077888 | bytes 11029504 | tf_op jit(solution)/shard_map/add | solution.py:749
  359.7 3.7 copy.89
  364.1 3.5 stack.96
  367.6 3.0 fusion.6.refs_0_
  370.6 28.9 %shard_map.317 = f32[160,768]{1,0:T(8,128)} custom-call(bf16[16,160,768]{2,1,0:T(8,128)(2,1)} %fusion.6.refs_0_), custom_call_target="tpu_custom_call" | custom-call | tf_op jit(solution)/shard_map/pallas_call | solution.py:384
  399.5 1.3 slice.117
  400.8 1.5 slice_bitcast_fusion.3
  402.3 1.8 slice_bitcast_fusion
  404.1 0.7 copy.102
  404.8 0.8 copy.103
  405.6 0.8 copy.104
  (99 shorter events, 12.7 us)
Async XLA Ops:
  136.4 3.8 slice-start.1
  136.5 3.8 slice-start.2
  139.8 22.1 %copy-start = (f32[1024,768]{0,1:T(8,128)}, f32[1024,768]{0,1:T(8,128)S(1)}, u32[]{:S(2)}) copy-start(f32[1024,768]{0,1:T(8,128)S(1)} %get-tuple-element.119) | copy-start | bytes 9437188
  139.8 9.7 %slice-start.3 = ((s8[4718592]{0:T(1024)(128)(4,1)}), s8[4194304]{0:T(1024)(128)(4,1)S(1)}, s32[]{:S(2)}) async-start(s8[4718592]{0:T(1024)(128)(4,1)} %bitcast.117), calls=%async_computation.3 | async-start | bytes 8388608
  140.3 9.3 %slice-start.4 = ((s8[4718592]{0:T(1024)(128)(4,1)}), s8[524288]{0:T(1024)(128)(4,1)S(1)}, s32[]{:S(2)}) async-start(s8[4718592]{0:T(1024)(128)(4,1)} %bitcast.117), calls=%async_computation.4 | async-start | bytes 1048576
  161.9 13.3 %copy-start.8 = (bf16[1024,3072]{1,0:T(8,128)(2,1)}, bf16[1024,3072]{1,0:T(8,128)(2,1)S(1)}, u32[]{:S(2)}) copy-start(bf16[1024,3072]{1,0:T(8,128)(2,1)S(1)} %get-tuple-element.127) | copy-start | bytes 18874372
  189.5 4.0 copy-start.1
  212.4 5.0 %copy-start.3 = (f32[1024,768]{0,1:T(8,128)S(1)}, f32[1024,768]{0,1:T(8,128)}, u32[]{:S(2)}) copy-start(f32[1024,768]{0,1:T(8,128)} %get-tuple-element.99) | copy-start | bytes 9437188
  212.4 5.0 %copy-start.4 = (bf16[16,48,1024]{2,1,0:T(8,128)(2,1)S(1)}, bf16[16,48,1024]{2,1,0:T(8,128)(2,1)}, u32[]{:S(2)}) copy-start(bf16[16,48,1024]{2,1,0:T(8,128)(2,1)} %get-tuple-element.26.refs_3_) | copy-start | bytes 4718596
  343.5 1.9 copy-start.2
  359.7 7.9 %slice-start = ((bf16[16,160,768]{2,1,0:T(8,128)(2,1)}), bf16[16,144,768]{2,1,0:T(8,128)(2,1)S(1)}, s32[]{:S(2)}) async-start(bf16[16,160,768]{2,1,0:T(8,128)(2,1)} %copy-done.2), calls=%async_computation | async-start | bytes 7077888 | tf_op jit(solution)/shard_map/slice | solution.py:768
  370.6 33.5 %copy-start.7 = (f32[48,768]{1,0:T(8,128)S(1)}, f32[48,768]{1,0:T(8,128)}, u32[]{:S(2)}) copy-start(f32[48,768]{1,0:T(8,128)} %get-tuple-element.32) | copy-start | bytes 442372
  370.6 34.2 %copy-start.6 = (f32[192,768]{1,0:T(8,128)S(1)}, f32[192,768]{1,0:T(8,128)}, u32[]{:S(2)}) copy-start(f32[192,768]{1,0:T(8,128)} %get-tuple-element.33) | copy-start | bytes 1769476
  370.6 35.0 %copy-start.5 = (f32[48,3072]{1,0:T(8,128)S(1)}, f32[48,3072]{1,0:T(8,128)}, u32[]{:S(2)}) copy-start(f32[48,3072]{1,0:T(8,128)} %get-tuple-element.34) | copy-start | bytes 1769476

commit v4 on v3

--- a/solution.py
+++ b/solution.py
@@ -6,6 +6,7 @@
 import jax.numpy as jnp
 from jax import lax
 from jax.experimental import pallas as pl
+from jax.experimental.layout import Layout, with_layout_constraint
 from jax.experimental.pallas import tpu as pltpu
 from jax.sharding import PartitionSpec as P
 
@@ -17,7 +18,7 @@
 MASKED = -1e30
 SPARE = 16
 SEGS = 4
-GATHER_STEPS = (1, HEADS)
+GATHER_STEPS = (2, HEADS + 3)
 SCATTER_STEPS = (0, HEADS)
 CHUNK = 512
 
@@ -343,8 +344,15 @@
         for out in outgoing:
             out.wait()
 
-    events = [first] + [add_pair(steps) for steps in whole]
-    for number in reversed(range(depth)):
+    def settle(steps):
+        def run():
+            add_pair(steps + (0,))()
+            add(steps)()
+        return run
+
+    events = [first] + [add_pair(steps) for steps in whole if steps[-1]]
+    events += [settle(steps) for steps in all_steps(depth - 1)]
+    for number in reversed(range(depth - 1)):
         events += [add(steps) for steps in all_steps(number)]
     return events + [last]
 
@@ -490,7 +498,8 @@
 
 def spread_over(number, begin, end):
     inner = number - 2
-    return [0] + [begin + n * (end - begin) // inner for n in range(inner)] + [HEADS - 1]
+    steps = [begin + n * (end - begin) // inner for n in range(inner)]
+    return [0] + [min(step, HEADS - 1) for step in steps] + [HEADS - 1]
 
 
 def run_stages(plan, when, chips):
@@ -624,8 +633,12 @@
     return values * cdf, cdf + values * pdf
 
 
+def by_rows(values):
+    return with_layout_constraint(values, Layout((0, 1)))
+
+
 def row_sums(values):
-    return jnp.sum(values.astype(F32), 0)
+    return dims(jnp.ones((8, values.shape[0]), BF16), values, 1, 0)[0]
 
 
 def widen(vector, width):
@@ -688,9 +701,9 @@
     seg = segment[0]
     extra, pad = masking_rows(seg, live)
 
-    x = tokens.astype(F32)
+    x = by_rows(tokens).astype(F32)
     xhat_one, factor_one = norm(x)
-    h_one = (xhat_one * gain_one_f + bias_one_f).astype(BF16)
+    h_one = lax.optimization_barrier((xhat_one * gain_one_f + bias_one_f).astype(BF16))
     block = 3 * head_dim + SPARE
     offsets = jnp.concatenate(
         [
@@ -714,14 +727,14 @@
     hidden_t = hidden_t.reshape(hidden, width)
     proj_t = proj_t.reshape(width, hidden)
     o_flat = o_t.reshape(width, count)
-    x_one = x + dims(o_flat, out_t, 0, 1) + b_out_f
+    x_one = by_rows(x + dims(o_flat, out_t, 0, 1) + b_out_f)
     xhat_two, factor_two = norm(x_one)
-    h_two = (xhat_two * gain_two_f + bias_two_f).astype(BF16)
+    h_two = lax.optimization_barrier((xhat_two * gain_two_f + bias_two_f).astype(BF16))
     upper = dims(h_two, hidden_t, 1, 1) + b_hidden_f
     act, slope = [v.astype(BF16) for v in gelu_pair(upper)]
     mixed = (x_one + dims(act, proj_t, 1, 1) + b_proj_f).astype(BF16)
 
-    d_y = cotangent.astype(F32) * live.astype(F32)[:, None]
+    d_y = by_rows(cotangent).astype(F32) * live.astype(F32)[:, None]
     d_m = d_y.astype(BF16)
     grad_proj = dims(d_m, act, 0, 0).astype(BF16)
     d_upper = (dims(d_m, proj_t, 1, 0) * slope.astype(F32)).astype(BF16)
@@ -729,7 +742,7 @@
     d_two, grad_gain_two, grad_bias_two = norm_back(
         dims(d_upper, hidden_t, 1, 0), xhat_two, factor_two, gain_two_f
     )
-    d_x_one = d_y + d_two
+    d_x_one = by_rows(d_y + d_two)
     d_attn = d_x_one.astype(BF16)
     grad_out = dims(d_attn, o_flat, 0, 1).astype(BF16)
     d_o = dims(out_t, d_attn, 0, 1).astype(BF16).reshape(HEADS, head_dim, count)
@@ -742,13 +755,14 @@
         (d_qkv,) = attention_back(qkv, extra, pad, o_t, d_o, lse)
     d_flat = d_qkv.reshape(HEADS * block, count)
     grad_qkv = dims(d_flat, h_one, 1, 0).reshape(HEADS, block, width)
-    bias_sums = jnp.sum(d_qkv.astype(F32), -1)
+    bias_sums = dims(jnp.ones((8, count), BF16), d_flat, 1, 1)[0].reshape(HEADS, block)
     d_one, grad_gain_one, grad_bias_one = norm_back(
         dims(d_flat, joined_t, 0, 0), xhat_one, factor_one, gain_one_f
     )
     grad_tokens = d_x_one + d_one
 
-    sums = (
+    part = width // chips
+    sums = jnp.stack([
         grad_gain_one,
         grad_bias_one,
         bias_sums[:, :head_dim].reshape(-1),
@@ -756,14 +770,12 @@
         row_sums(d_attn),
         grad_gain_two,
         grad_bias_two,
-        row_sums(d_upper),
         row_sums(d_m),
-    )
-    sums = jnp.stack(
-        [jnp.pad(s.reshape(chips, -1), ((0, 0), (0, width - s.size // chips))) for s in sums], 1
-    )
-    sums = jnp.pad(sums, ((0, 0), (0, SPARE - sums.shape[1]), (0, 0)))
-    part = width // chips
+    ])
+    sums = sums.reshape(-1, chips, part).transpose(1, 0, 2)
+    more = row_sums(d_upper).reshape(chips, -1, part)
+    sums = jnp.concatenate([sums, more], 1)
+    sums = jnp.pad(sums, ((0, 0), (0, SPARE - sums.shape[1]), (0, width - part)))
     if own_copies:
         early = jnp.concatenate([grad_qkv[:, : 3 * head_dim], sums], 1).astype(BF16)
         (early,) = scatter([early], 3)
@@ -794,7 +806,9 @@
         ]
     g_query, g_key, g_value = [g.T for g in grads]
     g_out, g_hidden, g_proj = [g.T for g in late]
-    g_vec = [vector_grads[n, : v.shape[0]] for n, v in enumerate(vectors)]
+    g_vec = [vector_grads[n, :part] for n in range(8)]
+    ratio = hidden // width
+    g_vec.insert(7, vector_grads[8 : 8 + ratio, :part].reshape(-1))
     return (
         mixed, grad_tokens, g_vec[0], g_vec[1], g_query, g_vec[2], g_key, g_value, g_vec[3],
         g_out, g_vec[4], g_vec[5], g_vec[6], g_hidden, g_vec[7], g_proj, g_vec[8],

time: 413 us -> 360 us (0.87)
  the two profiles are of different devices: /device:TPU:0 before, /device:TPU:9 now
where the time goes in v4:
time: 360 us; the launch traced here: 353 us
  Pallas kernels  223 us (62%)
  matrix products  91.7 us (25%)
  local copies, waits for them, and re-layouts  20 us (6%)
  other arithmetic  17.6 us (5%)
    dot_general x16, matrix products, dims(): lax.dot_general(left, right, (((a,), (b,)), ((), ())), preferred_element_...  91.7 us
    pallas_call x1, Pallas kernels, attention_back(): pl.pallas_call(body, grid=(HEADS,), out_shape=[jax.ShapeDtypeStruct((HEAD...  81.5 us
    pallas_call x1, Pallas kernels, attention(): pl.pallas_call(body, grid=(HEADS,), out_shape=[jax.ShapeDtypeStruct((HEAD...  77.4 us
    pallas_call x1, Pallas kernels, scatter(): pl.pallas_call(functools.partial(scatter_kernel, arrays[0].shape[0], len(...  32.4 us
    pallas_call x1, Pallas kernels, gather(): pl.pallas_call(functools.partial(gather_kernel, chips, len(arrays)), out_...  31.5 us
    unnamed x47, local copies, waits for them, and re-layouts  7.26 us

profile of v4, /device:TPU:9, one launch (start us, length us, event | category | flops | bytes accessed | tf_op | source)
XLA Modules:
  0.0 353.4 jit_solution(11753807589024003102)
XLA Ops:
  0.9 0.8 pad.38
  1.7 0.7 pad.39
  2.4 0.7 pad.40
  3.1 0.7 pad.41
  3.7 0.7 pad.42
  4.4 0.7 pad.43
  5.1 0.7 pad.44
  5.7 0.7 pad.45
  6.4 0.7 pad.46
  7.1 0.7 convert_element_type.195
  7.8 1.7 convert_reduce_fusion
  9.5 2.0 fusion.18
  13.6 0.7 fusion.33.refs_0_
  14.3 31.5 %shard_map.314 = bf16[16,160,768]{2,1,0:T(8,128)(2,1)} custom-call(bf16[160,768]{1,0:T(8,128)(2,1)} %fusion.33.refs_0_), custom_call_target="tpu_custom_call" | custom-call | tf_op jit(solution)/shard_map/pallas_call | solution.py:206
  45.9 0.9 convert_reduce_fusion.1
  46.8 0.9 fusion.56
  47.8 1.3 convert_reduce_fusion.2
  50.2 1.1 copy-done.7
  51.3 8.1 %select_convert_fusion.refs_0_ = bf16[16,160,1024]{2,1,0:T(8,128)(2,1)} fusion(bf16[160]{0:T(256)(128)(2,1)S(1)} %compare_select_fusion.2, f32[16,160]{1,0:T(8,128)S(1)} %maximum_maximum_fusion, pred[160]{0:T(512)(128)(4,1)S(1)} %iota_compare_fusion.4, bf16[16,160,768]{2,1,0:T(8,128)(2,1)} %shard_map.314, bf16[1024,768]{1,0:T(8,128)(2,1)S(1)} %fusion.12), kind=kOutput, calls=%fused_computation.9 | convolution fusion | flops 4031774720 | bytes 10758624 | tf_op jit(solution)/shard_map/dot_general | solution.py:27
  59.4 77.4 %shard_map.315 = (bf16[16,48,1024]{2,1,0:T(8,128)(2,1)}, f32[16,1,1024]{2,1,0:T(1,128)}, bf16[16,48,768]{2,1,0:T(8,128)(2,1)}, bf16[16,192,768]{2,1,0:T(8,128)(2,1)}, bf16[16,48,3072]{2,1,0:T(8,128)(2,1)}) custom-call(bf16[16,160,1024]{2,1,0:T(8,128)(2,1)} %select_convert_fusion.refs_0_, bf16[2,16,1024]{2,1,0:T(8,128)(2,1)} %pad_maximum_fusion.1.refs_1_, ...), custom_call_target="tpu_custom_call" | custom-call | tf_op jit(solution)/shard_map/pallas_call | solution.py:537
  136.9 3.4 fusion.57
  141.3 1.8 copy-done.19
  143.1 8.7 %multiply_convert_fusion.1 = (bf16[1024,3072]{1,0:T(8,128)(2,1)S(1)}, f32[1024,3072]{1,0:T(8,128)}) fusion(f32[3072]{0:T(1024)S(1)} %reshape.444, bf16[1024,768]{1,0:T(8,128)(2,1)S(1)} %add_convert_fusion.1, bf16[3072,768]{1,0:T(8,128)(2,1)S(1)} %bitcast.114), kind=kOutput, calls=%fused_computation.7 | convolution fusion | flops 4850712576 | bytes 25178112 | tf_op jit(solution)/shard_map/dot_general | solution.py:27
  151.8 14.1 %multiply_convert_fusion = bf16[1024,3072]{1,0:T(8,128)(2,1)S(1)} fusion(bf16[768,3072]{1,0:T(8,128)(2,1)S(1)} %bitcast.118, f32[1024,3072]{1,0:T(8,128)} %get-tuple-element.69, f32[3072]{0:T(1024)S(1)} %reshape.444, bf16[1024,768]{1,0:T(8,128)(2,1)S(1)} %copy-done.4, f32[1024]{0:T(1024)S(1)} %bitcast.107), kind=kOutput, calls=%fused_computation.6 | convolution fusion | flops 4875091968 | bytes 25182208 | tf_op jit(solution)/shard_map/dot_general | solution.py:27
  166.0 6.6 %add_convert_fusion = bf16[1024,768]{1,0:T(8,128)(2,1)} fusion(f32[1024,768]{1,0:T(8,128)S(1)} %get-tuple-element.67, bf16[1024,3072]{1,0:T(8,128)(2,1)S(1)} %get-tuple-element.68, bf16[768,3072]{1,0:T(8,128)(2,1)S(1)} %bitcast.119, f32[768]{0:T(1024)S(1)} %reshape.445), kind=kOutput, calls=%fused_computation.40 | convolution fusion | flops 4834197504 | bytes 15731712 | tf_op jit(solution)/shard_map/dot_general | solution.py:27
  172.6 7.2 %convolution_convert_fusion = bf16[768,3072]{1,0:T(8,128)(2,1)} fusion(bf16[1024,3072]{1,0:T(8,128)(2,1)S(1)} %get-tuple-element.68, bf16[1024,768]{1,0:T(8,128)(2,1)S(1)} %copy-done.4, f32[1024]{0:T(1024)S(1)} %bitcast.108), kind=kOutput, calls=%fused_computation.11 | convolution fusion | flops 4836556800 | bytes 12587008 | tf_op jit(solution)/shard_map/dot_general | solution.py:27
  179.9 5.8 %multiply_reduce_fusion = (bf16[768]{0:T(1024)(128)(2,1)S(1)}, f32[1024]{0:T(1024)S(1)}, f32[1024]{0:T(1024)S(1)}, bf16[768]{0:T(1024)(128)(2,1)S(1)}, f32[1024,768]{1,0:T(8,128)S(1)}) fusion(f32[1024,768]{1,0:T(8,128)S(1)} %get-tuple-element.67, f32[1024]{0:T(1024)S(1)} %add_rsqrt_fusion, f32[1024]{0:T(1024)S(1)} %broadcast_multiply_fusion.4, ...), kind=kOutput, calls=%fused_computation.35 | convolution fusion | flops 4838912000 | bytes 17324032 | tf_op jit(solution)/shard_map/dot_general | solution.py:27
  185.7 1.5 multiply_add_fusion
  187.9 3.9 %fusion.40 = bf16[8,3072]{1,0:T(8,128)(2,1)S(1)} fusion(bf16[1024,3072]{1,0:T(8,128)(2,1)} %copy-done.2), kind=kOutput, calls=%fused_computation.87 | convolution fusion | flops 50331648 | bytes 6340608 | tf_op jit(solution)/shard_map/dot_general | solution.py:27
  191.7 0.7 copy-done.3
  192.5 8.5 %convolution_convert_fusion.1 = bf16[3072,768]{1,0:T(8,128)(2,1)} fusion(bf16[1024,3072]{1,0:T(8,128)(2,1)S(1)} %copy-done.3, bf16[1024,768]{1,0:T(8,128)(2,1)} %copy-done.9), kind=kOutput, calls=%fused_computation.12 | convolution fusion | flops 4834197504 | bytes 12582912 | tf_op jit(solution)/shard_map/dot_general | solution.py:27
  201.1 4.0 %convolution_convert_fusion.3 = bf16[768,1024]{1,0:T(8,128)(2,1)} fusion(bf16[768,768]{1,0:T(8,128)(2,1)} %bitcast.121, f32[1024,768]{1,0:T(8,128)S(1)} %multiply_add_fusion), kind=kOutput, calls=%fused_computation.46 | convolution fusion | flops 1209532416 | bytes 5898240 | tf_op jit(solution)/shard_map/dot_general | solution.py:27
  205.1 2.5 convolution_convert_fusion.4
  207.6 81.5 %shard_map.316 = (bf16[16,160,1024]{2,1,0:T(8,128)(2,1)}, f32[48,768]{1,0:T(8,128)}, f32[192,768]{1,0:T(8,128)}, f32[48,3072]{1,0:T(8,128)}) custom-call(bf16[16,160,1024]{2,1,0:T(8,128)(2,1)} %select_convert_fusion.refs_0_, bf16[2,16,1024]{2,1,0:T(8,128)(2,1)} %pad_maximum_fusion.1.refs_1_, f32[1,1024]{1,0:T(1,128)} %get-tuple-element.64.refs_2_, ...), custom_call_target="tpu_custom_call" | custom-call | tf_op jit(solution)/shard_map/pallas_call | solution.py:574
  289.1 9.4 %fusion.17 = (bf16[768]{0:T(1024)(128)(2,1)S(1)}, f32[1024]{0:T(1024)S(1)}, f32[1024]{0:T(1024)S(1)}, bf16[768]{0:T(1024)(128)(2,1)S(1)}, f32[1024,768,1]{1,0,2:T(8,128)S(1)}) fusion(bf16[1024,768]{1,0:T(8,128)(2,1)} %param.19, f32[1024]{0:T(1024)S(1)} %add_rsqrt_fusion.1, f32[1024]{0:T(1024)S(1)} %broadcast_multiply_fusion.5, f32[768]{0:T(1024)S(1)} %reshape.437, ...), kind=kOutput, calls=%fused_computation.30 | convolution fusion | flops 4034392576 | bytes 13916160 | tf_op jit(solution)/shard_map/dot_general | solution.py:27
  298.6 2.4 fusion.16
  300.9 1.3 copy-done.6
  302.2 1.5 fusion.25
  304.2 7.1 %fusion.22 = bf16[16,160,768]{2,1,0:T(8,128)(2,1)S(1)} fusion(bf16[16,160,1024]{2,1,0:T(8,128)(2,1)} %get-tuple-element.31, bf16[1024,768]{1,0:T(8,128)(2,1)S(1)} %copy-done.8), kind=kOutput, calls=%fused_computation.47 | convolution fusion | flops 4026531840 | bytes 10747904 | tf_op jit(solution)/shard_map/dot_general | solution.py:27
  311.6 2.3 pad_maximum_fusion.refs_0_
  313.9 32.4 %shard_map.317 = f32[160,768]{1,0:T(8,128)} custom-call(bf16[16,160,768]{2,1,0:T(8,128)(2,1)} %pad_maximum_fusion.refs_0_), custom_call_target="tpu_custom_call" | custom-call | tf_op jit(solution)/shard_map/pallas_call | solution.py:392
  346.3 0.7 slice.136
  346.9 0.6 reshape.436
  347.6 1.5 slice_bitcast_fusion.5
  349.1 1.8 slice_bitcast_fusion
  350.9 0.7 copy.62
  351.6 0.8 copy.63
  352.4 0.8 copy.64
  (102 shorter events, 6.2 us)
Async XLA Ops:
  0.7 11.5 %copy-start.4 = (bf16[1024,768]{1,0:T(8,128)(2,1)S(1)}, bf16[1024,768]{1,0:T(8,128)(2,1)}, u32[]{:S(2)}) copy-start(bf16[1024,768]{1,0:T(8,128)(2,1)} %param.22) | copy-start | bytes 4718596
  0.7 10.9 %copy-start.17 = (s32[1,1024]{1,0:T(1,128)S(1)}, s32[1,1024]{1,0:T(1,128)}, u32[]{:S(2)}) copy-start(s32[1,1024]{1,0:T(1,128)} %param.21) | copy-start | bytes 12292
  0.7 12.9 %copy-start.14 = (bf16[768,48]{0,1:T(8,128)(2,1)S(1)}, bf16[768,48]{0,1:T(8,128)(2,1)}, u32[]{:S(2)}) copy-start(bf16[768,48]{0,1:T(8,128)(2,1)} %param.28) | copy-start | bytes 221188
  0.7 12.9 %copy-start.15 = (bf16[768,48]{0,1:T(8,128)(2,1)S(1)}, bf16[768,48]{0,1:T(8,128)(2,1)}, u32[]{:S(2)}) copy-start(bf16[768,48]{0,1:T(8,128)(2,1)} %param.27) | copy-start | bytes 221188
  0.7 12.9 %copy-start.16 = (bf16[768,48]{0,1:T(8,128)(2,1)S(1)}, bf16[768,48]{0,1:T(8,128)(2,1)}, u32[]{:S(2)}) copy-start(bf16[768,48]{0,1:T(8,128)(2,1)} %param.25) | copy-start | bytes 221188
  0.7 12.1 %copy-start.18 = (s32[1,1024]{1,0:T(1,128)S(1)}, s32[1,1024]{1,0:T(1,128)}, u32[]{:S(2)}) copy-start(s32[1,1024]{1,0:T(1,128)} %param.20) | copy-start | bytes 12292
  12.2 37.4 %copy-start = (bf16[1024,768]{1,0:T(8,128)(2,1)S(1)}, bf16[1024,768]{1,0:T(8,128)(2,1)}, u32[]{:S(2)}) copy-start(bf16[1024,768]{1,0:T(8,128)(2,1)} %param.19) | copy-start | bytes 4718596
  50.2 1.1 copy-start.7
  140.8 2.3 copy-start.19
  140.8 11.0 %slice-start = ((s8[4718592]{0:T(1024)(128)(4,1)}), s8[4194304]{0:T(1024)(128)(4,1)S(1)}, s32[]{:S(2)}) async-start(s8[4718592]{0:T(1024)(128)(4,1)} %bitcast.116), calls=%async_computation | async-start | bytes 8388608
  143.1 8.7 %copy-start.9 = (bf16[1024,768]{1,0:T(8,128)(2,1)}, bf16[1024,768]{1,0:T(8,128)(2,1)S(1)}, u32[]{:S(2)}) copy-start(bf16[1024,768]{1,0:T(8,128)(2,1)S(1)} %add_convert_fusion.1) | copy-start | bytes 4718596
  143.1 8.7 %slice-start.1 = ((s8[4718592]{0:T(1024)(128)(4,1)}), s8[524288]{0:T(1024)(128)(4,1)S(1)}, s32[]{:S(2)}) async-start(s8[4718592]{0:T(1024)(128)(4,1)} %bitcast.116), calls=%async_computation.1 | async-start | bytes 1048576
  166.0 13.9 %copy-start.2 = (bf16[1024,3072]{1,0:T(8,128)(2,1)}, bf16[1024,3072]{1,0:T(8,128)(2,1)S(1)}, u32[]{:S(2)}) copy-start(bf16[1024,3072]{1,0:T(8,128)(2,1)S(1)} %multiply_convert_fusion) | copy-start | bytes 18874372
  179.9 5.9 %copy-start.5 = (bf16[1024,768]{1,0:T(8,128)(2,1)S(1)}, bf16[1024,768]{1,0:T(8,128)(2,1)}, u32[]{:S(2)}) copy-start(bf16[1024,768]{1,0:T(8,128)(2,1)} %param.22) | copy-start | bytes 4718596
  187.9 4.6 %copy-start.3 = (bf16[1024,3072]{1,0:T(8,128)(2,1)S(1)}, bf16[1024,3072]{1,0:T(8,128)(2,1)}, u32[]{:S(2)}) copy-start(bf16[1024,3072]{1,0:T(8,128)(2,1)} %copy-done.2) | copy-start | bytes 18874372
  201.1 4.0 %copy-start.10 = (bf16[16,48,1024]{2,1,0:T(8,128)(2,1)S(1)}, bf16[16,48,1024]{2,1,0:T(8,128)(2,1)}, u32[]{:S(2)}) copy-start(bf16[16,48,1024]{2,1,0:T(8,128)(2,1)} %get-tuple-element.26.refs_3_) | copy-start | bytes 4718596
  289.1 9.5 %copy-start.1 = (bf16[1024,768]{1,0:T(8,128)(2,1)S(1)}, bf16[1024,768]{1,0:T(8,128)(2,1)}, u32[]{:S(2)}) copy-start(bf16[1024,768]{1,0:T(8,128)(2,1)} %param.19) | copy-start | bytes 4718596
  298.6 3.6 %copy-start.6 = (bf16[16,160,1024]{2,1,0:T(8,128)(2,1)S(1)}, bf16[16,160,1024]{2,1,0:T(8,128)(2,1)}, u32[]{:S(2)}) copy-start(bf16[16,160,1024]{2,1,0:T(8,128)(2,1)} %get-tuple-element.31) | copy-start | bytes 15728644
  302.2 2.0 copy-start.8
  313.9 37.0 %copy-start.13 = (f32[48,768]{1,0:T(8,128)S(1)}, f32[48,768]{1,0:T(8,128)}, u32[]{:S(2)}) copy-start(f32[48,768]{1,0:T(8,128)} %get-tuple-element.32) | copy-start | bytes 442372
  313.9 37.7 %copy-start.12 = (f32[192,768]{1,0:T(8,128)S(1)}, f32[192,768]{1,0:T(8,128)}, u32[]{:S(2)}) copy-start(f32[192,768]{1,0:T(8,128)} %get-tuple-element.33) | copy-start | bytes 1769476
  313.9 38.5 %copy-start.11 = (f32[48,3072]{1,0:T(8,128)S(1)}, f32[48,3072]{1,0:T(8,128)}, u32[]{:S(2)}) copy-start(f32[48,3072]{1,0:T(8,128)} %get-tuple-element.34) | copy-start | bytes 1769476

commit v5 on v4

--- a/solution.py
+++ b/solution.py
@@ -18,8 +18,6 @@
 MASKED = -1e30
 SPARE = 16
 SEGS = 4
-GATHER_STEPS = (2, HEADS + 3)
-SCATTER_STEPS = (0, HEADS)
 CHUNK = 512
 
 
@@ -47,7 +45,11 @@
 def peer(me, axis, step):
     stride, size = axis
     mine = place(me, axis)
-    other = lax.rem(mine + step, size)
+    other, bit = 0, 1
+    while bit < size:
+        digit = lax.rem(lax.div(mine, bit), 2)
+        other = other + bit * ((1 - digit) if step & bit else digit)
+        bit *= 2
     return me + (other - mine) * stride
 
 
@@ -64,12 +66,10 @@
     pl.semaphore_wait(barrier, count)
 
 
-def moved(me, axes, order, steps, sign):
+def moved(me, axes, order, steps):
     for a, step in zip(order, steps):
-        size = axes[a][1]
         if step:
-            other = peer(me, axes[a], step if sign > 0 else size - step)
-            me = me + (other - me)
+            me = peer(me, axes[a], step)
     return me
 
 
@@ -103,11 +103,11 @@
     slots = slots_of(axes, order)
 
     def block_of(steps):
-        return moved(me, axes, order, steps, -1)
+        return moved(me, axes, order, steps)
 
     def message(steps):
         before = steps[:-1]
-        target = moved(me, axes, order[len(before) :], steps[-1:], 1)
+        target = moved(me, axes, order[len(before) :], steps[-1:])
         block = block_of(before)
         fresh = not any(before)
         return [
@@ -124,7 +124,7 @@
     def send_on(steps):
         for k in range(len(steps), len(order)):
             lead = steps + (0,) * (k - len(steps))
-            for step in range(1, axes[order[k]][1]):
+            for step in reversed(range(1, axes[order[k]][1])):
                 for copy in message(lead + (step,)):
                     copy.start()
 
@@ -167,7 +167,7 @@
         other = axis_orders(axes)[1 - c]
         other_slots = slots_of(axes, other)
         for steps, slot in other_slots.items():
-            block = moved(me, axes, other, steps, -1)
+            block = moved(me, axes, other, steps)
             for k, dst in enumerate(outs):
                 n = slot * arrays + k
                 pltpu.make_async_remote_copy(
@@ -177,7 +177,7 @@
                 ).wait_recv()
 
     def cost(steps):
-        return (sum(1 for s in steps if s), len(steps), steps)
+        return (sum(1 for s in steps if s), len(steps), [-s for s in steps])
 
     return [first] + [arrive(steps) for steps in sorted(slots, key=cost)] + [last]
 
@@ -225,7 +225,7 @@
         return sorted(steps, key=lambda t: (-sum(1 for s in t if s), [-s for s in reversed(t)]))
 
     def owner(steps):
-        return moved(me, axes, order, steps, 1)
+        return moved(me, axes, order, steps)
 
     whole = all_steps(depth)
 
@@ -233,7 +233,7 @@
         there = axis_orders(axes)[core]
         names = all_steps_of(there)
         n = names.index(steps)
-        block = moved(me, axes, there, steps, 1)
+        block = moved(me, axes, there, steps)
         return [
             pltpu.make_async_remote_copy(
                 half(ins[k], block, core), halves[k].at[block],
@@ -257,7 +257,7 @@
 
     def message(steps):
         block = owner(steps)
-        target = moved(me, axes, order[len(steps) - 1 :], steps[-1:], 1)
+        target = moved(me, axes, order[len(steps) - 1 :], steps[-1:])
         slot = slots[steps]
         return [
             pltpu.make_async_remote_copy(
@@ -496,9 +496,17 @@
     return pl.BlockSpec(shape, lambda h: (0,) * len(shape))
 
 
-def spread_over(number, begin, end):
+def gather_step(n, count):
+    return 4 + n * 22 // count
+
+
+def scatter_step(n, count):
+    return n // 2 if n < 8 else n - 4
+
+
+def spread_over(number, when):
     inner = number - 2
-    steps = [begin + n * (end - begin) // inner for n in range(inner)]
+    steps = [when(n, inner) for n in range(inner)]
     return [0] + [min(step, HEADS - 1) for step in steps] + [HEADS - 1]
 
 
@@ -513,7 +521,7 @@
 
     for c in range(2):
         stages = plan(me, c, axes)
-        for stage, step in zip(stages, spread_over(len(stages), *when)):
+        for stage, step in zip(stages, spread_over(len(stages), when)):
             @pl.when((core == c) & (h == step))
             def _(stage=stage):
                 stage()
@@ -530,7 +538,7 @@
         if n:
             run_stages(
                 lambda me, c, axes: gather_plan(ins, outs, sems, me, c, axes),
-                GATHER_STEPS, chips,
+                gather_step, chips,
             )
         forward_head(qkv_ref, extra_ref, pad_ref, out, lse, head_dim)
 
@@ -566,7 +574,7 @@
             parts, sems = scatter_parts(n, rest[2:])
             run_stages(
                 lambda me, c, axes: scatter_plan(g_ins, g_outs, *parts, sems, me, c, axes),
-                SCATTER_STEPS, chips,
+                scatter_step, chips,
             )
         backward_head(*ins, grad, d_key, d_value, head_dim)
 
@@ -673,8 +681,9 @@
     head_dim = width // HEADS
     hidden = w_hidden.shape[1] * chips
     vectors = (gain_one, bias_one, b_query, b_value, b_out, gain_two, bias_two, b_hidden, b_proj)
-    packed = jnp.stack([widen(v, width) for v in vectors])
-    packed = jnp.pad(packed, ((0, SPARE - len(vectors)), (0, 0)))
+    packed = widen(jnp.concatenate(vectors), width)[None]
+    packed = jnp.pad(packed, ((0, SPARE - 1), (0, 0)))
+    ends = list(itertools.accumulate(v.shape[0] for v in vectors))
 
     if own_copies:
         first = jnp.concatenate([w_query.T, w_key.T, w_value.T, packed], 0)
@@ -694,7 +703,8 @@
         ]
     joined_t = joined_t.reshape(HEADS * (3 * head_dim + SPARE), width)
     gain_one_f, bias_one_f, b_query_f, b_value_f, b_out_f, gain_two_f, bias_two_f, b_hidden_f, b_proj_f = [
-        vector_rows[:, n, : v.shape[0]].reshape(-1).astype(F32) for n, v in enumerate(vectors)
+        vector_rows[:, 0, end - v.shape[0] : end].reshape(-1).astype(F32)
+        for v, end in zip(vectors, ends)
     ]
 
     live = keep[0]
@@ -731,7 +741,7 @@
     xhat_two, factor_two = norm(x_one)
     h_two = lax.optimization_barrier((xhat_two * gain_two_f + bias_two_f).astype(BF16))
     upper = dims(h_two, hidden_t, 1, 1) + b_hidden_f
-    act, slope = [v.astype(BF16) for v in gelu_pair(upper)]
+    act, slope = lax.optimization_barrier([v.astype(BF16) for v in gelu_pair(upper)])
     mixed = (x_one + dims(act, proj_t, 1, 1) + b_proj_f).astype(BF16)
 
     d_y = by_rows(cotangent).astype(F32) * live.astype(F32)[:, None]

time: 360 us -> 343 us (0.953)
  Pallas kernels: 223 us -> 209 us
    pallas_call x1, Pallas kernels: 77.4 us -> 69 us  [attention(): pl.pallas_call(body, grid=(HEADS,), out_shape=[jax.ShapeDtypeStruct((HEAD...]
    concatenate x0 -> x1, local copies, waits for them, and re-layouts: none -> 6.25 us  [shards(): packed = widen(jnp.concatenate(vectors), width)[None]]
    pad x9 -> x1, local copies, waits for them, and re-layouts: 6.09 us -> 0.01 us  [widen(): return jnp.pad(vector, (0, width - vector.shape[0]))]
where the time goes in v5:
time: 343 us; the launch traced here: 337 us
  Pallas kernels  209 us (61%)
  matrix products  89.3 us (26%)
  local copies, waits for them, and re-layouts  20.2 us (6%)
  other arithmetic  17.6 us (5%)
    dot_general x16, matrix products, dims(): lax.dot_general(left, right, (((a,), (b,)), ((), ())), preferred_element_...  89.3 us
    pallas_call x1, Pallas kernels, attention_back(): pl.pallas_call(body, grid=(HEADS,), out_shape=[jax.ShapeDtypeStruct((HEAD...  78.9 us
    pallas_call x1, Pallas kernels, attention(): pl.pallas_call(body, grid=(HEADS,), out_shape=[jax.ShapeDtypeStruct((HEAD...  69 us
    pallas_call x1, Pallas kernels, gather(): pl.pallas_call(functools.partial(gather_kernel, chips, len(arrays)), out_...  30.6 us
    pallas_call x1, Pallas kernels, scatter(): pl.pallas_call(functools.partial(scatter_kernel, arrays[0].shape[0], len(...  30.3 us
    unnamed x47, local copies, waits for them, and re-layouts  7.36 us

profile of v5, /device:TPU:9, one launch (start us, length us, event | category | flops | bytes accessed | tf_op | source)
XLA Modules:
  0.0 337.2 jit_solution(12715471004240126988)
XLA Ops:
  0.9 6.3 %concatenate.19 = bf16[576]{0:T(1024)(128)(2,1)S(1)} concatenate(bf16[48]{0:T(256)(128)(2,1)} %param.23, bf16[48]{0:T(256)(128)(2,1)} %param.24, bf16[48]{0:T(256)(128)(2,1)} %param.26, bf16[48]{0:T(256)(128)(2,1)} %param.29, bf16[48]{0:T(256)(128)(2,1)} %param.31, bf16[48]{0:T(256)(128)(2,1)} %param.32, bf16[48]{0:T(256)(128)(2,1)} %param.33, bf16[192]{0:T(256)(128)(2,1)} %param.35, ...), dimensions={0} | concatenate | bytes 2304 | tf_op jit(solution)/shard_map/concatenate | solution.py:684
  7.2 0.7 convert_element_type.187
  7.9 1.7 convert_reduce_fusion
  9.6 2.0 fusion.18
  11.6 0.6 compare_select_fusion
  12.2 0.5 fusion.36
  13.0 0.6 pad_maximum_fusion.1.refs_1_
  13.6 0.7 fusion.33.refs_0_
  14.3 30.6 %shard_map.314 = bf16[16,160,768]{2,1,0:T(8,128)(2,1)} custom-call(bf16[160,768]{1,0:T(8,128)(2,1)} %fusion.33.refs_0_), custom_call_target="tpu_custom_call" | custom-call | tf_op jit(solution)/shard_map/pallas_call | solution.py:206
  44.9 1.0 convert_reduce_fusion.1
  46.0 0.9 fusion.56
  47.1 1.1 convert_reduce_fusion.2
  48.6 0.6 fusion.12
  49.3 1.2 copy-done.7
  50.5 8.4 %select_convert_fusion.refs_0_ = bf16[16,160,1024]{2,1,0:T(8,128)(2,1)} fusion(bf16[160]{0:T(256)(128)(2,1)S(1)} %compare_select_fusion.2, f32[16,160]{1,0:T(8,128)S(1)} %maximum_maximum_fusion, pred[160]{0:T(512)(128)(4,1)S(1)} %iota_compare_fusion.4, bf16[16,160,768]{2,1,0:T(8,128)(2,1)} %shard_map.314, bf16[1024,768]{1,0:T(8,128)(2,1)S(1)} %fusion.12), kind=kOutput, calls=%fused_computation.9 | convolution fusion | flops 4031774720 | bytes 10758624 | tf_op jit(solution)/shard_map/dot_general | solution.py:25
  58.9 69.0 %shard_map.315 = (bf16[16,48,1024]{2,1,0:T(8,128)(2,1)}, f32[16,1,1024]{2,1,0:T(1,128)}, bf16[16,48,768]{2,1,0:T(8,128)(2,1)}, bf16[16,192,768]{2,1,0:T(8,128)(2,1)}, bf16[16,48,3072]{2,1,0:T(8,128)(2,1)}) custom-call(bf16[16,160,1024]{2,1,0:T(8,128)(2,1)} %select_convert_fusion.refs_0_, bf16[2,16,1024]{2,1,0:T(8,128)(2,1)} %pad_maximum_fusion.1.refs_1_, ...), custom_call_target="tpu_custom_call" | custom-call | tf_op jit(solution)/shard_map/pallas_call | solution.py:545
  128.0 3.3 fusion.57
  131.3 0.5 multiply_reduce_fusion.2
  131.9 0.5 add_convert_fusion.1
  132.5 1.8 copy-done.19
  134.2 12.8 %fusion.4 = (bf16[1024,3072]{1,0:T(8,128)(2,1)}, bf16[1024,3072]{1,0:T(8,128)(2,1)S(1)}) fusion(f32[3072]{0:T(1024)S(1)} %reshape.444, bf16[1024,768]{1,0:T(8,128)(2,1)S(1)} %add_convert_fusion.1, bf16[3072,768]{1,0:T(8,128)(2,1)S(1)} %bitcast.114), kind=kOutput, calls=%fused_computation.5 | convolution fusion | flops 4869586944 | bytes 18886656 | tf_op jit(solution)/shard_map/dot_general | solution.py:25
  147.0 7.5 %multiply_convert_fusion = bf16[1024,3072]{1,0:T(8,128)(2,1)S(1)} fusion(bf16[1024,3072]{1,0:T(8,128)(2,1)} %get-tuple-element.33, bf16[768,3072]{1,0:T(8,128)(2,1)S(1)} %bitcast.118, bf16[1024,768]{1,0:T(8,128)(2,1)S(1)} %copy-done.4, f32[1024]{0:T(1024)S(1)} %bitcast.107), kind=kOutput, calls=%fused_computation.6 | convolution fusion | flops 4843634688 | bytes 18878464 | tf_op jit(solution)/shard_map/dot_general | solution.py:25
  154.6 6.6 %add_convert_fusion = bf16[1024,768]{1,0:T(8,128)(2,1)} fusion(f32[1024,768]{1,0:T(8,128)S(1)} %get-tuple-element.73, bf16[1024,3072]{1,0:T(8,128)(2,1)S(1)} %get-tuple-element.31, bf16[768,3072]{1,0:T(8,128)(2,1)S(1)} %bitcast.119, f32[768]{0:T(1024)S(1)} %reshape.445), kind=kOutput, calls=%fused_computation.40 | convolution fusion | flops 4834197504 | bytes 15731712 | tf_op jit(solution)/shard_map/dot_general | solution.py:25
  161.2 7.2 %convolution_convert_fusion = bf16[768,3072]{1,0:T(8,128)(2,1)} fusion(bf16[1024,3072]{1,0:T(8,128)(2,1)S(1)} %get-tuple-element.31, bf16[1024,768]{1,0:T(8,128)(2,1)S(1)} %copy-done.4, f32[1024]{0:T(1024)S(1)} %bitcast.108), kind=kOutput, calls=%fused_computation.11 | convolution fusion | flops 4836556800 | bytes 12587008 | tf_op jit(solution)/shard_map/dot_general | solution.py:25
  168.4 5.8 %multiply_reduce_fusion = (bf16[768]{0:T(1024)(128)(2,1)S(1)}, f32[1024]{0:T(1024)S(1)}, f32[1024]{0:T(1024)S(1)}, bf16[768]{0:T(1024)(128)(2,1)S(1)}, f32[1024,768]{1,0:T(8,128)S(1)}) fusion(f32[1024,768]{1,0:T(8,128)S(1)} %get-tuple-element.73, f32[1024]{0:T(1024)S(1)} %add_rsqrt_fusion, f32[1024]{0:T(1024)S(1)} %broadcast_multiply_fusion.4, ...), kind=kOutput, calls=%fused_computation.35 | convolution fusion | flops 4838912000 | bytes 17324032 | tf_op jit(solution)/shard_map/dot_general | solution.py:25
  174.2 1.5 multiply_add_fusion
  175.9 0.3 fusion.38
  176.4 3.9 %fusion.40 = bf16[8,3072]{1,0:T(8,128)(2,1)S(1)} fusion(bf16[1024,3072]{1,0:T(8,128)(2,1)} %copy-done.2), kind=kOutput, calls=%fused_computation.87 | convolution fusion | flops 50331648 | bytes 6340608 | tf_op jit(solution)/shard_map/dot_general | solution.py:25
  180.2 0.7 copy-done.3
  181.0 8.4 %convolution_convert_fusion.1 = bf16[3072,768]{1,0:T(8,128)(2,1)} fusion(bf16[1024,3072]{1,0:T(8,128)(2,1)S(1)} %copy-done.3, bf16[1024,768]{1,0:T(8,128)(2,1)} %copy-done.9), kind=kOutput, calls=%fused_computation.12 | convolution fusion | flops 4834197504 | bytes 12582912 | tf_op jit(solution)/shard_map/dot_general | solution.py:25
  189.6 4.0 %convolution_convert_fusion.3 = bf16[768,1024]{1,0:T(8,128)(2,1)} fusion(bf16[768,768]{1,0:T(8,128)(2,1)} %bitcast.121, f32[1024,768]{1,0:T(8,128)S(1)} %multiply_add_fusion), kind=kOutput, calls=%fused_computation.46 | convolution fusion | flops 1209532416 | bytes 5898240 | tf_op jit(solution)/shard_map/dot_general | solution.py:25
  193.5 2.5 convolution_convert_fusion.4
  196.0 78.9 %shard_map.316 = (bf16[16,160,1024]{2,1,0:T(8,128)(2,1)}, f32[48,768]{1,0:T(8,128)}, f32[192,768]{1,0:T(8,128)}, f32[48,3072]{1,0:T(8,128)}) custom-call(bf16[16,160,1024]{2,1,0:T(8,128)(2,1)} %select_convert_fusion.refs_0_, bf16[2,16,1024]{2,1,0:T(8,128)(2,1)} %pad_maximum_fusion.1.refs_1_, f32[1,1024]{1,0:T(1,128)} %get-tuple-element.70.refs_2_, ...), custom_call_target="tpu_custom_call" | custom-call | tf_op jit(solution)/shard_map/pallas_call | solution.py:582
  275.0 9.4 %fusion.17 = (bf16[768]{0:T(1024)(128)(2,1)S(1)}, f32[1024]{0:T(1024)S(1)}, f32[1024]{0:T(1024)S(1)}, bf16[768]{0:T(1024)(128)(2,1)S(1)}, f32[1024,768,1]{1,0,2:T(8,128)S(1)}) fusion(bf16[1024,768]{1,0:T(8,128)(2,1)} %param.19, f32[1024]{0:T(1024)S(1)} %add_rsqrt_fusion.1, f32[1024]{0:T(1024)S(1)} %broadcast_multiply_fusion.5, f32[768]{0:T(1024)S(1)} %reshape.437, ...), kind=kOutput, calls=%fused_computation.30 | convolution fusion | flops 4034392576 | bytes 13916160 | tf_op jit(solution)/shard_map/dot_general | solution.py:25
  284.5 2.4 fusion.16
  286.8 1.3 copy-done.6
  288.1 1.5 fusion.25
  290.1 7.1 %fusion.22 = bf16[16,160,768]{2,1,0:T(8,128)(2,1)S(1)} fusion(bf16[16,160,1024]{2,1,0:T(8,128)(2,1)} %get-tuple-element.35, bf16[1024,768]{1,0:T(8,128)(2,1)S(1)} %copy-done.8), kind=kOutput, calls=%fused_computation.47 | convolution fusion | flops 4026531840 | bytes 10747904 | tf_op jit(solution)/shard_map/dot_general | solution.py:25
  297.2 0.2 slice.177
  297.5 2.3 pad_maximum_fusion.refs_0_
  299.8 30.3 %shard_map.317 = f32[160,768]{1,0:T(8,128)} custom-call(bf16[16,160,768]{2,1,0:T(8,128)(2,1)} %pad_maximum_fusion.refs_0_), custom_call_target="tpu_custom_call" | custom-call | tf_op jit(solution)/shard_map/pallas_call | solution.py:392
  330.0 0.7 slice.136
  330.7 0.6 reshape.436
  331.4 1.5 slice_bitcast_fusion.5
  332.9 1.8 slice_bitcast_fusion
  334.7 0.7 copy.62
  335.4 0.8 copy.63
  336.2 0.8 copy.64
  (86 shorter events, 2.1 us)
Async XLA Ops:
  0.7 11.6 %copy-start.4 = (bf16[1024,768]{1,0:T(8,128)(2,1)S(1)}, bf16[1024,768]{1,0:T(8,128)(2,1)}, u32[]{:S(2)}) copy-start(bf16[1024,768]{1,0:T(8,128)(2,1)} %param.22) | copy-start | bytes 4718596
  0.7 10.9 %copy-start.17 = (s32[1,1024]{1,0:T(1,128)S(1)}, s32[1,1024]{1,0:T(1,128)}, u32[]{:S(2)}) copy-start(s32[1,1024]{1,0:T(1,128)} %param.21) | copy-start | bytes 12292
  0.7 13.0 %copy-start.14 = (bf16[768,48]{0,1:T(8,128)(2,1)S(1)}, bf16[768,48]{0,1:T(8,128)(2,1)}, u32[]{:S(2)}) copy-start(bf16[768,48]{0,1:T(8,128)(2,1)} %param.28) | copy-start | bytes 221188
  0.7 12.9 %copy-start.15 = (bf16[768,48]{0,1:T(8,128)(2,1)S(1)}, bf16[768,48]{0,1:T(8,128)(2,1)}, u32[]{:S(2)}) copy-start(bf16[768,48]{0,1:T(8,128)(2,1)} %param.27) | copy-start | bytes 221188
  0.7 12.9 %copy-start.16 = (bf16[768,48]{0,1:T(8,128)(2,1)S(1)}, bf16[768,48]{0,1:T(8,128)(2,1)}, u32[]{:S(2)}) copy-start(bf16[768,48]{0,1:T(8,128)(2,1)} %param.25) | copy-start | bytes 221188
  0.7 12.1 %copy-start.18 = (s32[1,1024]{1,0:T(1,128)S(1)}, s32[1,1024]{1,0:T(1,128)}, u32[]{:S(2)}) copy-start(s32[1,1024]{1,0:T(1,128)} %param.20) | copy-start | bytes 12292
  12.2 36.4 %copy-start = (bf16[1024,768]{1,0:T(8,128)(2,1)S(1)}, bf16[1024,768]{1,0:T(8,128)(2,1)}, u32[]{:S(2)}) copy-start(bf16[1024,768]{1,0:T(8,128)(2,1)} %param.19) | copy-start | bytes 4718596
  49.3 1.2 copy-start.7
  131.9 2.3 copy-start.19
  131.9 15.1 %slice-start = ((s8[4718592]{0:T(1024)(128)(4,1)}), s8[4194304]{0:T(1024)(128)(4,1)S(1)}, s32[]{:S(2)}) async-start(s8[4718592]{0:T(1024)(128)(4,1)} %bitcast.116), calls=%async_computation | async-start | bytes 8388608
  134.2 12.8 %copy-start.9 = (bf16[1024,768]{1,0:T(8,128)(2,1)}, bf16[1024,768]{1,0:T(8,128)(2,1)S(1)}, u32[]{:S(2)}) copy-start(bf16[1024,768]{1,0:T(8,128)(2,1)S(1)} %add_convert_fusion.1) | copy-start | bytes 4718596
  134.2 12.8 %slice-start.1 = ((s8[4718592]{0:T(1024)(128)(4,1)}), s8[524288]{0:T(1024)(128)(4,1)S(1)}, s32[]{:S(2)}) async-start(s8[4718592]{0:T(1024)(128)(4,1)} %bitcast.116), calls=%async_computation.1 | async-start | bytes 1048576
  154.6 13.8 %copy-start.2 = (bf16[1024,3072]{1,0:T(8,128)(2,1)}, bf16[1024,3072]{1,0:T(8,128)(2,1)S(1)}, u32[]{:S(2)}) copy-start(bf16[1024,3072]{1,0:T(8,128)(2,1)S(1)} %multiply_convert_fusion) | copy-start | bytes 18874372
  168.4 5.9 %copy-start.5 = (bf16[1024,768]{1,0:T(8,128)(2,1)S(1)}, bf16[1024,768]{1,0:T(8,128)(2,1)}, u32[]{:S(2)}) copy-start(bf16[1024,768]{1,0:T(8,128)(2,1)} %param.22) | copy-start | bytes 4718596
  176.4 4.6 %copy-start.3 = (bf16[1024,3072]{1,0:T(8,128)(2,1)S(1)}, bf16[1024,3072]{1,0:T(8,128)(2,1)}, u32[]{:S(2)}) copy-start(bf16[1024,3072]{1,0:T(8,128)(2,1)} %copy-done.2) | copy-start | bytes 18874372
  189.6 4.0 %copy-start.10 = (bf16[16,48,1024]{2,1,0:T(8,128)(2,1)S(1)}, bf16[16,48,1024]{2,1,0:T(8,128)(2,1)}, u32[]{:S(2)}) copy-start(bf16[16,48,1024]{2,1,0:T(8,128)(2,1)} %get-tuple-element.28.refs_3_) | copy-start | bytes 4718596
  275.0 9.5 %copy-start.1 = (bf16[1024,768]{1,0:T(8,128)(2,1)S(1)}, bf16[1024,768]{1,0:T(8,128)(2,1)}, u32[]{:S(2)}) copy-start(bf16[1024,768]{1,0:T(8,128)(2,1)} %param.19) | copy-start | bytes 4718596
  284.5 3.6 %copy-start.6 = (bf16[16,160,1024]{2,1,0:T(8,128)(2,1)S(1)}, bf16[16,160,1024]{2,1,0:T(8,128)(2,1)}, u32[]{:S(2)}) copy-start(bf16[16,160,1024]{2,1,0:T(8,128)(2,1)} %get-tuple-element.35) | copy-start | bytes 15728644
  288.1 2.0 copy-start.8
  299.8 34.9 %copy-start.13 = (f32[48,768]{1,0:T(8,128)S(1)}, f32[48,768]{1,0:T(8,128)}, u32[]{:S(2)}) copy-start(f32[48,768]{1,0:T(8,128)} %get-tuple-element.36) | copy-start | bytes 442372
  299.8 35.6 %copy-start.12 = (f32[192,768]{1,0:T(8,128)S(1)}, f32[192,768]{1,0:T(8,128)}, u32[]{:S(2)}) copy-start(f32[192,768]{1,0:T(8,128)} %get-tuple-element.37) | copy-start | bytes 1769476
  299.8 36.4 %copy-start.11 = (f32[48,3072]{1,0:T(8,128)S(1)}, f32[48,3072]{1,0:T(8,128)}, u32[]{:S(2)}) copy-start(f32[48,3072]{1,0:T(8,128)} %get-tuple-element.38) | copy-start | bytes 1769476
